TPU v7x, 256 devices: a whole 4x4x8 slice. The times are simulated.
256 devices in a mesh: mz: 64 (over z, x, core), rep: 4 (over y).
Axes of the slice: x: 4, y: 4, z: 8, core: 2. Of those that a mesh axis runs over, the one named last changes fastest.
Arguments:
- spectra: bfloat16 [1048576, 512], P(('mz', 'rep')), may hold values from -6 to 6
- reach_back: int32 [1048576], P(('mz', 'rep')), may hold values from 0 to 256
- reach_ahead: int32 [1048576], P(('mz', 'rep')), may hold values from 0 to 256
- live: int32 [256], P(('mz', 'rep')), may hold values from 1024 to 4096, as said below
- cluster_ids: int32 [1048576], P(('mz', 'rep')), may hold values from 0 to 131071, as said below
Outputs:
- cluster_vectors: float32 [131072, 512], P(('mz', 'rep'))
Inputs may be any that keep to these rules, and one draw needn't show every extreme that they name: Device d holds slots d * 4096 to (d + 1) * 4096 - 1, of which the first live[d] are occupied; at least one device is full. `cluster_ids`: cluster k is owned by m/z range k div (512 * 4). Range d is held by devices d * 4 to d * 4 + 4 - 1 in order of rising m/z; a spectrum on the first of them belongs to a cluster owned by range d - 1 or d, one on the last of them to a cluster owned by range d or d + 1, and one on any other to a cluster owned by range d.
All inputs are finite; a program needn't handle non-finite values.
Results may differ from a plain program's by a relative error of at most 0.0046.
Values may be sent and summed in bfloat16 or wider, within the bound.
No kernel may reach another device: no remote copies, remote signals or barrier semaphores. Data moves between devices by JAX's collectives and lax.ppermute only.
A program may use at most 128 MiB of HBM per device.

v0:
```python
import jax
import jax.numpy as jnp
from jax import lax
from jax.sharding import PartitionSpec as P

DIM = 512
BLOCK = 256
CL_DEV = 512


sharpness = 3.0


def with_halo(array, sides, width):
    edges = {}
    for axis, dim in sides:
        size, length = (lax.axis_size(axis), array.shape[dim])
        up = [(i, (i + 1) % size) for i in range(size - 1)]
        last = lax.slice_in_dim(array, length - width, length, axis=dim)
        leading = lax.slice_in_dim(array, 0, width, axis=dim)
        edges[dim] = (
            lax.ppermute(last, axis, up),
            lax.ppermute(leading, axis, [(b, a) for a, b in up]),
        )
    done = []
    for _, dim in sides:
        low, high = edges[dim]
        around = [(width, width) if d in done else (0, 0) for d in range(array.ndim)]
        array = jnp.concatenate([jnp.pad(low, around), array, jnp.pad(high, around)], axis=dim)
        done.append(dim)
    return array


def shifted(block, axis, distance):
    devices = range(lax.axis_size(axis))
    route = [(i - distance, i) for i in devices if i - distance in devices]
    return lax.ppermute(block, axis, route)


def split_up(array, dim, size):
    before, after = (array.shape[:dim], array.shape[dim + 1 :])
    return jnp.moveaxis(array.reshape(*before, size, -1, *after), dim, 0)


def summed_on_arrival(array, axis, dim):
    size = lax.axis_size(axis)
    parts = lax.all_to_all(split_up(array, dim, size), axis, 0, 0, tiled=True)
    return jnp.sum(parts, axis=0)


def rows_block(queries, query_pos, back, ahead, keys, key_flags, key_start):
    scores = lax.dot_general(
        queries, keys, (((1,), (1,)), ((), ())), preferred_element_type=jnp.float32
    )
    key_pos = key_start + jnp.arange(keys.shape[0], dtype=jnp.int32)
    offset = key_pos[None, :] - query_pos[:, None]
    inside = (offset >= -back[:, None]) & (offset <= ahead[:, None]) & (key_flags[None, :] > 0)
    keep = inside | (offset == 0)
    weight = jnp.where(keep, jnp.exp(sharpness * (scores - 1.0)), jnp.float32(0.0))
    total = jnp.sum(weight, axis=1, keepdims=True)
    mixed = jnp.dot(weight.astype(jnp.bfloat16), keys, preferred_element_type=jnp.float32)
    return (mixed / total).astype(jnp.bfloat16)


def shards(spectra, reach_back, reach_ahead, live, cluster_ids):
    rows = spectra.shape[0]
    values = spectra.astype(jnp.float32)
    unit = (values / jnp.sqrt(jnp.sum(values * values, axis=1, keepdims=True) + 1e-06)).astype(
        jnp.bfloat16
    )
    present = jnp.arange(rows, dtype=jnp.int32) < live[0]
    flags = present.astype(jnp.bfloat16)
    wide_unit, wide_flags = (
        with_halo(unit, ((("mz", "rep"), 0),), BLOCK),
        with_halo(flags, ((("mz", "rep"), 0),), BLOCK),
    )
    pieces = []
    for index in range(rows // BLOCK):
        start = index * BLOCK
        query_pos = start + jnp.arange(BLOCK, dtype=jnp.int32)
        pieces.append(
            rows_block(
                unit[start : start + BLOCK],
                query_pos,
                reach_back[start : start + BLOCK],
                reach_ahead[start : start + BLOCK],
                wide_unit[start : start + 3 * BLOCK],
                wide_flags[start : start + 3 * BLOCK],
                start - BLOCK,
            )
        )
    consensus = jnp.concatenate(pieces, axis=0)
    kept = consensus.astype(jnp.float32) * present.astype(jnp.float32)[:, None]
    rep_count = lax.axis_size("rep")
    per_range = CL_DEV * rep_count
    local_slot = cluster_ids - (lax.axis_index("mz") - 1) * per_range
    partial_value = jax.ops.segment_sum(kept, local_slot, num_segments=3 * per_range).reshape(
        3, per_range, DIM
    )
    from_below = shifted(partial_value[2].astype(jnp.bfloat16), "mz", 1).astype(jnp.float32)
    from_above = shifted(partial_value[0].astype(jnp.bfloat16), "mz", -1).astype(jnp.float32)
    combined = partial_value[1] + from_below + from_above
    owned = summed_on_arrival(combined, "rep", 0)
    scale = jnp.sqrt(jnp.mean(owned * owned, axis=1, keepdims=True) + 1e-06)
    return owned / scale


def solution(mesh):
    return jax.shard_map(
        shards,
        mesh=mesh,
        in_specs=(
            P(("mz", "rep"), None),
            P(("mz", "rep")),
            P(("mz", "rep")),
            P(("mz", "rep")),
            P(("mz", "rep")),
        ),
        out_specs=P(("mz", "rep"), None),
        check_vma=False,
    )
```

profile of v0, /device:TPU:103, one launch (start us, length us, event | category | flops | bytes accessed | tf_op | source)
XLA Modules:
  0.0 186.5 jit_solution(517610912541796616)
XLA Ops:
  0.8 5.3 %collective-permute-start.2 = (bf16[256]{0:T(256)(128)(2,1)S(1)}, bf16[256]{0:T(256)(128)(2,1)S(1)}, u32[]{:S(2)}, u32[]{:S(2)}) collective-permute-start(bf16[256]{0:T(256)(128)(2,1)S(1)} %get-tuple-element.59), channel_id=1, source_target_pairs={{1,0},{2,1},{3,2},{4,3},{5,4},{6,5},{7,6},{8,7},{9,8},{10,9},{11,1... | collective-permute-start | bytes 1544 | tf_op jit(solution)/shard_map/ppermute | solution.py:23
  6.2 1.9 %collective-permute-start = (bf16[256]{0:T(256)(128)(2,1)S(1)}, bf16[256]{0:T(256)(128)(2,1)S(1)}, u32[]{:S(2)}, u32[]{:S(2)}) collective-permute-start(bf16[256]{0:T(256)(128)(2,1)S(1)} %get-tuple-element.60), channel_id=1, source_target_pairs={{0,1},{1,2},{2,3},{3,4},{4,5},{5,6},{6,7},{7,8},{8,9},{9,10},{10,1... | collective-permute-start | bytes 1544 | tf_op jit(solution)/shard_map/ppermute | solution.py:22
  8.1 3.1 %fusion = f32[4096]{0:T(1024)S(1)} fusion(bf16[4096,512]{1,0:T(8,128)(2,1)} %param.5), kind=kLoop, calls=%fused_computation.3 | loop fusion | flops 6287360 | bytes 4210688 | tf_op jit(solution)/shard_map/reduce_sum | solution.py:68
  12.3 1.9 %copy-done = bf16[4096,512]{1,0:T(8,128)(2,1)} copy-done((bf16[4096,512]{1,0:T(8,128)(2,1)}, bf16[4096,512]{1,0:T(8,128)(2,1)S(1)}, u32[]{:S(2)}) %copy-start) | copy-done | bytes 4194328
  14.3 4.9 %collective-permute-start.3 = (bf16[256,512]{1,0:T(8,128)(2,1)S(1)}, bf16[256,512]{1,0:T(8,128)(2,1)S(1)}, u32[]{:S(2)}, u32[]{:S(2)}) collective-permute-start(bf16[256,512]{1,0:T(8,128)(2,1)S(1)} %get-tuple-element.9), channel_id=1, source_target_pairs={{1,0},{2,1},{3,2},{4,3},{5,4},{6,5},{7,6},{8,7},{9,8},{10,9},{11,1... | collective-permute-start | bytes 786440 | tf_op jit(solution)/shard_map/ppermute | solution.py:23
  19.1 1.9 %collective-permute-start.1 = (bf16[256,512]{1,0:T(8,128)(2,1)S(1)}, bf16[256,512]{1,0:T(8,128)(2,1)S(1)}, u32[]{:S(2)}, u32[]{:S(2)}) collective-permute-start(bf16[256,512]{1,0:T(8,128)(2,1)S(1)} %get-tuple-element.10), channel_id=1, source_target_pairs={{0,1},{1,2},{2,3},{3,4},{4,5},{5,6},{6,7},{7,8},{8,9},{9,10},{10,1... | collective-permute-start | bytes 786440 | tf_op jit(solution)/shard_map/ppermute | solution.py:22
  21.5 2.0 %fusion.224 = (f32[256]{0:T(256)S(1)}, bf16[256,768]{1,0:T(8,128)(2,1)S(1)}) fusion(bf16[4096,512]{1,0:T(8,128)(2,1)} %copy-done, pred[768]{0:T(1024)(128)(4,1)S(1)} %get-tuple-element.45, s32[256]{0:T(256)S(1)} %get-tuple-element.42, s32[256]{0:T(256)S(1)} %get-tuple-element.26, s32[256]{0:T(256)S(1)} %iota_add_fusion.16, s32[768]{0:T(1024)S(1)} %iota_add_fusion.1), kind=kOutput, calls=%fused_computation.374 | convolution fusion | flops 203685632 | bytes 1449728 | tf_op jit(solution)/shard_map/dot_general | solution.py:52
  33.4 1.1 fusion.57
  35.6 1.1 fusion.61
  43.1 1.1 fusion.75
  44.2 1.1 fusion.77
  46.3 1.2 fusion.81
  47.6 1.1 fusion.83
  50.4 1.1 fusion.87
  51.5 32.5 %scatter_custom_fusion = f32[6144,512]{1,0:T(8,128)} fusion(s32[4096]{0:T(1024)S(1)} %broadcast_subtract_fusion, bf16[4096,512]{1,0:T(8,128)(2,1)} %fusion.87, f32[]{:T(128)} %constant.26.clone.1, f32[4096]{0:T(1024)S(1)} %get-tuple-element.93), kind=kCustom, calls=%fused_computation.5 | custom fusion | flops 6291456 | bytes 16793604 | tf_op jit(solution)/shard_map/scatter-add | solution.py:97
  84.0 5.4 %convert.4 = bf16[6144,512]{1,0:T(8,128)(2,1)S(1)} convert(f32[6144,512]{1,0:T(8,128)} %scatter_custom_fusion) | non-fusion elementwise | flops 3145728 | bytes 18874368 | tf_op jit(solution)/shard_map/convert.1
  89.6 10.4 %collective-permute-start.4 = (bf16[2048,512]{1,0:T(8,128)(2,1)S(1)}, bf16[2048,512]{1,0:T(8,128)(2,1)S(1)}, u32[]{:S(2)}, u32[]{:S(2)}) collective-permute-start(bf16[2048,512]{1,0:T(8,128)(2,1)S(1)} %get-tuple-element.5), channel_id=1, source_target_pairs={{0,4},{4,8},{8,12},{12,16},{16,20},{20,24},{24,28},{28,32},{32,36}... | collective-permute-start | bytes 6291464 | tf_op jit(solution)/shard_map/ppermute | solution.py:37
  100.0 1.9 %collective-permute-start.5 = (bf16[2048,512]{1,0:T(8,128)(2,1)S(1)}, bf16[2048,512]{1,0:T(8,128)(2,1)S(1)}, u32[]{:S(2)}, u32[]{:S(2)}) collective-permute-start(bf16[2048,512]{1,0:T(8,128)(2,1)S(1)} %get-tuple-element.6), channel_id=1, source_target_pairs={{4,0},{8,4},{12,8},{16,12},{20,16},{24,20},{28,24},{32,28},{36,32}... | collective-permute-start | bytes 6291464 | tf_op jit(solution)/shard_map/ppermute | solution.py:37
  101.9 21.0 %collective-permute-done.4 = bf16[2048,512]{1,0:T(8,128)(2,1)S(1)} collective-permute-done((bf16[2048,512]{1,0:T(8,128)(2,1)S(1)}, bf16[2048,512]{1,0:T(8,128)(2,1)S(1)}, u32[]{:S(2)}, u32[]{:S(2)}) %collective-permute-start.4) | collective-permute-done | bytes 2097184 | tf_op jit(solution)/shard_map/ppermute | solution.py:37
  122.9 7.7 %collective-permute-done.5 = bf16[2048,512]{1,0:T(8,128)(2,1)S(1)} collective-permute-done((bf16[2048,512]{1,0:T(8,128)(2,1)S(1)}, bf16[2048,512]{1,0:T(8,128)(2,1)S(1)}, u32[]{:S(2)}, u32[]{:S(2)}) %collective-permute-start.5) | collective-permute-done | bytes 2097184 | tf_op jit(solution)/shard_map/ppermute | solution.py:37
  130.7 3.0 %fusion.6 = f32[2048,512]{1,0:T(8,128)S(1)} fusion(f32[6144,512]{1,0:T(8,128)} %scatter_custom_fusion, bf16[2048,512]{1,0:T(8,128)(2,1)S(1)} %collective-permute-done.5, bf16[2048,512]{1,0:T(8,128)(2,1)S(1)} %collective-permute-done.4), kind=kLoop, calls=%fused_computation.10 | loop fusion | flops 4194304 | bytes 12582912 | tf_op jit(solution)/shard_map/add | solution.py:102
  133.7 48.7 %all_to_all.5 = f32[4,512,512]{2,1,0:T(8,128)} all-to-all(f32[4,512,512]{2,1,0:T(8,128)S(1)} %bitcast.23), channel_id=1, replica_groups=mesh['mz'=64,'rep'=4] {'rep'}, dimensions={0} | all-to-all | bytes 8388608 | tf_op jit(solution)/shard_map/all_to_all | solution.py:47
  182.4 2.8 %reduce_sum.188 = f32[512,512]{1,0:T(8,128)S(1)} reduce(f32[4,512,512]{2,1,0:T(8,128)} %all_to_all.5, f32[]{:T(128)} %constant.26.clone.1), dimensions={0}, to_apply=%region_18.19 | reduce | flops 786432 | bytes 5242884 | tf_op jit(solution)/shard_map/reduce_sum | solution.py:48
  185.3 1.1 broadcast_divide_fusion
  (81 shorter events, 21.9 us)
Async XLA Ops:
  0.0 11.2 %copy-start.2 = (bf16[4096,512]{1,0:T(8,128)(2,1)S(1)}, bf16[4096,512]{1,0:T(8,128)(2,1)}, u32[]{:S(2)}) copy-start(bf16[4096,512]{1,0:T(8,128)(2,1)} %param.5) | copy-start | bytes 12582916
  0.8 20.6 %collective-permute-start.2 = (bf16[256]{0:T(256)(128)(2,1)S(1)}, bf16[256]{0:T(256)(128)(2,1)S(1)}, u32[]{:S(2)}, u32[]{:S(2)}) collective-permute-start(bf16[256]{0:T(256)(128)(2,1)S(1)} %get-tuple-element.59), channel_id=1, source_target_pairs={{1,0},{2,1},{3,2},{4,3},{5,4},{6,5},{7,6},{8,7},{9,8},{10,9},{11,1... | collective-permute-start | bytes 1544 | tf_op jit(solution)/shard_map/ppermute | solution.py:23
  6.2 15.3 %collective-permute-start = (bf16[256]{0:T(256)(128)(2,1)S(1)}, bf16[256]{0:T(256)(128)(2,1)S(1)}, u32[]{:S(2)}, u32[]{:S(2)}) collective-permute-start(bf16[256]{0:T(256)(128)(2,1)S(1)} %get-tuple-element.60), channel_id=1, source_target_pairs={{0,1},{1,2},{2,3},{3,4},{4,5},{5,6},{6,7},{7,8},{8,9},{9,10},{10,1... | collective-permute-start | bytes 1544 | tf_op jit(solution)/shard_map/ppermute | solution.py:22
  11.2 10.1 %copy-start.3 = (s32[4096]{0:T(1024)S(1)}, s32[4096]{0:T(1024)}, u32[]{:S(2)}) copy-start(s32[4096]{0:T(1024)} %param.7) | copy-start | bytes 49156
  11.2 10.1 %copy-start.4 = (s32[4096]{0:T(1024)S(1)}, s32[4096]{0:T(1024)}, u32[]{:S(2)}) copy-start(s32[4096]{0:T(1024)} %param.6) | copy-start | bytes 49156
  11.2 10.2 %copy-start.5 = (s32[4096]{0:T(1024)S(1)}, s32[4096]{0:T(1024)}, u32[]{:S(2)}) copy-start(s32[4096]{0:T(1024)} %param.9) | copy-start | bytes 49156
  12.3 1.9 %copy-start = (bf16[4096,512]{1,0:T(8,128)(2,1)}, bf16[4096,512]{1,0:T(8,128)(2,1)S(1)}, u32[]{:S(2)}) copy-start(bf16[4096,512]{1,0:T(8,128)(2,1)S(1)} %fusion.1) | copy-start | bytes 12582916
  14.3 18.3 %collective-permute-start.3 = (bf16[256,512]{1,0:T(8,128)(2,1)S(1)}, bf16[256,512]{1,0:T(8,128)(2,1)S(1)}, u32[]{:S(2)}, u32[]{:S(2)}) collective-permute-start(bf16[256,512]{1,0:T(8,128)(2,1)S(1)} %get-tuple-element.9), channel_id=1, source_target_pairs={{1,0},{2,1},{3,2},{4,3},{5,4},{6,5},{7,6},{8,7},{9,8},{10,9},{11,1... | collective-permute-start | bytes 786440 | tf_op jit(solution)/shard_map/ppermute | solution.py:23
  19.1 13.5 %collective-permute-start.1 = (bf16[256,512]{1,0:T(8,128)(2,1)S(1)}, bf16[256,512]{1,0:T(8,128)(2,1)S(1)}, u32[]{:S(2)}, u32[]{:S(2)}) collective-permute-start(bf16[256,512]{1,0:T(8,128)(2,1)S(1)} %get-tuple-element.10), channel_id=1, source_target_pairs={{0,1},{1,2},{2,3},{3,4},{4,5},{5,6},{6,7},{7,8},{8,9},{9,10},{10,1... | collective-permute-start | bytes 786440 | tf_op jit(solution)/shard_map/ppermute | solution.py:22
  21.4 2.5 %copy-start.1 = (bf16[4096,512]{1,0:T(8,128)(2,1)S(1)}, bf16[4096,512]{1,0:T(8,128)(2,1)}, u32[]{:S(2)}) copy-start(bf16[4096,512]{1,0:T(8,128)(2,1)} %copy-done) | copy-start | bytes 12582916
  89.6 33.3 %collective-permute-start.4 = (bf16[2048,512]{1,0:T(8,128)(2,1)S(1)}, bf16[2048,512]{1,0:T(8,128)(2,1)S(1)}, u32[]{:S(2)}, u32[]{:S(2)}) collective-permute-start(bf16[2048,512]{1,0:T(8,128)(2,1)S(1)} %get-tuple-element.5), channel_id=1, source_target_pairs={{0,4},{4,8},{8,12},{12,16},{16,20},{20,24},{24,28},{28,32},{32,36}... | collective-permute-start | bytes 6291464 | tf_op jit(solution)/shard_map/ppermute | solution.py:37
  100.0 30.7 %collective-permute-start.5 = (bf16[2048,512]{1,0:T(8,128)(2,1)S(1)}, bf16[2048,512]{1,0:T(8,128)(2,1)S(1)}, u32[]{:S(2)}, u32[]{:S(2)}) collective-permute-start(bf16[2048,512]{1,0:T(8,128)(2,1)S(1)} %get-tuple-element.6), channel_id=1, source_target_pairs={{4,0},{8,4},{12,8},{16,12},{20,16},{24,20},{28,24},{32,28},{36,32}... | collective-permute-start | bytes 6291464 | tf_op jit(solution)/shard_map/ppermute | solution.py:37
where the time goes:
time: 187 us; the launch traced here: 186 us
  other arithmetic  49.3 us (26%)
  blocking collectives  48.7 us (26%)
  matrix products  29.4 us (16%)
  waiting for transfers between devices  28.8 us (15%)
  starting transfers between devices  26.3 us (14%)
  local copies, waits for them, and re-layouts  2.66 us (1%)
    all_to_all x1, blocking collectives, summed_on_arrival(): parts = lax.all_to_all(split_up(array, dim, size), axis, 0, 0, tiled=True)  48.7 us
    scatter-add x1, other arithmetic, shards(): jax.ops.segment_sum(kept, local_slot, num_segments=3 * per_range)  32.5 us
    ppermute x2, waiting for transfers between devices, shifted(): return lax.ppermute(block, axis, route)  28.7 us
    dot_general x16, matrix products, rows_block(): jnp.dot(weight.astype(jnp.bfloat16), keys, preferred_element_type=jnp.flo...  17.4 us
    ppermute x2, starting transfers between devices, shifted(): return lax.ppermute(block, axis, route)  12.3 us
    dot_general x16, matrix products, rows_block(): lax.dot_general(queries, keys, (((1,), (1,)), ((), ())), preferred_elemen...  12 us
    ppermute x2, starting transfers between devices, with_halo(): lax.ppermute(leading, axis, [(b, a) for a, b in up])  10.2 us
    another operation x1, other arithmetic  5.38 us
  transfers between devices with their start and end apart: 6, of which 2 were waited for; matrix products, arithmetic and copies ran while one was open for 8% of the time, Pallas kernels for 0%

commit v1 on v0

v1 whole, which is shorter than its diff:
```python
import functools

import jax
import jax.numpy as jnp
from jax import lax
from jax.experimental import pallas as pl
from jax.experimental.pallas import tpu as pltpu
from jax.sharding import PartitionSpec as P

DIM = 512
BLOCK = 256
CL_DEV = 512
ROWS = 4096
NBLK = ROWS // BLOCK
HALO = BLOCK + 16
FAR = -(1 << 24)
SCALE = 3.0 * 1.4426950408889634
f32, bf16, i32 = jnp.float32, jnp.bfloat16, jnp.int32
NT = (((1,), (1,)), ((), ()))


def unit_rows(block):
    values = block.astype(f32)
    square = jnp.sum(values * values, axis=1, keepdims=True)
    return (values * lax.rsqrt(square + 1e-06)).astype(bf16)


def transposed(unit):
    return jnp.transpose(unit)


def attend(query, back, ahead, cap, keys, keys_t, low_cap, high_cap):
    at = lax.broadcasted_iota(i32, (1, BLOCK), 1) + BLOCK
    low = at - back
    high = at + ahead
    own = jnp.minimum(high, cap - 1)
    total = None
    mixed = None
    for k in range(3):
        scores = lax.dot_general(keys[k], query, NT, preferred_element_type=f32)
        slot = lax.broadcasted_iota(i32, (BLOCK, BLOCK), 0) + k * BLOCK
        if k == 0:
            keep = slot >= low
            if low_cap is not None:
                keep = keep & (slot < low_cap)
        elif k == 1:
            keep = ((slot >= low) & (slot <= own)) | (slot == at)
        elif high_cap is None:
            keep = slot <= own
        else:
            keep = slot <= jnp.minimum(high, high_cap - 1)
        weight = jnp.where(keep, jnp.exp2(scores * SCALE - SCALE), 0.0)
        part = jnp.sum(weight, axis=0, keepdims=True)
        term = jnp.dot(keys_t[k], weight.astype(bf16), preferred_element_type=f32)
        total = part if total is None else total + part
        mixed = term if mixed is None else mixed + term
    return (mixed * (1.0 / total)).astype(bf16)


def interior_kernel(live_ref, back_ref, ahead_ref, spectra_ref, out_ref, unit_ref, unit_t_ref):
    def prepare(index):
        start = pl.multiple_of(index * BLOCK, BLOCK)
        unit = unit_rows(spectra_ref[pl.ds(start, BLOCK), :])
        unit_ref[index] = unit
        unit_t_ref[index] = transposed(unit)

    for index in range(3):
        prepare(index)
    live = live_ref[0]

    def step(index, _):
        start = pl.multiple_of(index * BLOCK, BLOCK)
        lanes = pl.ds(start, BLOCK)
        prepare(jnp.minimum(index + 2, NBLK - 1))
        out_ref[:, pl.ds(pl.multiple_of(start - BLOCK, BLOCK), BLOCK)] = attend(
            unit_ref[index],
            back_ref[:, lanes],
            ahead_ref[:, lanes],
            live - (start - BLOCK),
            [unit_ref[index + k] for k in (-1, 0, 1)],
            [unit_t_ref[index + k] for k in (-1, 0, 1)],
            None,
            None,
        )
        return 0

    lax.fori_loop(1, NBLK - 1, step, 0)


def edges_kernel(live_ref, back_ref, ahead_ref, spectra_ref, below_ref, above_ref, out_ref):
    live = live_ref[0]

    def count(ref):
        digits = ref[BLOCK : BLOCK + 8, :BLOCK].astype(f32)
        return (digits[0:1] * 64.0 + digits[1:2]).astype(i32)

    def unit(block):
        return unit_rows(spectra_ref[block * BLOCK : (block + 1) * BLOCK, :])

    keys = [unit_rows(below_ref[:BLOCK, :]), unit(0), unit(1)]
    out_ref[:, :BLOCK] = attend(
        keys[1], back_ref[:, :BLOCK], ahead_ref[:, :BLOCK], live + BLOCK, keys,
        [transposed(k) for k in keys], count(below_ref) - (ROWS - BLOCK), None,
    )
    keys = [unit(NBLK - 2), unit(NBLK - 1), unit_rows(above_ref[:BLOCK, :])]
    out_ref[:, BLOCK:] = attend(
        keys[1], back_ref[:, ROWS - BLOCK :], ahead_ref[:, ROWS - BLOCK :],
        live - (ROWS - 2 * BLOCK), keys, [transposed(k) for k in keys],
        None, count(above_ref) + 2 * BLOCK,
    )


INNER = ROWS - 2 * BLOCK
CHUNK = INNER // 4


def added(first, live, ids_ref, rows, start):
    width = rows.shape[1]
    slot = lax.broadcasted_iota(i32, (1, width), 1) + start
    wanted = jnp.where(slot < live, ids_ref[:, start : start + width] - first, FAR)
    hot = lax.broadcasted_iota(i32, (CL_DEV, width), 0) == wanted
    hot = jnp.where(hot, 1.0, 0.0).astype(bf16)
    return lax.dot_general(hot, rows, NT, preferred_element_type=f32)


def sums_kernel(turns, away, rep_count, live_ref, ids_ref, inner_ref, edge_ref, *outs):
    rep = lax.axis_index("rep")
    band = lax.axis_index("mz")
    per_range = CL_DEV * rep_count
    if away:
        band = band + jnp.where(rep == 0, -1, 1)

    def work():
        live = live_ref[0]
        for turn, out_ref in zip(turns, outs):
            owner = lax.rem(rep + turn, rep_count)
            first = band * per_range + owner * CL_DEV

            acc = added(first, live, ids_ref, edge_ref[:, :BLOCK], 0)
            acc = acc + added(first, live, ids_ref, edge_ref[:, BLOCK:], ROWS - BLOCK)
            for start in range(0, INNER, CHUNK):
                acc = acc + added(first, live, ids_ref, inner_ref[:, start : start + CHUNK], start + BLOCK)
            out_ref[...] = acc.astype(out_ref.dtype)

    if away:
        pl.when((rep == 0) | (rep == rep_count - 1))(work)
    else:
        work()


def finish_kernel(own_ref, *rest):
    out_ref = rest[-1]
    owned = own_ref[...]
    for ref in rest[:-1]:
        owned = owned + ref[...].astype(f32)
    mean = jnp.sum(owned * owned, axis=1, keepdims=True) * (1.0 / DIM)
    out_ref[...] = owned / jnp.sqrt(mean + 1e-06)


VMEM = pl.BlockSpec(memory_space=pltpu.VMEM)
SMEM = pl.BlockSpec(memory_space=pltpu.SMEM)
LIMIT = 40 * 1024 * 1024


def call(kernel, name, inputs, out_shape, flops, scratch=(), limit=LIMIT):
    one = not isinstance(out_shape, (list, tuple))
    in_specs = [SMEM if x.dtype == i32 and x.size < 64 else VMEM for x in inputs]
    moved = sum(x.size * x.dtype.itemsize for x in inputs)
    return pl.pallas_call(
        kernel,
        out_shape=out_shape,
        in_specs=in_specs,
        out_specs=VMEM if one else [VMEM] * len(out_shape),
        scratch_shapes=list(scratch),
        name=name,
        cost_estimate=pl.CostEstimate(flops=flops, bytes_accessed=moved, transcendentals=0),
        compiler_params=pltpu.CompilerParams(vmem_limit_bytes=limit),
    )(*inputs)


def shape(rows, columns, dtype):
    return jax.ShapeDtypeStruct((rows, columns), dtype)


def shards(spectra, reach_back, reach_ahead, live, cluster_ids):
    bands, reps = lax.axis_size("mz"), lax.axis_size("rep")
    every = bands * reps
    both = ("mz", "rep")

    def sum_blocks(turns, away, dtype, name):
        return call(
            functools.partial(sums_kernel, turns, away, reps), name,
            [live, ids, inner, edge], [shape(CL_DEV, DIM, dtype)] * len(turns),
            2 * CL_DEV * ROWS * DIM * len(turns),
        )

    tail = jnp.concatenate(
        [jnp.full((1, DIM), live[0] // 64), jnp.full((15, DIM), live[0] % 64)], axis=0
    ).astype(bf16)
    from_below = lax.ppermute(
        jnp.concatenate([spectra[ROWS - BLOCK :], tail]), both, [(i, i + 1) for i in range(every - 1)]
    )
    from_above = lax.ppermute(
        jnp.concatenate([spectra[:BLOCK], tail]), both, [(i + 1, i) for i in range(every - 1)]
    )
    back, ahead, ids = (x.reshape(1, ROWS) for x in (reach_back, reach_ahead, cluster_ids))
    per_block = 4 * BLOCK * 3 * BLOCK * DIM
    inner = call(
        interior_kernel, "interior", [live, back, ahead, spectra], shape(DIM, INNER, bf16), per_block * (NBLK - 2),
        [pltpu.VMEM((NBLK, BLOCK, DIM), bf16), pltpu.VMEM((NBLK, DIM, BLOCK), bf16)],
    )
    edge = call(
        edges_kernel, "edges", [live, back, ahead, spectra, from_below, from_above],
        shape(DIM, 2 * BLOCK, bf16), 2 * per_block,
    )

    away_pairs = [(d * reps, (d - 1) * reps) for d in range(1, bands)]
    away_pairs += [(d * reps + reps - 1, (d + 1) * reps + reps - 1) for d in range(bands - 1)]
    moved = {}
    for turn in (2, 1, 3, 0):
        (block,) = sum_blocks((turn,), True, bf16, f"away{turn}")
        moved[turn] = lax.ppermute(block, both, away_pairs)
    up = [(i, (i + 1) % reps) for i in range(reps)]
    down = [(b, a) for a, b in up]
    own = {}
    (own[2],) = sum_blocks((2,), False, f32, "own2")
    far = (own[2] + moved[2].astype(f32)).astype(bf16)
    half = CL_DEV // 2
    low_half = lax.ppermute(far[:half], "rep", up)
    high_half = lax.ppermute(far[half:], "rep", down)
    own[1], own[3] = sum_blocks((1, 3), False, f32, "own13")
    (own[0],) = sum_blocks((0,), False, f32, "own0")
    next_up = own[1] + moved[1].astype(f32)
    next_up = jnp.concatenate([next_up[:half] + low_half.astype(f32), next_up[half:]]).astype(bf16)
    next_down = own[3] + moved[3].astype(f32)
    next_down = jnp.concatenate([next_down[:half], next_down[half:] + high_half.astype(f32)]).astype(bf16)
    got_up = lax.ppermute(next_up, "rep", up)
    got_down = lax.ppermute(next_down, "rep", down)
    return call(finish_kernel, "finish", [own[0], moved[0], got_up, got_down], shape(CL_DEV, DIM, f32), 1 << 20)


def solution(mesh):
    rows = P(("mz", "rep"))
    return jax.shard_map(
        shards,
        mesh=mesh,
        in_specs=(P(("mz", "rep"), None), rows, rows, rows, rows),
        out_specs=P(("mz", "rep"), None),
        check_vma=False,
    )
```

time: 187 us -> 90.6 us (0.48)
  the two profiles are of different devices: /device:TPU:103 before, /device:TPU:102 now
where the time goes in v1:
time: 90.6 us; the launch traced here: 90.2 us
  Pallas kernels  41.6 us (46%)
  starting transfers between devices  25.4 us (28%)
  waiting for transfers between devices  16.5 us (18%)
  local copies, waits for them, and re-layouts  4.79 us (5%)
  between operations  0.97 us (1%)
    pallas_call x10, Pallas kernels, call(): pl.pallas_call(kernel, out_shape=out_shape, in_specs=in_specs, out_specs=...  41.6 us
    ppermute x4, starting transfers between devices, shards(): moved[turn] = lax.ppermute(block, both, away_pairs)  9.4 us
    ppermute x1, waiting for transfers between devices, shards(): got_down = lax.ppermute(next_down, 'rep', down)  7.66 us
    ppermute x1, waiting for transfers between devices, shards(): high_half = lax.ppermute(far[half:], 'rep', down)  5.23 us
    ppermute x1, starting transfers between devices, shards(): high_half = lax.ppermute(far[half:], 'rep', down)  4.44 us
    ppermute x1, starting transfers between devices, shards(): lax.ppermute(jnp.concatenate([spectra[:BLOCK], tail]), both, [(i + 1, i)...  4.19 us
    ppermute x1, starting transfers between devices, shards(): got_down = lax.ppermute(next_down, 'rep', down)  3.77 us
    unnamed x8, local copies, waits for them, and re-layouts  3.62 us
  transfers between devices with their start and end apart: 10, of which 3 were waited for; matrix products, arithmetic and copies ran while one was open for 1% of the time, Pallas kernels for 31%

profile of v1, /device:TPU:102, one launch (start us, length us, event | category | flops | bytes accessed | tf_op | source)
XLA Modules:
  0.0 90.2 jit_solution(17594099298844416335)
XLA Ops:
  0.7 1.1 %fusion.3 = (bf16[256,512]{1,0:T(8,128)(2,1)S(1)}, bf16[256,512]{1,0:T(8,128)(2,1)S(1)}) fusion(bf16[4096,512]{1,0:T(8,128)(2,1)} %spectra_ref.3), kind=kLoop, calls=%fused_computation.15 | loop fusion | bytes 1048576 | tf_op jit(solution)/shard_map/slice | solution.py:204
  1.9 3.5 %collective-permute-start = (bf16[272,512]{1,0:T(8,128)(2,1)S(1)}, bf16[272,512]{1,0:T(8,128)(2,1)S(1)}, u32[]{:S(2)}, u32[]{:S(2)}) collective-permute-start(bf16[272,512]{1,0:T(8,128)(2,1)S(1)} %get-tuple-element.14), channel_id=1, source_target_pairs={{0,1},{1,2},{2,3},{3,4},{4,5},{5,6},{6,7},{7,8},{8,9},{9,10},{10,1... | collective-permute-start | bytes 835592 | tf_op jit(solution)/shard_map/ppermute | solution.py:200
  5.4 4.2 %collective-permute-start.1 = (bf16[272,512]{1,0:T(8,128)(2,1)S(1)}, bf16[272,512]{1,0:T(8,128)(2,1)S(1)}, u32[]{:S(2)}, u32[]{:S(2)}) collective-permute-start(bf16[272,512]{1,0:T(8,128)(2,1)S(1)} %get-tuple-element.13), channel_id=1, source_target_pairs={{1,0},{2,1},{3,2},{4,3},{5,4},{6,5},{7,6},{8,7},{9,8},{10,9},{11,1... | collective-permute-start | bytes 835592 | tf_op jit(solution)/shard_map/ppermute | solution.py:203
  9.6 2.2 %copy-done = bf16[4096,512]{1,0:T(8,128)(2,1)S(1)} copy-done((bf16[4096,512]{1,0:T(8,128)(2,1)S(1)}, bf16[4096,512]{1,0:T(8,128)(2,1)}, u32[]{:S(2)}) %copy-start) | copy-done | bytes 4194328
  11.8 0.7 copy-done.1
  13.3 17.6 %interior.1.inner_ref = bf16[512,3584]{1,0:T(8,128)(2,1)S(1)} custom-call(s32[1]{0:T(128)} %copy.6.live_ref, s32[1,4096]{1,0:T(1,128)S(1)} %bitcast.9, s32[1,4096]{1,0:T(1,128)S(1)} %bitcast.11, bf16[4096,512]{1,0:T(8,128)(2,1)S(1)} %copy-done), custom_call_target="tpu_custom_call" | custom-call | flops 5637144576 | bytes 4227076 | tf_op jit(solution)/shard_map/interior/pallas_call | solution.py:169
  30.9 1.8 %edges.1.edge_ref = bf16[512,512]{1,0:T(8,128)(2,1)S(1)} custom-call(s32[1]{0:T(128)} %copy.6.live_ref, s32[1,4096]{1,0:T(1,128)S(1)} %bitcast.10, s32[1,4096]{1,0:T(1,128)S(1)} %bitcast.12, bf16[4096,512]{1,0:T(8,128)(2,1)S(1)} %copy-done, bf16[272,512]{1,0:T(8,128)(2,1)S(1)} %collective-permute-done.below_ref, ...), custom_call_target="tpu_custom_call" | custom-call | flops 805306368 | bytes 4784132 | tf_op jit(solution)/shard_map/edges/pallas_call | solution.py:169
  32.7 2.6 %away3.1 = bf16[512,512]{1,0:T(8,128)(2,1)S(1)} custom-call(s32[1]{0:T(128)} %copy.6.live_ref, s32[1,4096]{1,0:T(1,128)S(1)} %bitcast.13, bf16[512,3584]{1,0:T(8,128)(2,1)S(1)} %interior.1.inner_ref, bf16[512,512]{1,0:T(8,128)(2,1)S(1)} %edges.1.edge_ref), custom_call_target="tpu_custom_call" | custom-call | flops 2147483648 | bytes 4210692 | tf_op jit(solution)/shard_map/away3/pallas_call | solution.py:169
  35.4 2.6 %away2.1 = bf16[512,512]{1,0:T(8,128)(2,1)S(1)} custom-call(s32[1]{0:T(128)} %copy.6.live_ref, s32[1,4096]{1,0:T(1,128)S(1)} %bitcast.14, bf16[512,3584]{1,0:T(8,128)(2,1)S(1)} %interior.1.inner_ref, bf16[512,512]{1,0:T(8,128)(2,1)S(1)} %edges.1.edge_ref), custom_call_target="tpu_custom_call" | custom-call | flops 2147483648 | bytes 4210692 | tf_op jit(solution)/shard_map/away2/pallas_call | solution.py:169
  38.0 2.6 %own2.1 = f32[512,512]{1,0:T(8,128)S(1)} custom-call(s32[1]{0:T(128)} %copy.6.live_ref, s32[1,4096]{1,0:T(1,128)S(1)} %bitcast.15, bf16[512,3584]{1,0:T(8,128)(2,1)S(1)} %interior.1.inner_ref, bf16[512,512]{1,0:T(8,128)(2,1)S(1)} %edges.1.edge_ref), custom_call_target="tpu_custom_call" | custom-call | flops 2147483648 | bytes 4210692 | tf_op jit(solution)/shard_map/own2/pallas_call | solution.py:169
  40.6 2.6 %away1.1 = bf16[512,512]{1,0:T(8,128)(2,1)S(1)} custom-call(s32[1]{0:T(128)} %copy.6.live_ref, s32[1,4096]{1,0:T(1,128)S(1)} %bitcast.16, bf16[512,3584]{1,0:T(8,128)(2,1)S(1)} %interior.1.inner_ref, bf16[512,512]{1,0:T(8,128)(2,1)S(1)} %edges.1.edge_ref), custom_call_target="tpu_custom_call" | custom-call | flops 2147483648 | bytes 4210692 | tf_op jit(solution)/shard_map/away1/pallas_call | solution.py:169
  43.3 1.9 %collective-permute-start.7 = (bf16[512,512]{1,0:T(8,128)(2,1)S(1)}, bf16[512,512]{1,0:T(8,128)(2,1)S(1)}, u32[]{:S(2)}, u32[]{:S(2)}) collective-permute-start(bf16[512,512]{1,0:T(8,128)(2,1)S(1)} %away3.1), channel_id=1, source_target_pairs={{4,0},{8,4},{12,8},{16,12},{20,16},{24,20},{28,24},{32,28},{36,32}... | collective-permute-start | bytes 1572872 | tf_op jit(solution)/shard_map/ppermute | solution.py:222
  45.2 3.0 %collective-permute-start.4 = (bf16[512,512]{1,0:T(8,128)(2,1)S(1)}, bf16[512,512]{1,0:T(8,128)(2,1)S(1)}, u32[]{:S(2)}, u32[]{:S(2)}) collective-permute-start(bf16[512,512]{1,0:T(8,128)(2,1)S(1)} %away2.1), channel_id=1, source_target_pairs={{4,0},{8,4},{12,8},{16,12},{20,16},{24,20},{28,24},{32,28},{36,32}... | collective-permute-start | bytes 1572872 | tf_op jit(solution)/shard_map/ppermute | solution.py:222
  48.2 5.1 %own13.1 = (f32[512,512]{1,0:T(8,128)S(1)}, f32[512,512]{1,0:T(8,128)S(1)}) custom-call(s32[1]{0:T(128)} %copy.6.live_ref, s32[1,4096]{1,0:T(1,128)S(1)} %bitcast.17, bf16[512,3584]{1,0:T(8,128)(2,1)S(1)} %interior.1.inner_ref, bf16[512,512]{1,0:T(8,128)(2,1)S(1)} %edges.1.edge_ref), custom_call_target="tpu_custom_call" | custom-call | flops 4294967296 | bytes 4210692 | tf_op jit(solution)/shard_map/own13/pallas_call | solution.py:169
  53.3 2.6 %away0.1 = bf16[512,512]{1,0:T(8,128)(2,1)S(1)} custom-call(s32[1]{0:T(128)} %copy.6.live_ref, s32[1,4096]{1,0:T(1,128)S(1)} %bitcast.18, bf16[512,3584]{1,0:T(8,128)(2,1)S(1)} %interior.1.inner_ref, bf16[512,512]{1,0:T(8,128)(2,1)S(1)} %edges.1.edge_ref), custom_call_target="tpu_custom_call" | custom-call | flops 2147483648 | bytes 4210692 | tf_op jit(solution)/shard_map/away0/pallas_call | solution.py:169
  55.9 1.9 %collective-permute-start.3 = (bf16[512,512]{1,0:T(8,128)(2,1)S(1)}, bf16[512,512]{1,0:T(8,128)(2,1)S(1)}, u32[]{:S(2)}, u32[]{:S(2)}) collective-permute-start(bf16[512,512]{1,0:T(8,128)(2,1)S(1)} %away1.1), channel_id=1, source_target_pairs={{4,0},{8,4},{12,8},{16,12},{20,16},{24,20},{28,24},{32,28},{36,32}... | collective-permute-start | bytes 1572872 | tf_op jit(solution)/shard_map/ppermute | solution.py:222
  57.9 2.5 %collective-permute-start.2 = (bf16[512,512]{1,0:T(8,128)(2,1)S(1)}, bf16[512,512]{1,0:T(8,128)(2,1)S(1)}, u32[]{:S(2)}, u32[]{:S(2)}) collective-permute-start(bf16[512,512]{1,0:T(8,128)(2,1)S(1)} %away0.1), channel_id=1, source_target_pairs={{4,0},{8,4},{12,8},{16,12},{20,16},{24,20},{28,24},{32,28},{36,32}... | collective-permute-start | bytes 1572872 | tf_op jit(solution)/shard_map/ppermute | solution.py:222
  60.6 4.4 %collective-permute-start.8 = (bf16[256,512]{1,0:T(8,128)(2,1)S(1)}, bf16[256,512]{1,0:T(8,128)(2,1)S(1)}, u32[]{:S(2)}, u32[]{:S(2)}) collective-permute-start(bf16[256,512]{1,0:T(8,128)(2,1)S(1)} %get-tuple-element.11), channel_id=1, source_target_pairs={{1,0},{2,1},{3,2},{0,3},{5,4},{6,5},{7,6},{4,7},{9,8},{10,9},{11,1... | collective-permute-start | bytes 786440 | tf_op jit(solution)/shard_map/ppermute | solution.py:230
  65.6 5.2 %collective-permute-done.8 = bf16[256,512]{1,0:T(8,128)(2,1)S(1)} collective-permute-done((bf16[256,512]{1,0:T(8,128)(2,1)S(1)}, bf16[256,512]{1,0:T(8,128)(2,1)S(1)}, u32[]{:S(2)}, u32[]{:S(2)}) %collective-permute-start.8) | collective-permute-done | bytes 262176 | tf_op jit(solution)/shard_map/ppermute | solution.py:230
  70.9 3.8 %collective-permute-start.9 = (bf16[512,512]{1,0:T(8,128)(2,1)S(1)}, bf16[512,512]{1,0:T(8,128)(2,1)S(1)}, u32[]{:S(2)}, u32[]{:S(2)}) collective-permute-start(bf16[512,512]{1,0:T(8,128)(2,1)S(1)} %pad_maximum_fusion.1), channel_id=1, source_target_pairs={{1,0},{2,1},{3,2},{0,3},{5,4},{6,5},{7,6},{4,7},{9,8},{10,9},{11,1... | collective-permute-start | bytes 1572872 | tf_op jit(solution)/shard_map/ppermute | solution.py:238
  74.9 2.6 %own0.1.own_ref = f32[512,512]{1,0:T(8,128)S(1)} custom-call(s32[1]{0:T(128)} %copy.6.live_ref, s32[1,4096]{1,0:T(1,128)S(1)} %bitcast.19, bf16[512,3584]{1,0:T(8,128)(2,1)S(1)} %interior.1.inner_ref, bf16[512,512]{1,0:T(8,128)(2,1)S(1)} %edges.1.edge_ref), custom_call_target="tpu_custom_call" | custom-call | flops 2147483648 | bytes 4210692 | tf_op jit(solution)/shard_map/own0/pallas_call | solution.py:169
  77.5 7.7 %collective-permute-done.9.rest_2_ = bf16[512,512]{1,0:T(8,128)(2,1)S(1)} collective-permute-done((bf16[512,512]{1,0:T(8,128)(2,1)S(1)}, bf16[512,512]{1,0:T(8,128)(2,1)S(1)}, u32[]{:S(2)}, u32[]{:S(2)}) %collective-permute-start.9) | collective-permute-done | bytes 524320 | tf_op jit(solution)/shard_map/ppermute | solution.py:238
  85.2 3.6 %collective-permute-done.6.rest_1_ = bf16[512,512]{1,0:T(8,128)(2,1)S(1)} collective-permute-done((bf16[512,512]{1,0:T(8,128)(2,1)S(1)}, bf16[512,512]{1,0:T(8,128)(2,1)S(1)}, u32[]{:S(2)}, u32[]{:S(2)}) %collective-permute-start.6) | collective-permute-done | bytes 524320 | tf_op jit(solution)/shard_map/ppermute | solution.py:237
  88.8 1.4 %finish.1 = f32[512,512]{1,0:T(8,128)} custom-call(f32[512,512]{1,0:T(8,128)S(1)} %own0.1.own_ref, bf16[512,512]{1,0:T(8,128)(2,1)S(1)} %collective-permute-done.2.rest_0_, bf16[512,512]{1,0:T(8,128)(2,1)S(1)} %collective-permute-done.6.rest_1_, bf16[512,512]{1,0:T(8,128)(2,1)S(1)} %collective-permute-done.9.rest_2_), custom_call_target="tpu_custom_call" | custom-call | flops 1048576 | bytes 2621440 | tf_op jit(solution)/shard_map/finish/pallas_call | solution.py:169
  (27 shorter events, 1.9 us)
Async XLA Ops:
  1.9 29.0 %collective-permute-start = (bf16[272,512]{1,0:T(8,128)(2,1)S(1)}, bf16[272,512]{1,0:T(8,128)(2,1)S(1)}, u32[]{:S(2)}, u32[]{:S(2)}) collective-permute-start(bf16[272,512]{1,0:T(8,128)(2,1)S(1)} %get-tuple-element.14), channel_id=1, source_target_pairs={{0,1},{1,2},{2,3},{3,4},{4,5},{5,6},{6,7},{7,8},{8,9},{9,10},{10,1... | collective-permute-start | bytes 835592 | tf_op jit(solution)/shard_map/ppermute | solution.py:200
  5.4 25.5 %collective-permute-start.1 = (bf16[272,512]{1,0:T(8,128)(2,1)S(1)}, bf16[272,512]{1,0:T(8,128)(2,1)S(1)}, u32[]{:S(2)}, u32[]{:S(2)}) collective-permute-start(bf16[272,512]{1,0:T(8,128)(2,1)S(1)} %get-tuple-element.13), channel_id=1, source_target_pairs={{1,0},{2,1},{3,2},{4,3},{5,4},{6,5},{7,6},{8,7},{9,8},{10,9},{11,1... | collective-permute-start | bytes 835592 | tf_op jit(solution)/shard_map/ppermute | solution.py:203
  9.6 2.2 %copy-start = (bf16[4096,512]{1,0:T(8,128)(2,1)S(1)}, bf16[4096,512]{1,0:T(8,128)(2,1)}, u32[]{:S(2)}) copy-start(bf16[4096,512]{1,0:T(8,128)(2,1)} %spectra_ref.3) | copy-start | bytes 12582916
  11.8 0.7 copy-start.1
  12.5 0.7 copy-start.2
  30.9 1.8 %copy-start.3 = (s32[4096]{0:T(1024)S(1)}, s32[4096]{0:T(1024)}, u32[]{:S(2)}) copy-start(s32[4096]{0:T(1024)} %param.9) | copy-start | bytes 49156
  43.3 21.8 %collective-permute-start.7 = (bf16[512,512]{1,0:T(8,128)(2,1)S(1)}, bf16[512,512]{1,0:T(8,128)(2,1)S(1)}, u32[]{:S(2)}, u32[]{:S(2)}) collective-permute-start(bf16[512,512]{1,0:T(8,128)(2,1)S(1)} %away3.1), channel_id=1, source_target_pairs={{4,0},{8,4},{12,8},{16,12},{20,16},{24,20},{28,24},{32,28},{36,32}... | collective-permute-start | bytes 1572872 | tf_op jit(solution)/shard_map/ppermute | solution.py:222
  45.2 15.2 %collective-permute-start.4 = (bf16[512,512]{1,0:T(8,128)(2,1)S(1)}, bf16[512,512]{1,0:T(8,128)(2,1)S(1)}, u32[]{:S(2)}, u32[]{:S(2)}) collective-permute-start(bf16[512,512]{1,0:T(8,128)(2,1)S(1)} %away2.1), channel_id=1, source_target_pairs={{4,0},{8,4},{12,8},{16,12},{20,16},{24,20},{28,24},{32,28},{36,32}... | collective-permute-start | bytes 1572872 | tf_op jit(solution)/shard_map/ppermute | solution.py:222
  55.9 9.4 %collective-permute-start.3 = (bf16[512,512]{1,0:T(8,128)(2,1)S(1)}, bf16[512,512]{1,0:T(8,128)(2,1)S(1)}, u32[]{:S(2)}, u32[]{:S(2)}) collective-permute-start(bf16[512,512]{1,0:T(8,128)(2,1)S(1)} %away1.1), channel_id=1, source_target_pairs={{4,0},{8,4},{12,8},{16,12},{20,16},{24,20},{28,24},{32,28},{36,32}... | collective-permute-start | bytes 1572872 | tf_op jit(solution)/shard_map/ppermute | solution.py:222
  57.9 19.7 %collective-permute-start.2 = (bf16[512,512]{1,0:T(8,128)(2,1)S(1)}, bf16[512,512]{1,0:T(8,128)(2,1)S(1)}, u32[]{:S(2)}, u32[]{:S(2)}) collective-permute-start(bf16[512,512]{1,0:T(8,128)(2,1)S(1)} %away0.1), channel_id=1, source_target_pairs={{4,0},{8,4},{12,8},{16,12},{20,16},{24,20},{28,24},{32,28},{36,32}... | collective-permute-start | bytes 1572872 | tf_op jit(solution)/shard_map/ppermute | solution.py:222
  60.6 10.2 %collective-permute-start.8 = (bf16[256,512]{1,0:T(8,128)(2,1)S(1)}, bf16[256,512]{1,0:T(8,128)(2,1)S(1)}, u32[]{:S(2)}, u32[]{:S(2)}) collective-permute-start(bf16[256,512]{1,0:T(8,128)(2,1)S(1)} %get-tuple-element.11), channel_id=1, source_target_pairs={{1,0},{2,1},{3,2},{0,3},{5,4},{6,5},{7,6},{4,7},{9,8},{10,9},{11,1... | collective-permute-start | bytes 786440 | tf_op jit(solution)/shard_map/ppermute | solution.py:230
  65.3 9.4 %collective-permute-start.5 = (bf16[256,512]{1,0:T(8,128)(2,1)S(1)}, bf16[256,512]{1,0:T(8,128)(2,1)S(1)}, u32[]{:S(2)}, u32[]{:S(2)}) collective-permute-start(bf16[256,512]{1,0:T(8,128)(2,1)S(1)} %get-tuple-element.12), channel_id=1, source_target_pairs={{0,1},{1,2},{2,3},{3,0},{4,5},{5,6},{6,7},{7,4},{8,9},{9,10},{10,1... | collective-permute-start | bytes 786440 | tf_op jit(solution)/shard_map/ppermute | solution.py:229
  70.9 14.3 %collective-permute-start.9 = (bf16[512,512]{1,0:T(8,128)(2,1)S(1)}, bf16[512,512]{1,0:T(8,128)(2,1)S(1)}, u32[]{:S(2)}, u32[]{:S(2)}) collective-permute-start(bf16[512,512]{1,0:T(8,128)(2,1)S(1)} %pad_maximum_fusion.1), channel_id=1, source_target_pairs={{1,0},{2,1},{3,2},{0,3},{5,4},{6,5},{7,6},{4,7},{9,8},{10,9},{11,1... | collective-permute-start | bytes 1572872 | tf_op jit(solution)/shard_map/ppermute | solution.py:238
  74.8 14.0 %collective-permute-start.6 = (bf16[512,512]{1,0:T(8,128)(2,1)S(1)}, bf16[512,512]{1,0:T(8,128)(2,1)S(1)}, u32[]{:S(2)}, u32[]{:S(2)}) collective-permute-start(bf16[512,512]{1,0:T(8,128)(2,1)S(1)} %pad_maximum_fusion), channel_id=1, source_target_pairs={{0,1},{1,2},{2,3},{3,0},{4,5},{5,6},{6,7},{7,4},{8,9},{9,10},{10,1... | collective-permute-start | bytes 1572872 | tf_op jit(solution)/shard_map/ppermute | solution.py:237

commit v2 on v1

v2 whole, which is shorter than its diff:
```python
import functools

import jax
import jax.numpy as jnp
from jax import lax
from jax.experimental import pallas as pl
from jax.experimental.pallas import tpu as pltpu
from jax.sharding import PartitionSpec as P


DIM = 512
BLOCK = 256
CL_DEV = 512
ROWS = 4096
NBLK = ROWS // BLOCK
HALO = BLOCK + 16
FAR = -(1 << 24)
SCALE = 3.0 * 1.4426950408889634
f32, bf16, i32 = jnp.float32, jnp.bfloat16, jnp.int32
NT = (((1,), (1,)), ((), ()))


def unit_rows(block):
    values = block.astype(f32)
    square = jnp.sum(values * values, axis=1, keepdims=True)
    return (values * lax.rsqrt(square + 1e-06)).astype(bf16)


def transposed(unit):
    return jnp.transpose(unit)


def attend(query, back, ahead, cap, keys, keys_t, low_cap, high_cap):
    at = lax.broadcasted_iota(i32, (1, BLOCK), 1) + BLOCK
    low = at - back
    high = at + ahead
    own = jnp.minimum(high, cap - 1)
    total = None
    mixed = None
    for k in range(3):
        scores = lax.dot_general(keys[k], query, NT, preferred_element_type=f32)
        slot = lax.broadcasted_iota(i32, (BLOCK, BLOCK), 0) + k * BLOCK
        if k == 0:
            keep = slot >= low
            if low_cap is not None:
                keep = keep & (slot < low_cap)
        elif k == 1:
            keep = ((slot >= low) & (slot <= own)) | (slot == at)
        elif high_cap is None:
            keep = slot <= own
        else:
            keep = slot <= jnp.minimum(high, high_cap - 1)
        weight = jnp.where(keep, jnp.exp2(scores * SCALE - SCALE), 0.0)
        part = jnp.sum(weight, axis=0, keepdims=True)
        term = jnp.dot(keys_t[k], weight.astype(bf16), preferred_element_type=f32)
        total = part if total is None else total + part
        mixed = term if mixed is None else mixed + term
    return (mixed * (1.0 / total)).astype(bf16)


def pack_kernel(live_ref, first_ref, last_ref, low_ref, high_ref):
    live = live_ref[0]
    row = lax.broadcasted_iota(i32, (HALO - BLOCK, DIM), 0)
    digits = jnp.where(row == 0, live >> 6, live & 63).astype(f32).astype(bf16)
    for source, ref in ((first_ref, low_ref), (last_ref, high_ref)):
        ref[:BLOCK, :] = source[...]
        ref[BLOCK:, :] = digits


def interior_kernel(
    live_ref, back_ref, ahead_ref, rows_ref, out_ref,
    unit_ref, unit_t_ref, score_a, score_b, weight_a, weight_b,
):
    live = live_ref[0]

    def block(index):
        return pl.ds(pl.multiple_of(index * BLOCK, BLOCK), BLOCK)

    def prepare(index):
        unit = unit_rows(rows_ref[block(index), :])
        unit_ref[block(index), :] = unit
        unit_t_ref[:, block(index)] = transposed(unit)

    def score(index, score_ref):
        query = unit_ref[block(index), :]
        for k in range(3):
            score_ref[k * BLOCK : (k + 1) * BLOCK, :] = lax.dot_general(
                unit_ref[block(index + k - 1), :], query, NT, preferred_element_type=f32
            )

    def finish(index, score_ref, weight_ref):
        at = lax.broadcasted_iota(i32, (1, BLOCK), 1) + BLOCK
        low = at - back_ref[:, block(index)]
        high = jnp.minimum(at + ahead_ref[:, block(index)], live - (index - 1) * BLOCK - 1)
        total = jnp.zeros((1, BLOCK), f32)
        for k in range(3):
            slot = lax.broadcasted_iota(i32, (BLOCK, BLOCK), 0) + k * BLOCK
            keep = (slot >= low, ((slot >= low) & (slot <= high)) | (slot == at), slot <= high)[k]
            span = slice(k * BLOCK, (k + 1) * BLOCK)
            weight = jnp.where(keep, jnp.exp2(score_ref[span, :] * SCALE - SCALE), 0.0)
            total = total + jnp.sum(weight, axis=0, keepdims=True)
            weight_ref[span, :] = weight.astype(bf16)
        keys_t = unit_t_ref[:, pl.ds(pl.multiple_of((index - 1) * BLOCK, BLOCK), 3 * BLOCK)]
        mixed = jnp.dot(keys_t, weight_ref[...], preferred_element_type=f32)
        out_ref[:, block(index - 1)] = (mixed * (1.0 / total)).astype(bf16)

    def early(index, _):
        prepare(index)
        return 0

    lax.fori_loop(0, 4, early, 0)
    score(1, score_a)

    def step(pair, _):
        index = 2 * pair + 1
        score(index + 1, score_b)
        finish(index, score_a, weight_a)
        prepare(jnp.minimum(index + 3, NBLK - 1))
        score(jnp.minimum(index + 2, NBLK - 2), score_a)
        finish(index + 1, score_b, weight_b)
        prepare(jnp.minimum(index + 4, NBLK - 1))
        return 0

    lax.fori_loop(0, (NBLK - 2) // 2, step, 0)


def edges_kernel(live_ref, back_ref, ahead_ref, spectra_ref, below_ref, above_ref, out_ref):
    live = live_ref[0]

    def count(ref):
        digits = ref[BLOCK : BLOCK + 8, :BLOCK].astype(f32)
        return (digits[0:1] * 64.0 + digits[1:2]).astype(i32)

    def unit(block):
        return unit_rows(spectra_ref[block * BLOCK : (block + 1) * BLOCK, :])

    keys = [unit_rows(below_ref[:BLOCK, :]), unit(0), unit(1)]
    out_ref[:, :BLOCK] = attend(
        keys[1], back_ref[:, :BLOCK], ahead_ref[:, :BLOCK], live + BLOCK, keys,
        [transposed(k) for k in keys], count(below_ref) - (ROWS - BLOCK), None,
    )
    keys = [unit(NBLK - 2), unit(NBLK - 1), unit_rows(above_ref[:BLOCK, :])]
    out_ref[:, BLOCK:] = attend(
        keys[1], back_ref[:, ROWS - BLOCK :], ahead_ref[:, ROWS - BLOCK :],
        live - (ROWS - 2 * BLOCK), keys, [transposed(k) for k in keys],
        None, count(above_ref) + 2 * BLOCK,
    )


INNER = ROWS - 2 * BLOCK
CHUNK = INNER // 4


def added(first, live, ids_ref, rows, start):
    width = rows.shape[1]
    slot = lax.broadcasted_iota(i32, (1, width), 1) + start
    wanted = jnp.where(slot < live, ids_ref[:, start : start + width] - first, FAR)
    hot = lax.broadcasted_iota(i32, (CL_DEV, width), 0) == wanted
    hot = jnp.where(hot, 1.0, 0.0).astype(bf16)
    return lax.dot_general(hot, rows, NT, preferred_element_type=f32)


def sums_kernel(turns, away, halves, rep_count, live_ref, ids_ref, inner_ref, edge_ref, *outs):
    rep = lax.axis_index("rep")
    band = lax.axis_index("mz")
    per_range = CL_DEV * rep_count
    if away:
        band = band + jnp.where(rep == 0, -1, 1)

    def work():
        live = live_ref[0]
        for turn, out_ref in zip(turns, outs):
            owner = lax.rem(rep + turn, rep_count)
            first = band * per_range + owner * CL_DEV

            acc = added(first, live, ids_ref, edge_ref[:, :BLOCK], 0)
            acc = acc + added(first, live, ids_ref, edge_ref[:, BLOCK:], ROWS - BLOCK)
            for start in range(0, INNER, CHUNK):
                acc = acc + added(first, live, ids_ref, inner_ref[:, start : start + CHUNK], start + BLOCK)
            acc = acc.astype(out_ref.dtype)
            if halves:
                outs[0][...] = acc[: CL_DEV // 2]
                outs[1][...] = acc[CL_DEV // 2 :]
            else:
                out_ref[...] = acc

    if away:
        pl.when((rep == 0) | (rep == rep_count - 1))(work)
    else:
        work()


def join_kernel(own_up, own_down, low_half, high_half, moved_1, moved_2, next_up, next_down):
    rep, last = lax.axis_index("rep"), lax.axis_size("rep") - 1
    half = CL_DEV // 2
    far = moved_2[...].astype(f32)
    above = own_up[...] + moved_1[...].astype(f32) + jnp.where(rep == 1, far, 0.0)
    below = own_down[...] + jnp.where(rep == last - 1, far, 0.0)
    next_up[:half, :] = (above[:half] + low_half[...].astype(f32)).astype(bf16)
    next_up[half:, :] = above[half:].astype(bf16)
    next_down[:half, :] = below[:half].astype(bf16)
    next_down[half:, :] = (below[half:] + high_half[...].astype(f32)).astype(bf16)


def finish_kernel(own_ref, *rest):
    out_ref = rest[-1]
    owned = own_ref[...]
    for ref in rest[:-1]:
        owned = owned + ref[...].astype(f32)
    mean = jnp.sum(owned * owned, axis=1, keepdims=True) * (1.0 / DIM)
    out_ref[...] = owned / jnp.sqrt(mean + 1e-06)


VMEM = pl.BlockSpec(memory_space=pltpu.VMEM)
SMEM = pl.BlockSpec(memory_space=pltpu.SMEM)
FARREF = pl.BlockSpec(memory_space=pltpu.HBM)
MIB = 1024 * 1024


def call(kernel, inputs, out_shape, flops, scratch=(), far=(), limit=16):
    one = not isinstance(out_shape, (list, tuple))
    in_specs = [
        FARREF if n in far else SMEM if x.dtype == i32 and x.size < 64 else VMEM for n, x in enumerate(inputs)
    ]
    moved = sum(x.size * x.dtype.itemsize for x in inputs)
    return pl.pallas_call(
        kernel,
        out_shape=out_shape,
        in_specs=in_specs,
        out_specs=VMEM if one else [VMEM] * len(out_shape),
        scratch_shapes=list(scratch),
        cost_estimate=pl.CostEstimate(flops=flops, bytes_accessed=moved, transcendentals=0),
        compiler_params=pltpu.CompilerParams(vmem_limit_bytes=limit * MIB),
    )(*inputs)


def shape(rows, columns, dtype):
    return jax.ShapeDtypeStruct((rows, columns), dtype)


def shards(spectra, reach_back, reach_ahead, live, cluster_ids):
    bands, reps = lax.axis_size("mz"), lax.axis_size("rep")
    every = bands * reps
    both = ("mz", "rep")

    def sum_blocks(turns, away, dtype, halves=False):
        outs = [shape(CL_DEV // 2, DIM, dtype)] * 2 if halves else [shape(CL_DEV, DIM, dtype)] * len(turns)
        return call(
            functools.partial(sums_kernel, turns, away, halves, reps),
            [live, ids, inner, edge], outs,
            2 * CL_DEV * ROWS * DIM * len(turns),
        )

    back, ahead, ids = (x.reshape(1, ROWS) for x in (reach_back, reach_ahead, cluster_ids))
    low_rows, high_rows = call(
        pack_kernel, [live, spectra[:BLOCK], spectra[ROWS - BLOCK :]],
        [shape(HALO, DIM, bf16)] * 2, 1 << 33, limit=2,
    )
    from_below = lax.ppermute(high_rows, both, [(i, i + 1) for i in range(every - 1)])
    from_above = lax.ppermute(low_rows, both, [(i + 1, i) for i in range(every - 1)])
    per_block = 4 * BLOCK * 3 * BLOCK * DIM
    inner = call(
        interior_kernel, [live, back, ahead, spectra], shape(DIM, INNER, bf16), per_block * (NBLK - 2),
        [
            pltpu.VMEM((ROWS, DIM), bf16), pltpu.VMEM((DIM, ROWS), bf16),
            pltpu.VMEM((3 * BLOCK, BLOCK), f32), pltpu.VMEM((3 * BLOCK, BLOCK), f32),
            pltpu.VMEM((3 * BLOCK, BLOCK), bf16), pltpu.VMEM((3 * BLOCK, BLOCK), bf16),
        ],
        limit=32,
    )
    edge = call(
        edges_kernel, [live, back, ahead, spectra, from_below, from_above],
        shape(DIM, 2 * BLOCK, bf16), 2 * per_block,
    )

    def away_pairs(inwards):
        pairs = [(d * reps, (d - 1) * reps + inwards % reps) for d in range(1, bands)]
        return pairs + [
            (d * reps + reps - 1, (d + 1) * reps + (reps - 1 - inwards) % reps) for d in range(bands - 1)
        ]

    last = reps - 1
    up = [(i, (i + 1) % reps) for i in range(reps)]
    down = [(b, a) for a, b in up]
    low_half, high_half = sum_blocks((2,), False, bf16, halves=True)
    low_half = lax.ppermute(low_half, "rep", up)
    high_half = lax.ppermute(high_half, "rep", down)
    (block,) = sum_blocks((2,), True, bf16)
    moved_2 = lax.ppermute(block, both, away_pairs(1))
    (block,) = sum_blocks((1,), True, bf16)
    moved_1 = lax.ppermute(block, both, away_pairs(0))
    own_1, own_3 = sum_blocks((1, 3), False, f32)
    next_up, next_down = call(
        join_kernel, [own_1, own_3, low_half, high_half, moved_1, moved_2],
        [shape(CL_DEV, DIM, bf16)] * 2, 1 << 20,
    )
    got_up = lax.ppermute(next_up, "rep", up)
    got_down = lax.ppermute(next_down, "rep", down)
    (block,) = sum_blocks((3,), True, bf16)
    pairs = [(d * reps, (d - 1) * reps + last) for d in range(1, bands)]
    pairs += [(d * reps + last, (d + 1) * reps + last - 1) for d in range(bands - 1)]
    moved_3 = lax.ppermute(block, both, pairs)
    (block,) = sum_blocks((0,), True, bf16)
    moved_0 = lax.ppermute(block, both, away_pairs(0))
    (own_0,) = sum_blocks((0,), False, f32)
    return call(finish_kernel, [own_0, got_up, got_down, moved_3, moved_0], shape(CL_DEV, DIM, f32), 1 << 20)


def solution(mesh):
    rows = P(("mz", "rep"))

    return jax.shard_map(
        shards,
        mesh=mesh,
        in_specs=(P(("mz", "rep"), None), rows, rows, rows, rows),
        out_specs=P(("mz", "rep"), None),
        check_vma=False,
    )
```

time: 90.6 us -> 80.1 us (0.88)
  the two profiles are of different devices: /device:TPU:102 before, /device:TPU:144 now
where the time goes in v2:
time: 80.1 us; the launch traced here: 79.8 us
  waiting for transfers between devices  33 us (41%)
  Pallas kernels  24.7 us (31%)
  starting transfers between devices  20.2 us (25%)
  local copies, waits for them, and re-layouts  1.09 us (1%)
  between operations  0.88 us (1%)
    pallas_call x12, Pallas kernels, call(): pl.pallas_call(kernel, out_shape=out_shape, in_specs=in_specs, out_specs=...  24.7 us
    ppermute x1, waiting for transfers between devices, shards(): high_half = lax.ppermute(high_half, 'rep', down)  16.5 us
    ppermute x1, waiting for transfers between devices, shards(): got_up = lax.ppermute(next_up, 'rep', up)  8.8 us
    ppermute x1, starting transfers between devices, shards(): low_half = lax.ppermute(low_half, 'rep', up)  7.84 us
    ppermute x1, waiting for transfers between devices, shards(): low_half = lax.ppermute(low_half, 'rep', up)  4.76 us
    ppermute x1, starting transfers between devices, shards(): lax.ppermute(high_rows, both, [(i, i + 1) for i in range(every - 1)])  3.45 us
    ppermute x1, waiting for transfers between devices, shards(): got_down = lax.ppermute(next_down, 'rep', down)  2.91 us
    ppermute x1, starting transfers between devices, shards(): lax.ppermute(low_rows, both, [(i + 1, i) for i in range(every - 1)])  2.65 us
  transfers between devices with their start and end apart: 10, of which 4 were waited for; matrix products, arithmetic and copies ran while one was open for 0% of the time, Pallas kernels for 20%

profile of v2, /device:TPU:144, one launch (start us, length us, event | category | flops | bytes accessed | tf_op | source)
XLA Modules:
  0.0 79.8 jit_solution(11750649701416150661)
XLA Ops:
  0.7 1.1 %fusion = (bf16[256,512]{1,0:T(8,128)(2,1)S(1)}, bf16[256,512]{1,0:T(8,128)(2,1)S(1)}) fusion(bf16[4096,512]{1,0:T(8,128)(2,1)} %spectra_ref.1), kind=kLoop, calls=%fused_computation | loop fusion | bytes 1048576 | tf_op jit(solution)/shard_map/slice | solution.py:256
  1.7 0.0 copy-start
  1.7 0.0 copy-start.1
  1.8 3.5 %collective-permute-start = (bf16[272,512]{1,0:T(8,128)(2,1)S(1)}, bf16[272,512]{1,0:T(8,128)(2,1)S(1)}, u32[]{:S(2)}, u32[]{:S(2)}) collective-permute-start(bf16[272,512]{1,0:T(8,128)(2,1)S(1)} %get-tuple-element.13), channel_id=1, source_target_pairs={{0,1},{1,2},{2,3},{3,4},{4,5},{5,6},{6,7},{7,8},{8,9},{9,10},{10,1... | collective-permute-start | bytes 835592 | tf_op jit(solution)/shard_map/ppermute | solution.py:259
  5.3 2.7 %collective-permute-start.1 = (bf16[272,512]{1,0:T(8,128)(2,1)S(1)}, bf16[272,512]{1,0:T(8,128)(2,1)S(1)}, u32[]{:S(2)}, u32[]{:S(2)}) collective-permute-start(bf16[272,512]{1,0:T(8,128)(2,1)S(1)} %get-tuple-element.14), channel_id=1, source_target_pairs={{1,0},{2,1},{3,2},{4,3},{5,4},{6,5},{7,6},{8,7},{9,8},{10,9},{11,1... | collective-permute-start | bytes 835592 | tf_op jit(solution)/shard_map/ppermute | solution.py:260
  8.0 10.7 %shard_map.55.inner_ref = bf16[512,3584]{1,0:T(8,128)(2,1)S(1)} custom-call(s32[1]{0:T(128)S(6)} %copy.6.live_ref, s32[1,4096]{1,0:T(1,128)S(1)} %bitcast.3, s32[1,4096]{1,0:T(1,128)S(1)} %bitcast.5, bf16[4096,512]{1,0:T(8,128)(2,1)S(1)} %copy-done), custom_call_target="tpu_custom_call" | custom-call | flops 5637144576 | bytes 4227076 | tf_op jit(solution)/shard_map/pallas_call | solution.py:226
  18.7 0.0 copy-start.3
  18.7 1.8 %shard_map.57.edge_ref = bf16[512,512]{1,0:T(8,128)(2,1)S(1)} custom-call(s32[1]{0:T(128)S(6)} %copy.6.live_ref, s32[1,4096]{1,0:T(1,128)S(1)} %bitcast.4, s32[1,4096]{1,0:T(1,128)S(1)} %bitcast.6, bf16[4096,512]{1,0:T(8,128)(2,1)S(1)} %copy-done, bf16[272,512]{1,0:T(8,128)(2,1)S(1)} %collective-permute-done.below_ref, ...), custom_call_target="tpu_custom_call" | custom-call | flops 805306368 | bytes 4784132 | tf_op jit(solution)/shard_map/pallas_call | solution.py:226
  20.5 5.1 %shard_map.59 = (f32[512,512]{1,0:T(8,128)S(1)}, f32[512,512]{1,0:T(8,128)S(1)}) custom-call(s32[1]{0:T(128)S(6)} %copy.6.live_ref, s32[1,4096]{1,0:T(1,128)S(1)} %bitcast.9, bf16[512,3584]{1,0:T(8,128)(2,1)S(1)} %shard_map.55.inner_ref, bf16[512,512]{1,0:T(8,128)(2,1)S(1)} %shard_map.57.edge_ref), custom_call_target="tpu_custom_call" | custom-call | flops 4294967296 | bytes 4210692 | tf_op jit(solution)/shard_map/pallas_call | solution.py:226
  25.6 0.7 collective-permute-start.4
  26.3 1.5 %collective-permute-start.5 = (bf16[512,512]{1,0:T(8,128)(2,1)S(1)}, bf16[512,512]{1,0:T(8,128)(2,1)S(1)}, u32[]{:S(2)}, u32[]{:S(2)}) collective-permute-start(bf16[512,512]{1,0:T(8,128)(2,1)S(1)} %shard_map.62), channel_id=1, source_target_pairs={{4,1},{8,5},{12,9},{16,13},{20,17},{24,21},{28,25},{32,29},{36,33}... | collective-permute-start | bytes 1572872 | tf_op jit(solution)/shard_map/ppermute | solution.py:289
  27.8 2.6 %shard_map.60 = (bf16[256,512]{1,0:T(8,128)(2,1)S(1)}, bf16[256,512]{1,0:T(8,128)(2,1)S(1)}) custom-call(s32[1]{0:T(128)S(6)} %copy.6.live_ref, s32[1,4096]{1,0:T(1,128)S(1)} %bitcast.10, bf16[512,3584]{1,0:T(8,128)(2,1)S(1)} %shard_map.55.inner_ref, bf16[512,512]{1,0:T(8,128)(2,1)S(1)} %shard_map.57.edge_ref), custom_call_target="tpu_custom_call" | custom-call | flops 2147483648 | bytes 4210692 | tf_op jit(solution)/shard_map/pallas_call | solution.py:226
  30.4 7.8 %collective-permute-start.2 = (bf16[256,512]{1,0:T(8,128)(2,1)S(1)}, bf16[256,512]{1,0:T(8,128)(2,1)S(1)}, u32[]{:S(2)}, u32[]{:S(2)}) collective-permute-start(bf16[256,512]{1,0:T(8,128)(2,1)S(1)} %get-tuple-element.17), channel_id=1, source_target_pairs={{0,1},{1,2},{2,3},{3,0},{4,5},{5,6},{6,7},{7,4},{8,9},{9,10},{10,1... | collective-permute-start | bytes 786440 | tf_op jit(solution)/shard_map/ppermute | solution.py:286
  38.3 1.3 %collective-permute-start.8 = (bf16[512,512]{1,0:T(8,128)(2,1)S(1)}, bf16[512,512]{1,0:T(8,128)(2,1)S(1)}, u32[]{:S(2)}, u32[]{:S(2)}) collective-permute-start(bf16[512,512]{1,0:T(8,128)(2,1)S(1)} %shard_map.64), channel_id=1, source_target_pairs={{4,3},{8,7},{12,11},{16,15},{20,19},{24,23},{28,27},{32,31},{36,35... | collective-permute-start | bytes 1572872 | tf_op jit(solution)/shard_map/ppermute | solution.py:302
  39.6 4.8 %collective-permute-done.2.low_half = bf16[256,512]{1,0:T(8,128)(2,1)S(1)} collective-permute-done((bf16[256,512]{1,0:T(8,128)(2,1)S(1)}, bf16[256,512]{1,0:T(8,128)(2,1)S(1)}, u32[]{:S(2)}, u32[]{:S(2)}) %collective-permute-start.2) | collective-permute-done | bytes 262176 | tf_op jit(solution)/shard_map/ppermute | solution.py:286
  44.3 0.7 collective-permute-start.9
  45.0 16.5 %collective-permute-done.3.high_half = bf16[256,512]{1,0:T(8,128)(2,1)S(1)} collective-permute-done((bf16[256,512]{1,0:T(8,128)(2,1)S(1)}, bf16[256,512]{1,0:T(8,128)(2,1)S(1)}, u32[]{:S(2)}, u32[]{:S(2)}) %collective-permute-start.3) | collective-permute-done | bytes 262176 | tf_op jit(solution)/shard_map/ppermute | solution.py:287
  61.6 0.4 shard_map.63
  61.9 0.1 collective-permute-start.6
  62.0 2.0 %collective-permute-start.7 = (bf16[512,512]{1,0:T(8,128)(2,1)S(1)}, bf16[512,512]{1,0:T(8,128)(2,1)S(1)}, u32[]{:S(2)}, u32[]{:S(2)}) collective-permute-start(bf16[512,512]{1,0:T(8,128)(2,1)S(1)} %get-tuple-element.20), channel_id=1, source_target_pairs={{1,0},{2,1},{3,2},{0,3},{5,4},{6,5},{7,6},{4,7},{9,8},{10,9},{11,1... | collective-permute-start | bytes 1572872 | tf_op jit(solution)/shard_map/ppermute | solution.py:298
  64.0 2.6 %shard_map.58.own_ref = f32[512,512]{1,0:T(8,128)S(1)} custom-call(s32[1]{0:T(128)S(6)} %copy.6.live_ref, s32[1,4096]{1,0:T(1,128)S(1)} %bitcast.13, bf16[512,3584]{1,0:T(8,128)(2,1)S(1)} %shard_map.55.inner_ref, bf16[512,512]{1,0:T(8,128)(2,1)S(1)} %shard_map.57.edge_ref), custom_call_target="tpu_custom_call" | custom-call | flops 2147483648 | bytes 4210692 | tf_op jit(solution)/shard_map/pallas_call | solution.py:226
  66.7 8.8 %collective-permute-done.6.rest_0_ = bf16[512,512]{1,0:T(8,128)(2,1)S(1)} collective-permute-done((bf16[512,512]{1,0:T(8,128)(2,1)S(1)}, bf16[512,512]{1,0:T(8,128)(2,1)S(1)}, u32[]{:S(2)}, u32[]{:S(2)}) %collective-permute-start.6) | collective-permute-done | bytes 524320 | tf_op jit(solution)/shard_map/ppermute | solution.py:297
  75.5 2.9 %collective-permute-done.7.rest_1_ = bf16[512,512]{1,0:T(8,128)(2,1)S(1)} collective-permute-done((bf16[512,512]{1,0:T(8,128)(2,1)S(1)}, bf16[512,512]{1,0:T(8,128)(2,1)S(1)}, u32[]{:S(2)}, u32[]{:S(2)}) %collective-permute-start.7) | collective-permute-done | bytes 524320 | tf_op jit(solution)/shard_map/ppermute | solution.py:298
  78.4 1.4 %shard_map.66 = f32[512,512]{1,0:T(8,128)} custom-call(f32[512,512]{1,0:T(8,128)S(1)} %shard_map.58.own_ref, bf16[512,512]{1,0:T(8,128)(2,1)S(1)} %collective-permute-done.6.rest_0_, bf16[512,512]{1,0:T(8,128)(2,1)S(1)} %collective-permute-done.7.rest_1_, bf16[512,512]{1,0:T(8,128)(2,1)S(1)} %collective-permute-done.8.rest_2_, ...), custom_call_target="tpu_custom_call" | custom-call | flops 1048576 | bytes 3145728 | tf_op jit(solution)/shard_map/pallas_call | solution.py:226
  (17 shorter events, 0.1 us)
Async XLA Ops:
  1.7 6.2 %copy-start = (bf16[4096,512]{1,0:T(8,128)(2,1)S(1)}, bf16[4096,512]{1,0:T(8,128)(2,1)}, u32[]{:S(2)}) copy-start(bf16[4096,512]{1,0:T(8,128)(2,1)} %spectra_ref.1) | copy-start | bytes 12582916
  1.7 6.2 %copy-start.1 = (s32[4096]{0:T(1024)S(1)}, s32[4096]{0:T(1024)}, u32[]{:S(2)}) copy-start(s32[4096]{0:T(1024)} %param.6) | copy-start | bytes 49156
  1.7 6.2 %copy-start.2 = (s32[4096]{0:T(1024)S(1)}, s32[4096]{0:T(1024)}, u32[]{:S(2)}) copy-start(s32[4096]{0:T(1024)} %param.7) | copy-start | bytes 49156
  1.8 16.9 %collective-permute-start = (bf16[272,512]{1,0:T(8,128)(2,1)S(1)}, bf16[272,512]{1,0:T(8,128)(2,1)S(1)}, u32[]{:S(2)}, u32[]{:S(2)}) collective-permute-start(bf16[272,512]{1,0:T(8,128)(2,1)S(1)} %get-tuple-element.13), channel_id=1, source_target_pairs={{0,1},{1,2},{2,3},{3,4},{4,5},{5,6},{6,7},{7,8},{8,9},{9,10},{10,1... | collective-permute-start | bytes 835592 | tf_op jit(solution)/shard_map/ppermute | solution.py:259
  5.3 13.4 %collective-permute-start.1 = (bf16[272,512]{1,0:T(8,128)(2,1)S(1)}, bf16[272,512]{1,0:T(8,128)(2,1)S(1)}, u32[]{:S(2)}, u32[]{:S(2)}) collective-permute-start(bf16[272,512]{1,0:T(8,128)(2,1)S(1)} %get-tuple-element.14), channel_id=1, source_target_pairs={{1,0},{2,1},{3,2},{4,3},{5,4},{6,5},{7,6},{8,7},{9,8},{10,9},{11,1... | collective-permute-start | bytes 835592 | tf_op jit(solution)/shard_map/ppermute | solution.py:260
  18.7 1.8 %copy-start.3 = (s32[4096]{0:T(1024)S(1)}, s32[4096]{0:T(1024)}, u32[]{:S(2)}) copy-start(s32[4096]{0:T(1024)} %param.9) | copy-start | bytes 49156
  25.6 36.0 %collective-permute-start.4 = (bf16[512,512]{1,0:T(8,128)(2,1)S(1)}, bf16[512,512]{1,0:T(8,128)(2,1)S(1)}, u32[]{:S(2)}, u32[]{:S(2)}) collective-permute-start(bf16[512,512]{1,0:T(8,128)(2,1)S(1)} %shard_map.61), channel_id=1, source_target_pairs={{4,0},{8,4},{12,8},{16,12},{20,16},{24,20},{28,24},{32,28},{36,32}... | collective-permute-start | bytes 1572872 | tf_op jit(solution)/shard_map/ppermute | solution.py:291
  26.3 35.3 %collective-permute-start.5 = (bf16[512,512]{1,0:T(8,128)(2,1)S(1)}, bf16[512,512]{1,0:T(8,128)(2,1)S(1)}, u32[]{:S(2)}, u32[]{:S(2)}) collective-permute-start(bf16[512,512]{1,0:T(8,128)(2,1)S(1)} %shard_map.62), channel_id=1, source_target_pairs={{4,1},{8,5},{12,9},{16,13},{20,17},{24,21},{28,25},{32,29},{36,33}... | collective-permute-start | bytes 1572872 | tf_op jit(solution)/shard_map/ppermute | solution.py:289
  30.4 13.9 %collective-permute-start.2 = (bf16[256,512]{1,0:T(8,128)(2,1)S(1)}, bf16[256,512]{1,0:T(8,128)(2,1)S(1)}, u32[]{:S(2)}, u32[]{:S(2)}) collective-permute-start(bf16[256,512]{1,0:T(8,128)(2,1)S(1)} %get-tuple-element.17), channel_id=1, source_target_pairs={{0,1},{1,2},{2,3},{3,0},{4,5},{5,6},{6,7},{7,4},{8,9},{9,10},{10,1... | collective-permute-start | bytes 786440 | tf_op jit(solution)/shard_map/ppermute | solution.py:286
  38.3 23.3 %collective-permute-start.3 = (bf16[256,512]{1,0:T(8,128)(2,1)S(1)}, bf16[256,512]{1,0:T(8,128)(2,1)S(1)}, u32[]{:S(2)}, u32[]{:S(2)}) collective-permute-start(bf16[256,512]{1,0:T(8,128)(2,1)S(1)} %get-tuple-element.18), channel_id=1, source_target_pairs={{1,0},{2,1},{3,2},{0,3},{5,4},{6,5},{7,6},{4,7},{9,8},{10,9},{11,1... | collective-permute-start | bytes 786440 | tf_op jit(solution)/shard_map/ppermute | solution.py:287
  38.3 28.4 %collective-permute-start.8 = (bf16[512,512]{1,0:T(8,128)(2,1)S(1)}, bf16[512,512]{1,0:T(8,128)(2,1)S(1)}, u32[]{:S(2)}, u32[]{:S(2)}) collective-permute-start(bf16[512,512]{1,0:T(8,128)(2,1)S(1)} %shard_map.64), channel_id=1, source_target_pairs={{4,3},{8,7},{12,11},{16,15},{20,19},{24,23},{28,27},{32,31},{36,35... | collective-permute-start | bytes 1572872 | tf_op jit(solution)/shard_map/ppermute | solution.py:302
  44.3 22.4 %collective-permute-start.9 = (bf16[512,512]{1,0:T(8,128)(2,1)S(1)}, bf16[512,512]{1,0:T(8,128)(2,1)S(1)}, u32[]{:S(2)}, u32[]{:S(2)}) collective-permute-start(bf16[512,512]{1,0:T(8,128)(2,1)S(1)} %shard_map.65), channel_id=1, source_target_pairs={{4,0},{8,4},{12,8},{16,12},{20,16},{24,20},{28,24},{32,28},{36,32}... | collective-permute-start | bytes 1572872 | tf_op jit(solution)/shard_map/ppermute | solution.py:304
  61.9 13.6 %collective-permute-start.6 = (bf16[512,512]{1,0:T(8,128)(2,1)S(1)}, bf16[512,512]{1,0:T(8,128)(2,1)S(1)}, u32[]{:S(2)}, u32[]{:S(2)}) collective-permute-start(bf16[512,512]{1,0:T(8,128)(2,1)S(1)} %get-tuple-element.19), channel_id=1, source_target_pairs={{0,1},{1,2},{2,3},{3,0},{4,5},{5,6},{6,7},{7,4},{8,9},{9,10},{10,1... | collective-permute-start | bytes 1572872 | tf_op jit(solution)/shard_map/ppermute | solution.py:297
  62.0 16.4 %collective-permute-start.7 = (bf16[512,512]{1,0:T(8,128)(2,1)S(1)}, bf16[512,512]{1,0:T(8,128)(2,1)S(1)}, u32[]{:S(2)}, u32[]{:S(2)}) collective-permute-start(bf16[512,512]{1,0:T(8,128)(2,1)S(1)} %get-tuple-element.20), channel_id=1, source_target_pairs={{1,0},{2,1},{3,2},{0,3},{5,4},{6,5},{7,6},{4,7},{9,8},{10,9},{11,1... | collective-permute-start | bytes 1572872 | tf_op jit(solution)/shard_map/ppermute | solution.py:298

commit v3 on v2

--- a/solution.py
+++ b/solution.py
@@ -160,7 +160,7 @@
     return lax.dot_general(hot, rows, NT, preferred_element_type=f32)
 
 
-def sums_kernel(turns, away, halves, rep_count, live_ref, ids_ref, inner_ref, edge_ref, *outs):
+def sums_kernel(turns, away, rep_count, live_ref, ids_ref, inner_ref, edge_ref, *outs):
     rep = lax.axis_index("rep")
     band = lax.axis_index("mz")
     per_range = CL_DEV * rep_count
@@ -177,12 +177,7 @@
             acc = acc + added(first, live, ids_ref, edge_ref[:, BLOCK:], ROWS - BLOCK)
             for start in range(0, INNER, CHUNK):
                 acc = acc + added(first, live, ids_ref, inner_ref[:, start : start + CHUNK], start + BLOCK)
-            acc = acc.astype(out_ref.dtype)
-            if halves:
-                outs[0][...] = acc[: CL_DEV // 2]
-                outs[1][...] = acc[CL_DEV // 2 :]
-            else:
-                out_ref[...] = acc
+            out_ref[...] = acc.astype(out_ref.dtype)
 
     if away:
         pl.when((rep == 0) | (rep == rep_count - 1))(work)
@@ -190,12 +185,16 @@
         work()
 
 
-def join_kernel(own_up, own_down, low_half, high_half, moved_1, moved_2, next_up, next_down):
-    rep, last = lax.axis_index("rep"), lax.axis_size("rep") - 1
+def far_kernel(own_ref, moved_ref, low_ref, high_ref):
+    total = (own_ref[...] + moved_ref[...].astype(f32)).astype(bf16)
+    low_ref[...] = total[: CL_DEV // 2]
+    high_ref[...] = total[CL_DEV // 2 :]
+
+
+def join_kernel(own_up, own_down, low_half, high_half, moved_1, moved_3, next_up, next_down):
     half = CL_DEV // 2
-    far = moved_2[...].astype(f32)
-    above = own_up[...] + moved_1[...].astype(f32) + jnp.where(rep == 1, far, 0.0)
-    below = own_down[...] + jnp.where(rep == last - 1, far, 0.0)
+    above = own_up[...] + moved_1[...].astype(f32)
+    below = own_down[...] + moved_3[...].astype(f32)
     next_up[:half, :] = (above[:half] + low_half[...].astype(f32)).astype(bf16)
     next_up[half:, :] = above[half:].astype(bf16)
     next_down[:half, :] = below[:half].astype(bf16)
@@ -243,10 +242,10 @@
     every = bands * reps
     both = ("mz", "rep")
 
-    def sum_blocks(turns, away, dtype, halves=False):
-        outs = [shape(CL_DEV // 2, DIM, dtype)] * 2 if halves else [shape(CL_DEV, DIM, dtype)] * len(turns)
+    def sum_blocks(turns, away, dtype):
+        outs = [shape(CL_DEV, DIM, dtype)] * len(turns)
         return call(
-            functools.partial(sums_kernel, turns, away, halves, reps),
+            functools.partial(sums_kernel, turns, away, reps),
             [live, ids, inner, edge], outs,
             2 * CL_DEV * ROWS * DIM * len(turns),
         )
@@ -273,37 +272,36 @@
         shape(DIM, 2 * BLOCK, bf16), 2 * per_block,
     )
 
-    def away_pairs(inwards):
-        pairs = [(d * reps, (d - 1) * reps + inwards % reps) for d in range(1, bands)]
-        return pairs + [
-            (d * reps + reps - 1, (d + 1) * reps + (reps - 1 - inwards) % reps) for d in range(bands - 1)
-        ]
-
     last = reps - 1
+    away_pairs = [(d * reps, (d - 1) * reps) for d in range(1, bands)]
+    away_pairs += [(d * reps + last, (d + 1) * reps + last) for d in range(bands - 1)]
     up = [(i, (i + 1) % reps) for i in range(reps)]
     down = [(b, a) for a, b in up]
-    low_half, high_half = sum_blocks((2,), False, bf16, halves=True)
+    arrived = {}
+    own = {}
+
+    def send_away(turn):
+        (block,) = sum_blocks((turn,), True, bf16)
+        arrived[turn] = lax.ppermute(block, both, away_pairs)
+
+    send_away(2)
+    (own[2],) = sum_blocks((2,), False, f32)
+    send_away(1)
+    half = shape(CL_DEV // 2, DIM, bf16)
+    low_half, high_half = call(far_kernel, [own[2], arrived[2]], [half] * 2, 1 << 20)
     low_half = lax.ppermute(low_half, "rep", up)
     high_half = lax.ppermute(high_half, "rep", down)
-    (block,) = sum_blocks((2,), True, bf16)
-    moved_2 = lax.ppermute(block, both, away_pairs(1))
-    (block,) = sum_blocks((1,), True, bf16)
-    moved_1 = lax.ppermute(block, both, away_pairs(0))
-    own_1, own_3 = sum_blocks((1, 3), False, f32)
+    send_away(3)
+    own[1], own[3] = sum_blocks((1, 3), False, f32)
     next_up, next_down = call(
-        join_kernel, [own_1, own_3, low_half, high_half, moved_1, moved_2],
+        join_kernel, [own[1], own[3], low_half, high_half, arrived[1], arrived[3]],
         [shape(CL_DEV, DIM, bf16)] * 2, 1 << 20,
     )
     got_up = lax.ppermute(next_up, "rep", up)
     got_down = lax.ppermute(next_down, "rep", down)
-    (block,) = sum_blocks((3,), True, bf16)
-    pairs = [(d * reps, (d - 1) * reps + last) for d in range(1, bands)]
-    pairs += [(d * reps + last, (d + 1) * reps + last - 1) for d in range(bands - 1)]
-    moved_3 = lax.ppermute(block, both, pairs)
-    (block,) = sum_blocks((0,), True, bf16)
-    moved_0 = lax.ppermute(block, both, away_pairs(0))
-    (own_0,) = sum_blocks((0,), False, f32)
-    return call(finish_kernel, [own_0, got_up, got_down, moved_3, moved_0], shape(CL_DEV, DIM, f32), 1 << 20)
+    send_away(0)
+    (own[0],) = sum_blocks((0,), False, f32)
+    return call(finish_kernel, [own[0], got_up, got_down, arrived[0]], shape(CL_DEV, DIM, f32), 1 << 20)
 
 
 def solution(mesh):

time: 80.1 us -> 74.1 us (0.925)
  the two profiles are of different devices: /device:TPU:144 before, /device:TPU:130 now
where the time goes in v3:
time: 74.1 us; the launch traced here: 73.8 us
  Pallas kernels  35.2 us (48%)
  starting transfers between devices  26.2 us (35%)
  waiting for transfers between devices  10.4 us (14%)
  local copies, waits for them, and re-layouts  1.09 us (1%)
  between operations  0.91 us (1%)
    pallas_call x13, Pallas kernels, call(): pl.pallas_call(kernel, out_shape=out_shape, in_specs=in_specs, out_specs=...  35.2 us
    ppermute x4, starting transfers between devices, send_away(): arrived[turn] = lax.ppermute(block, both, away_pairs)  11.6 us
    ppermute x1, waiting for transfers between devices, shards(): got_up = lax.ppermute(next_up, 'rep', up)  8.8 us
    ppermute x1, starting transfers between devices, shards(): lax.ppermute(low_rows, both, [(i + 1, i) for i in range(every - 1)])  4.19 us
    ppermute x1, starting transfers between devices, shards(): lax.ppermute(high_rows, both, [(i, i + 1) for i in range(every - 1)])  3.75 us
    ppermute x1, starting transfers between devices, shards(): high_half = lax.ppermute(high_half, 'rep', down)  3.22 us
    ppermute x1, starting transfers between devices, shards(): got_down = lax.ppermute(next_down, 'rep', down)  3.22 us
    ppermute x1, waiting for transfers between devices, shards(): low_half = lax.ppermute(low_half, 'rep', up)  1.6 us
  transfers between devices with their start and end apart: 10, of which 2 were waited for; matrix products, arithmetic and copies ran while one was open for 0% of the time, Pallas kernels for 36%

profile of v3, /device:TPU:130, one launch (start us, length us, event | category | flops | bytes accessed | tf_op | source)
XLA Modules:
  0.0 73.8 jit_solution(17150099053158216385)
XLA Ops:
  0.7 1.1 %fusion = (bf16[256,512]{1,0:T(8,128)(2,1)S(1)}, bf16[256,512]{1,0:T(8,128)(2,1)S(1)}) fusion(bf16[4096,512]{1,0:T(8,128)(2,1)} %spectra_ref.1), kind=kLoop, calls=%fused_computation | loop fusion | bytes 1048576 | tf_op jit(solution)/shard_map/slice | solution.py:255
  1.8 3.7 %collective-permute-start = (bf16[272,512]{1,0:T(8,128)(2,1)S(1)}, bf16[272,512]{1,0:T(8,128)(2,1)S(1)}, u32[]{:S(2)}, u32[]{:S(2)}) collective-permute-start(bf16[272,512]{1,0:T(8,128)(2,1)S(1)} %get-tuple-element.13), channel_id=1, source_target_pairs={{0,1},{1,2},{2,3},{3,4},{4,5},{5,6},{6,7},{7,8},{8,9},{9,10},{10,1... | collective-permute-start | bytes 835592 | tf_op jit(solution)/shard_map/ppermute | solution.py:258
  5.6 4.2 %collective-permute-start.1 = (bf16[272,512]{1,0:T(8,128)(2,1)S(1)}, bf16[272,512]{1,0:T(8,128)(2,1)S(1)}, u32[]{:S(2)}, u32[]{:S(2)}) collective-permute-start(bf16[272,512]{1,0:T(8,128)(2,1)S(1)} %get-tuple-element.14), channel_id=1, source_target_pairs={{1,0},{2,1},{3,2},{4,3},{5,4},{6,5},{7,6},{8,7},{9,8},{10,9},{11,1... | collective-permute-start | bytes 835592 | tf_op jit(solution)/shard_map/ppermute | solution.py:259
  9.8 10.7 %shard_map.55.inner_ref = bf16[512,3584]{1,0:T(8,128)(2,1)S(1)} custom-call(s32[1]{0:T(128)S(6)} %copy.6.live_ref, s32[1,4096]{1,0:T(1,128)S(1)} %bitcast.3, s32[1,4096]{1,0:T(1,128)S(1)} %bitcast.5, bf16[4096,512]{1,0:T(8,128)(2,1)S(1)} %copy-done), custom_call_target="tpu_custom_call" | custom-call | flops 5637144576 | bytes 4227076 | tf_op jit(solution)/shard_map/pallas_call | solution.py:225
  20.5 1.8 %shard_map.57.edge_ref = bf16[512,512]{1,0:T(8,128)(2,1)S(1)} custom-call(s32[1]{0:T(128)S(6)} %copy.6.live_ref, s32[1,4096]{1,0:T(1,128)S(1)} %bitcast.4, s32[1,4096]{1,0:T(1,128)S(1)} %bitcast.6, bf16[4096,512]{1,0:T(8,128)(2,1)S(1)} %copy-done, bf16[272,512]{1,0:T(8,128)(2,1)S(1)} %collective-permute-done.below_ref, ...), custom_call_target="tpu_custom_call" | custom-call | flops 805306368 | bytes 4784132 | tf_op jit(solution)/shard_map/pallas_call | solution.py:225
  22.3 2.6 %shard_map.61 = bf16[512,512]{1,0:T(8,128)(2,1)S(1)} custom-call(s32[1]{0:T(128)S(6)} %copy.6.live_ref, s32[1,4096]{1,0:T(1,128)S(1)} %bitcast.7, bf16[512,3584]{1,0:T(8,128)(2,1)S(1)} %shard_map.55.inner_ref, bf16[512,512]{1,0:T(8,128)(2,1)S(1)} %shard_map.57.edge_ref), custom_call_target="tpu_custom_call" | custom-call | flops 2147483648 | bytes 4210692 | tf_op jit(solution)/shard_map/pallas_call | solution.py:225
  25.0 2.6 %shard_map.63 = bf16[512,512]{1,0:T(8,128)(2,1)S(1)} custom-call(s32[1]{0:T(128)S(6)} %copy.6.live_ref, s32[1,4096]{1,0:T(1,128)S(1)} %bitcast.8, bf16[512,3584]{1,0:T(8,128)(2,1)S(1)} %shard_map.55.inner_ref, bf16[512,512]{1,0:T(8,128)(2,1)S(1)} %shard_map.57.edge_ref), custom_call_target="tpu_custom_call" | custom-call | flops 2147483648 | bytes 4210692 | tf_op jit(solution)/shard_map/pallas_call | solution.py:225
  27.6 1.9 %collective-permute-start.2 = (bf16[512,512]{1,0:T(8,128)(2,1)S(1)}, bf16[512,512]{1,0:T(8,128)(2,1)S(1)}, u32[]{:S(2)}, u32[]{:S(2)}) collective-permute-start(bf16[512,512]{1,0:T(8,128)(2,1)S(1)} %shard_map.61), channel_id=1, source_target_pairs={{4,0},{8,4},{12,8},{16,12},{20,16},{24,20},{28,24},{32,28},{36,32}... | collective-permute-start | bytes 1572872 | tf_op jit(solution)/shard_map/ppermute | solution.py:285
  29.5 5.9 %collective-permute-start.5 = (bf16[512,512]{1,0:T(8,128)(2,1)S(1)}, bf16[512,512]{1,0:T(8,128)(2,1)S(1)}, u32[]{:S(2)}, u32[]{:S(2)}) collective-permute-start(bf16[512,512]{1,0:T(8,128)(2,1)S(1)} %shard_map.63), channel_id=1, source_target_pairs={{4,0},{8,4},{12,8},{16,12},{20,16},{24,20},{28,24},{32,28},{36,32}... | collective-permute-start | bytes 1572872 | tf_op jit(solution)/shard_map/ppermute | solution.py:285
  35.4 2.6 %shard_map.64 = bf16[512,512]{1,0:T(8,128)(2,1)S(1)} custom-call(s32[1]{0:T(128)S(6)} %copy.6.live_ref, s32[1,4096]{1,0:T(1,128)S(1)} %bitcast.9, bf16[512,3584]{1,0:T(8,128)(2,1)S(1)} %shard_map.55.inner_ref, bf16[512,512]{1,0:T(8,128)(2,1)S(1)} %shard_map.57.edge_ref), custom_call_target="tpu_custom_call" | custom-call | flops 2147483648 | bytes 4210692 | tf_op jit(solution)/shard_map/pallas_call | solution.py:225
  38.0 1.9 %collective-permute-start.6 = (bf16[512,512]{1,0:T(8,128)(2,1)S(1)}, bf16[512,512]{1,0:T(8,128)(2,1)S(1)}, u32[]{:S(2)}, u32[]{:S(2)}) collective-permute-start(bf16[512,512]{1,0:T(8,128)(2,1)S(1)} %shard_map.64), channel_id=1, source_target_pairs={{4,0},{8,4},{12,8},{16,12},{20,16},{24,20},{28,24},{32,28},{36,32}... | collective-permute-start | bytes 1572872 | tf_op jit(solution)/shard_map/ppermute | solution.py:285
  40.0 2.8 %shard_map.66 = bf16[512,512]{1,0:T(8,128)(2,1)S(1)} custom-call(s32[1]{0:T(128)S(6)} %copy.6.live_ref, s32[1,4096]{1,0:T(1,128)S(1)} %bitcast.10, bf16[512,3584]{1,0:T(8,128)(2,1)S(1)} %shard_map.55.inner_ref, bf16[512,512]{1,0:T(8,128)(2,1)S(1)} %shard_map.57.edge_ref), custom_call_target="tpu_custom_call" | custom-call | flops 2147483648 | bytes 4210692 | tf_op jit(solution)/shard_map/pallas_call | solution.py:225
  42.8 1.9 %collective-permute-start.9 = (bf16[512,512]{1,0:T(8,128)(2,1)S(1)}, bf16[512,512]{1,0:T(8,128)(2,1)S(1)}, u32[]{:S(2)}, u32[]{:S(2)}) collective-permute-start(bf16[512,512]{1,0:T(8,128)(2,1)S(1)} %shard_map.66), channel_id=1, source_target_pairs={{4,0},{8,4},{12,8},{16,12},{20,16},{24,20},{28,24},{32,28},{36,32}... | collective-permute-start | bytes 1572872 | tf_op jit(solution)/shard_map/ppermute | solution.py:285
  44.7 2.6 %shard_map.60.own_ref = f32[512,512]{1,0:T(8,128)S(1)} custom-call(s32[1]{0:T(128)S(6)} %copy.6.live_ref, s32[1,4096]{1,0:T(1,128)S(1)} %bitcast.11, bf16[512,3584]{1,0:T(8,128)(2,1)S(1)} %shard_map.55.inner_ref, bf16[512,512]{1,0:T(8,128)(2,1)S(1)} %shard_map.57.edge_ref), custom_call_target="tpu_custom_call" | custom-call | flops 2147483648 | bytes 4210692 | tf_op jit(solution)/shard_map/pallas_call | solution.py:225
  47.4 0.1 shard_map.62
  47.5 0.1 collective-permute-start.3
  47.5 3.2 %collective-permute-start.4 = (bf16[256,512]{1,0:T(8,128)(2,1)S(1)}, bf16[256,512]{1,0:T(8,128)(2,1)S(1)}, u32[]{:S(2)}, u32[]{:S(2)}) collective-permute-start(bf16[256,512]{1,0:T(8,128)(2,1)S(1)} %get-tuple-element.18), channel_id=1, source_target_pairs={{1,0},{2,1},{3,2},{0,3},{5,4},{6,5},{7,6},{4,7},{9,8},{10,9},{11,1... | collective-permute-start | bytes 786440 | tf_op jit(solution)/shard_map/ppermute | solution.py:293
  50.8 5.1 %shard_map.59 = (f32[512,512]{1,0:T(8,128)S(1)}, f32[512,512]{1,0:T(8,128)S(1)}) custom-call(s32[1]{0:T(128)S(6)} %copy.6.live_ref, s32[1,4096]{1,0:T(1,128)S(1)} %bitcast.12, bf16[512,3584]{1,0:T(8,128)(2,1)S(1)} %shard_map.55.inner_ref, bf16[512,512]{1,0:T(8,128)(2,1)S(1)} %shard_map.57.edge_ref), custom_call_target="tpu_custom_call" | custom-call | flops 4294967296 | bytes 4210692 | tf_op jit(solution)/shard_map/pallas_call | solution.py:225
  55.8 1.6 %collective-permute-done.3.low_half = bf16[256,512]{1,0:T(8,128)(2,1)S(1)} collective-permute-done((bf16[256,512]{1,0:T(8,128)(2,1)S(1)}, bf16[256,512]{1,0:T(8,128)(2,1)S(1)}, u32[]{:S(2)}, u32[]{:S(2)}) %collective-permute-start.3) | collective-permute-done | bytes 262176 | tf_op jit(solution)/shard_map/ppermute | solution.py:292
  57.4 0.2 shard_map.65
  57.8 3.2 %collective-permute-start.8 = (bf16[512,512]{1,0:T(8,128)(2,1)S(1)}, bf16[512,512]{1,0:T(8,128)(2,1)S(1)}, u32[]{:S(2)}, u32[]{:S(2)}) collective-permute-start(bf16[512,512]{1,0:T(8,128)(2,1)S(1)} %get-tuple-element.20), channel_id=1, source_target_pairs={{1,0},{2,1},{3,2},{0,3},{5,4},{6,5},{7,6},{4,7},{9,8},{10,9},{11,1... | collective-permute-start | bytes 1572872 | tf_op jit(solution)/shard_map/ppermute | solution.py:301
  61.0 2.6 %shard_map.58.own_ref = f32[512,512]{1,0:T(8,128)S(1)} custom-call(s32[1]{0:T(128)S(6)} %copy.6.live_ref, s32[1,4096]{1,0:T(1,128)S(1)} %bitcast.13, bf16[512,3584]{1,0:T(8,128)(2,1)S(1)} %shard_map.55.inner_ref, bf16[512,512]{1,0:T(8,128)(2,1)S(1)} %shard_map.57.edge_ref), custom_call_target="tpu_custom_call" | custom-call | flops 2147483648 | bytes 4210692 | tf_op jit(solution)/shard_map/pallas_call | solution.py:225
  63.6 8.8 %collective-permute-done.7.rest_0_ = bf16[512,512]{1,0:T(8,128)(2,1)S(1)} collective-permute-done((bf16[512,512]{1,0:T(8,128)(2,1)S(1)}, bf16[512,512]{1,0:T(8,128)(2,1)S(1)}, u32[]{:S(2)}, u32[]{:S(2)}) %collective-permute-start.7) | collective-permute-done | bytes 524320 | tf_op jit(solution)/shard_map/ppermute | solution.py:300
  72.4 1.4 %shard_map.67 = f32[512,512]{1,0:T(8,128)} custom-call(f32[512,512]{1,0:T(8,128)S(1)} %shard_map.58.own_ref, bf16[512,512]{1,0:T(8,128)(2,1)S(1)} %collective-permute-done.7.rest_0_, bf16[512,512]{1,0:T(8,128)(2,1)S(1)} %collective-permute-done.8.rest_1_, bf16[512,512]{1,0:T(8,128)(2,1)S(1)} %collective-permute-done.9.rest_2_), custom_call_target="tpu_custom_call" | custom-call | flops 1048576 | bytes 2621440 | tf_op jit(solution)/shard_map/pallas_call | solution.py:225
  (18 shorter events, 0.2 us)
Async XLA Ops:
  1.7 8.0 %copy-start = (bf16[4096,512]{1,0:T(8,128)(2,1)S(1)}, bf16[4096,512]{1,0:T(8,128)(2,1)}, u32[]{:S(2)}) copy-start(bf16[4096,512]{1,0:T(8,128)(2,1)} %spectra_ref.1) | copy-start | bytes 12582916
  1.7 8.0 %copy-start.1 = (s32[4096]{0:T(1024)S(1)}, s32[4096]{0:T(1024)}, u32[]{:S(2)}) copy-start(s32[4096]{0:T(1024)} %param.6) | copy-start | bytes 49156
  1.7 8.0 %copy-start.2 = (s32[4096]{0:T(1024)S(1)}, s32[4096]{0:T(1024)}, u32[]{:S(2)}) copy-start(s32[4096]{0:T(1024)} %param.7) | copy-start | bytes 49156
  1.8 18.7 %collective-permute-start = (bf16[272,512]{1,0:T(8,128)(2,1)S(1)}, bf16[272,512]{1,0:T(8,128)(2,1)S(1)}, u32[]{:S(2)}, u32[]{:S(2)}) collective-permute-start(bf16[272,512]{1,0:T(8,128)(2,1)S(1)} %get-tuple-element.13), channel_id=1, source_target_pairs={{0,1},{1,2},{2,3},{3,4},{4,5},{5,6},{6,7},{7,8},{8,9},{9,10},{10,1... | collective-permute-start | bytes 835592 | tf_op jit(solution)/shard_map/ppermute | solution.py:258
  5.6 14.9 %collective-permute-start.1 = (bf16[272,512]{1,0:T(8,128)(2,1)S(1)}, bf16[272,512]{1,0:T(8,128)(2,1)S(1)}, u32[]{:S(2)}, u32[]{:S(2)}) collective-permute-start(bf16[272,512]{1,0:T(8,128)(2,1)S(1)} %get-tuple-element.14), channel_id=1, source_target_pairs={{1,0},{2,1},{3,2},{4,3},{5,4},{6,5},{7,6},{8,7},{9,8},{10,9},{11,1... | collective-permute-start | bytes 835592 | tf_op jit(solution)/shard_map/ppermute | solution.py:259
  20.5 1.8 %copy-start.3 = (s32[4096]{0:T(1024)S(1)}, s32[4096]{0:T(1024)}, u32[]{:S(2)}) copy-start(s32[4096]{0:T(1024)} %param.9) | copy-start | bytes 49156
  27.6 19.8 %collective-permute-start.2 = (bf16[512,512]{1,0:T(8,128)(2,1)S(1)}, bf16[512,512]{1,0:T(8,128)(2,1)S(1)}, u32[]{:S(2)}, u32[]{:S(2)}) collective-permute-start(bf16[512,512]{1,0:T(8,128)(2,1)S(1)} %shard_map.61), channel_id=1, source_target_pairs={{4,0},{8,4},{12,8},{16,12},{20,16},{24,20},{28,24},{32,28},{36,32}... | collective-permute-start | bytes 1572872 | tf_op jit(solution)/shard_map/ppermute | solution.py:285
  29.5 26.3 %collective-permute-start.5 = (bf16[512,512]{1,0:T(8,128)(2,1)S(1)}, bf16[512,512]{1,0:T(8,128)(2,1)S(1)}, u32[]{:S(2)}, u32[]{:S(2)}) collective-permute-start(bf16[512,512]{1,0:T(8,128)(2,1)S(1)} %shard_map.63), channel_id=1, source_target_pairs={{4,0},{8,4},{12,8},{16,12},{20,16},{24,20},{28,24},{32,28},{36,32}... | collective-permute-start | bytes 1572872 | tf_op jit(solution)/shard_map/ppermute | solution.py:285
  38.0 17.8 %collective-permute-start.6 = (bf16[512,512]{1,0:T(8,128)(2,1)S(1)}, bf16[512,512]{1,0:T(8,128)(2,1)S(1)}, u32[]{:S(2)}, u32[]{:S(2)}) collective-permute-start(bf16[512,512]{1,0:T(8,128)(2,1)S(1)} %shard_map.64), channel_id=1, source_target_pairs={{4,0},{8,4},{12,8},{16,12},{20,16},{24,20},{28,24},{32,28},{36,32}... | collective-permute-start | bytes 1572872 | tf_op jit(solution)/shard_map/ppermute | solution.py:285
  42.8 20.9 %collective-permute-start.9 = (bf16[512,512]{1,0:T(8,128)(2,1)S(1)}, bf16[512,512]{1,0:T(8,128)(2,1)S(1)}, u32[]{:S(2)}, u32[]{:S(2)}) collective-permute-start(bf16[512,512]{1,0:T(8,128)(2,1)S(1)} %shard_map.66), channel_id=1, source_target_pairs={{4,0},{8,4},{12,8},{16,12},{20,16},{24,20},{28,24},{32,28},{36,32}... | collective-permute-start | bytes 1572872 | tf_op jit(solution)/shard_map/ppermute | solution.py:285
  47.5 10.0 %collective-permute-start.3 = (bf16[256,512]{1,0:T(8,128)(2,1)S(1)}, bf16[256,512]{1,0:T(8,128)(2,1)S(1)}, u32[]{:S(2)}, u32[]{:S(2)}) collective-permute-start(bf16[256,512]{1,0:T(8,128)(2,1)S(1)} %get-tuple-element.17), channel_id=1, source_target_pairs={{0,1},{1,2},{2,3},{3,0},{4,5},{5,6},{6,7},{7,4},{8,9},{9,10},{10,1... | collective-permute-start | bytes 786440 | tf_op jit(solution)/shard_map/ppermute | solution.py:292
  47.5 9.9 %collective-permute-start.4 = (bf16[256,512]{1,0:T(8,128)(2,1)S(1)}, bf16[256,512]{1,0:T(8,128)(2,1)S(1)}, u32[]{:S(2)}, u32[]{:S(2)}) collective-permute-start(bf16[256,512]{1,0:T(8,128)(2,1)S(1)} %get-tuple-element.18), channel_id=1, source_target_pairs={{1,0},{2,1},{3,2},{0,3},{5,4},{6,5},{7,6},{4,7},{9,8},{10,9},{11,1... | collective-permute-start | bytes 786440 | tf_op jit(solution)/shard_map/ppermute | solution.py:293
  57.7 14.8 %collective-permute-start.7 = (bf16[512,512]{1,0:T(8,128)(2,1)S(1)}, bf16[512,512]{1,0:T(8,128)(2,1)S(1)}, u32[]{:S(2)}, u32[]{:S(2)}) collective-permute-start(bf16[512,512]{1,0:T(8,128)(2,1)S(1)} %get-tuple-element.19), channel_id=1, source_target_pairs={{0,1},{1,2},{2,3},{3,0},{4,5},{5,6},{6,7},{7,4},{8,9},{9,10},{10,1... | collective-permute-start | bytes 1572872 | tf_op jit(solution)/shard_map/ppermute | solution.py:300
  57.8 14.7 %collective-permute-start.8 = (bf16[512,512]{1,0:T(8,128)(2,1)S(1)}, bf16[512,512]{1,0:T(8,128)(2,1)S(1)}, u32[]{:S(2)}, u32[]{:S(2)}) collective-permute-start(bf16[512,512]{1,0:T(8,128)(2,1)S(1)} %get-tuple-element.20), channel_id=1, source_target_pairs={{1,0},{2,1},{3,2},{0,3},{5,4},{6,5},{7,6},{4,7},{9,8},{10,9},{11,1... | collective-permute-start | bytes 1572872 | tf_op jit(solution)/shard_map/ppermute | solution.py:301

commit v4 on v3

--- a/solution.py
+++ b/solution.py
@@ -148,36 +148,50 @@
 
 
 INNER = ROWS - 2 * BLOCK
-CHUNK = INNER // 4
-
-
-def added(first, live, ids_ref, rows, start):
-    width = rows.shape[1]
-    slot = lax.broadcasted_iota(i32, (1, width), 1) + start
-    wanted = jnp.where(slot < live, ids_ref[:, start : start + width] - first, FAR)
-    hot = lax.broadcasted_iota(i32, (CL_DEV, width), 0) == wanted
-    hot = jnp.where(hot, 1.0, 0.0).astype(bf16)
-    return lax.dot_general(hot, rows, NT, preferred_element_type=f32)
-
-
-def sums_kernel(turns, away, rep_count, live_ref, ids_ref, inner_ref, edge_ref, *outs):
+CHUNK = 512
+
+
+def partners(rep, parity, rep_count):
+    across = rep_count - 1 - rep
+    beside = rep + 1 - 2 * (rep & 1)
+    if isinstance(rep, int):
+        return (beside, across) if parity else (across, beside)
+    odd = parity == 1
+    return jnp.where(odd, beside, across), jnp.where(odd, across, beside)
+
+
+def sums_kernel(first_step, away, rep_count, live_ref, ids_ref, inner_ref, edge_ref, out_ref):
     rep = lax.axis_index("rep")
     band = lax.axis_index("mz")
-    per_range = CL_DEV * rep_count
     if away:
         band = band + jnp.where(rep == 0, -1, 1)
+    one, two = partners(rep, band & 1, rep_count)
+    owners = (partners(one, band & 1, rep_count)[1], one) if first_step else (two, rep)
+    firsts = [band * (CL_DEV * rep_count) + owner * CL_DEV for owner in owners]
 
     def work():
         live = live_ref[0]
-        for turn, out_ref in zip(turns, outs):
-            owner = lax.rem(rep + turn, rep_count)
-            first = band * per_range + owner * CL_DEV
-
-            acc = added(first, live, ids_ref, edge_ref[:, :BLOCK], 0)
-            acc = acc + added(first, live, ids_ref, edge_ref[:, BLOCK:], ROWS - BLOCK)
-            for start in range(0, INNER, CHUNK):
-                acc = acc + added(first, live, ids_ref, inner_ref[:, start : start + CHUNK], start + BLOCK)
-            out_ref[...] = acc.astype(out_ref.dtype)
+        lane = lax.broadcasted_iota(i32, (1, BLOCK), 1)
+
+        def added(pieces, rows):
+            wanted = jnp.concatenate(
+                [
+                    jnp.where(lane + start < live, ids_ref[:, start : start + BLOCK], FAR)
+                    for start in pieces
+                ],
+                axis=1,
+            )
+            cluster = lax.broadcasted_iota(i32, (CL_DEV, CHUNK), 0)
+            hot = jnp.concatenate(
+                [jnp.where(cluster == wanted - first, 1.0, 0.0).astype(bf16) for first in firsts], axis=0
+            )
+            return lax.dot_general(hot, rows, NT, preferred_element_type=f32)
+
+        acc = added((0, ROWS - BLOCK), edge_ref[...])
+        for start in range(0, INNER, CHUNK):
+            pieces = range(start + BLOCK, start + BLOCK + CHUNK, BLOCK)
+            acc = acc + added(pieces, inner_ref[:, start : start + CHUNK])
+        out_ref[...] = acc.astype(out_ref.dtype)
 
     if away:
         pl.when((rep == 0) | (rep == rep_count - 1))(work)
@@ -185,27 +199,18 @@
         work()
 
 
-def far_kernel(own_ref, moved_ref, low_ref, high_ref):
-    total = (own_ref[...] + moved_ref[...].astype(f32)).astype(bf16)
-    low_ref[...] = total[: CL_DEV // 2]
-    high_ref[...] = total[CL_DEV // 2 :]
-
-
-def join_kernel(own_up, own_down, low_half, high_half, moved_1, moved_3, next_up, next_down):
-    half = CL_DEV // 2
-    above = own_up[...] + moved_1[...].astype(f32)
-    below = own_down[...] + moved_3[...].astype(f32)
-    next_up[:half, :] = (above[:half] + low_half[...].astype(f32)).astype(bf16)
-    next_up[half:, :] = above[half:].astype(bf16)
-    next_down[:half, :] = below[:half].astype(bf16)
-    next_down[half:, :] = (below[half:] + high_half[...].astype(f32)).astype(bf16)
-
-
-def finish_kernel(own_ref, *rest):
-    out_ref = rest[-1]
-    owned = own_ref[...]
-    for ref in rest[:-1]:
-        owned = owned + ref[...].astype(f32)
+def far_kernel(own_ref, moved_ref, out_ref):
+    out_ref[...] = (own_ref[...] + moved_ref[...].astype(f32)).astype(bf16)
+
+
+def join_kernel(own_ref, moved_ref, got_ref, next_ref, mine_ref):
+    for half, ref in ((slice(0, CL_DEV), next_ref), (slice(CL_DEV, 2 * CL_DEV), mine_ref)):
+        total = own_ref[half, :] + moved_ref[half, :].astype(f32) + got_ref[half, :].astype(f32)
+        ref[...] = total.astype(ref.dtype)
+
+
+def finish_kernel(mine_ref, got_ref, out_ref):
+    owned = mine_ref[...] + got_ref[...].astype(f32)
     mean = jnp.sum(owned * owned, axis=1, keepdims=True) * (1.0 / DIM)
     out_ref[...] = owned / jnp.sqrt(mean + 1e-06)
 
@@ -242,12 +247,10 @@
     every = bands * reps
     both = ("mz", "rep")
 
-    def sum_blocks(turns, away, dtype):
-        outs = [shape(CL_DEV, DIM, dtype)] * len(turns)
+    def sum_pair(first_step, away, dtype):
         return call(
-            functools.partial(sums_kernel, turns, away, reps),
-            [live, ids, inner, edge], outs,
-            2 * CL_DEV * ROWS * DIM * len(turns),
+            functools.partial(sums_kernel, first_step, away, reps),
+            [live, ids, inner, edge], shape(2 * CL_DEV, DIM, dtype), 4 * CL_DEV * ROWS * DIM, limit=20,
         )
 
     back, ahead, ids = (x.reshape(1, ROWS) for x in (reach_back, reach_ahead, cluster_ids))
@@ -275,33 +278,22 @@
     last = reps - 1
     away_pairs = [(d * reps, (d - 1) * reps) for d in range(1, bands)]
     away_pairs += [(d * reps + last, (d + 1) * reps + last) for d in range(bands - 1)]
-    up = [(i, (i + 1) % reps) for i in range(reps)]
-    down = [(b, a) for a, b in up]
-    arrived = {}
-    own = {}
-
-    def send_away(turn):
-        (block,) = sum_blocks((turn,), True, bf16)
-        arrived[turn] = lax.ppermute(block, both, away_pairs)
-
-    send_away(2)
-    (own[2],) = sum_blocks((2,), False, f32)
-    send_away(1)
-    half = shape(CL_DEV // 2, DIM, bf16)
-    low_half, high_half = call(far_kernel, [own[2], arrived[2]], [half] * 2, 1 << 20)
-    low_half = lax.ppermute(low_half, "rep", up)
-    high_half = lax.ppermute(high_half, "rep", down)
-    send_away(3)
-    own[1], own[3] = sum_blocks((1, 3), False, f32)
-    next_up, next_down = call(
-        join_kernel, [own[1], own[3], low_half, high_half, arrived[1], arrived[3]],
-        [shape(CL_DEV, DIM, bf16)] * 2, 1 << 20,
-    )
-    got_up = lax.ppermute(next_up, "rep", up)
-    got_down = lax.ppermute(next_down, "rep", down)
-    send_away(0)
-    (own[0],) = sum_blocks((0,), False, f32)
-    return call(finish_kernel, [own[0], got_up, got_down, arrived[0]], shape(CL_DEV, DIM, f32), 1 << 20)
+    swaps = [
+        [(d * reps + r, d * reps + partners(r, d & 1, reps)[step]) for d in range(bands) for r in range(reps)]
+        for step in range(2)
+    ]
+    x_far = lax.ppermute(sum_pair(True, True, bf16), both, away_pairs)
+    x_near = lax.ppermute(sum_pair(False, True, bf16), both, away_pairs)
+    own_far = sum_pair(True, False, f32)
+    far = call(far_kernel, [own_far, x_far], shape(2 * CL_DEV, DIM, bf16), 1 << 20)
+    got_first = lax.ppermute(far, both, swaps[0])
+    own_near = sum_pair(False, False, f32)
+    after_first, mine = call(
+        join_kernel, [own_near, x_near, got_first],
+        [shape(CL_DEV, DIM, bf16), shape(CL_DEV, DIM, f32)], 1 << 20,
+    )
+    got_second = lax.ppermute(after_first, both, swaps[1])
+    return call(finish_kernel, [mine, got_second], shape(CL_DEV, DIM, f32), 1 << 20)
 
 
 def solution(mesh):

time: 74.1 us -> 73.6 us (level)
  the two profiles are of different devices: /device:TPU:130 before, /device:TPU:103 now
where the time goes in v4:
time: 73.6 us; the launch traced here: 73.5 us
  Pallas kernels  32.3 us (44%)
  waiting for transfers between devices  26.5 us (36%)
  starting transfers between devices  12.8 us (17%)
  local copies, waits for them, and re-layouts  1.09 us (1%)
  between operations  0.84 us (1%)
    pallas_call x10, Pallas kernels, call(): pl.pallas_call(kernel, out_shape=out_shape, in_specs=in_specs, out_specs=...  32.3 us
    ppermute x1, waiting for transfers between devices, shards(): got_second = lax.ppermute(after_first, both, swaps[1])  9.23 us
    ppermute x1, waiting for transfers between devices, shards(): x_far = lax.ppermute(sum_pair(True, True, bf16), both, away_pairs)  7.28 us
    ppermute x1, waiting for transfers between devices, shards(): x_near = lax.ppermute(sum_pair(False, True, bf16), both, away_pairs)  6.44 us
    ppermute x1, starting transfers between devices, shards(): lax.ppermute(low_rows, both, [(i + 1, i) for i in range(every - 1)])  3.92 us
    ppermute x1, waiting for transfers between devices, shards(): got_first = lax.ppermute(far, both, swaps[0])  3.49 us
    ppermute x1, starting transfers between devices, shards(): lax.ppermute(high_rows, both, [(i, i + 1) for i in range(every - 1)])  3.47 us
    ppermute x1, starting transfers between devices, shards(): x_far = lax.ppermute(sum_pair(True, True, bf16), both, away_pairs)  3.13 us
  transfers between devices with their start and end apart: 6, of which 4 were waited for; matrix products, arithmetic and copies ran while one was open for 0% of the time, Pallas kernels for 33%

profile of v4, /device:TPU:103, one launch (start us, length us, event | category | flops | bytes accessed | tf_op | source)
XLA Modules:
  0.0 73.5 jit_solution(5741186795901003315)
XLA Ops:
  0.7 1.1 %fusion = (bf16[256,512]{1,0:T(8,128)(2,1)S(1)}, bf16[256,512]{1,0:T(8,128)(2,1)S(1)}) fusion(bf16[4096,512]{1,0:T(8,128)(2,1)} %spectra_ref.1), kind=kLoop, calls=%fused_computation | loop fusion | bytes 1048576 | tf_op jit(solution)/shard_map/slice | solution.py:258
  1.7 0.0 copy-start
  1.7 0.0 copy-start.1
  1.7 0.0 copy-start.2
  1.8 3.5 %collective-permute-start = (bf16[272,512]{1,0:T(8,128)(2,1)S(1)}, bf16[272,512]{1,0:T(8,128)(2,1)S(1)}, u32[]{:S(2)}, u32[]{:S(2)}) collective-permute-start(bf16[272,512]{1,0:T(8,128)(2,1)S(1)} %get-tuple-element.9), channel_id=1, source_target_pairs={{0,1},{1,2},{2,3},{3,4},{4,5},{5,6},{6,7},{7,8},{8,9},{9,10},{10,1... | collective-permute-start | bytes 835592 | tf_op jit(solution)/shard_map/ppermute | solution.py:261
  5.3 3.9 %collective-permute-start.1 = (bf16[272,512]{1,0:T(8,128)(2,1)S(1)}, bf16[272,512]{1,0:T(8,128)(2,1)S(1)}, u32[]{:S(2)}, u32[]{:S(2)}) collective-permute-start(bf16[272,512]{1,0:T(8,128)(2,1)S(1)} %get-tuple-element.10), channel_id=1, source_target_pairs={{1,0},{2,1},{3,2},{4,3},{5,4},{6,5},{7,6},{8,7},{9,8},{10,9},{11,1... | collective-permute-start | bytes 835592 | tf_op jit(solution)/shard_map/ppermute | solution.py:262
  9.2 10.7 %shard_map.55.inner_ref = bf16[512,3584]{1,0:T(8,128)(2,1)S(1)} custom-call(s32[1]{0:T(128)S(6)} %copy.6.live_ref, s32[1,4096]{1,0:T(1,128)S(1)} %bitcast.3, s32[1,4096]{1,0:T(1,128)S(1)} %bitcast.5, bf16[4096,512]{1,0:T(8,128)(2,1)S(1)} %copy-done), custom_call_target="tpu_custom_call" | custom-call | flops 5637144576 | bytes 4227076 | tf_op jit(solution)/shard_map/pallas_call | solution.py:230
  19.9 0.0 copy-start.3
  20.0 1.8 %shard_map.57.edge_ref = bf16[512,512]{1,0:T(8,128)(2,1)S(1)} custom-call(s32[1]{0:T(128)S(6)} %copy.6.live_ref, s32[1,4096]{1,0:T(1,128)S(1)} %bitcast.4, s32[1,4096]{1,0:T(1,128)S(1)} %bitcast.6, bf16[4096,512]{1,0:T(8,128)(2,1)S(1)} %copy-done, bf16[272,512]{1,0:T(8,128)(2,1)S(1)} %collective-permute-done.below_ref, ...), custom_call_target="tpu_custom_call" | custom-call | flops 805306368 | bytes 4784132 | tf_op jit(solution)/shard_map/pallas_call | solution.py:230
  21.8 4.5 %shard_map.61 = bf16[1024,512]{1,0:T(8,128)(2,1)S(1)} custom-call(s32[1]{0:T(128)S(6)} %copy.6.live_ref, s32[1,4096]{1,0:T(1,128)S(1)} %bitcast.7, bf16[512,3584]{1,0:T(8,128)(2,1)S(1)} %shard_map.55.inner_ref, bf16[512,512]{1,0:T(8,128)(2,1)S(1)} %shard_map.57.edge_ref), custom_call_target="tpu_custom_call" | custom-call | flops 4294967296 | bytes 4210692 | tf_op jit(solution)/shard_map/pallas_call | solution.py:230
  26.3 3.1 %collective-permute-start.3 = (bf16[1024,512]{1,0:T(8,128)(2,1)S(1)}, bf16[1024,512]{1,0:T(8,128)(2,1)S(1)}, u32[]{:S(2)}, u32[]{:S(2)}) collective-permute-start(bf16[1024,512]{1,0:T(8,128)(2,1)S(1)} %shard_map.61), channel_id=1, source_target_pairs={{4,0},{8,4},{12,8},{16,12},{20,16},{24,20},{28,24},{32,28},{36,32}... | collective-permute-start | bytes 3145736 | tf_op jit(solution)/shard_map/ppermute | solution.py:285
  29.4 4.5 %shard_map.59 = bf16[1024,512]{1,0:T(8,128)(2,1)S(1)} custom-call(s32[1]{0:T(128)S(6)} %copy.6.live_ref, s32[1,4096]{1,0:T(1,128)S(1)} %bitcast.8, bf16[512,3584]{1,0:T(8,128)(2,1)S(1)} %shard_map.55.inner_ref, bf16[512,512]{1,0:T(8,128)(2,1)S(1)} %shard_map.57.edge_ref), custom_call_target="tpu_custom_call" | custom-call | flops 4294967296 | bytes 4210692 | tf_op jit(solution)/shard_map/pallas_call | solution.py:230
  34.0 2.1 %collective-permute-start.2 = (bf16[1024,512]{1,0:T(8,128)(2,1)S(1)}, bf16[1024,512]{1,0:T(8,128)(2,1)S(1)}, u32[]{:S(2)}, u32[]{:S(2)}) collective-permute-start(bf16[1024,512]{1,0:T(8,128)(2,1)S(1)} %shard_map.59), channel_id=1, source_target_pairs={{4,0},{8,4},{12,8},{16,12},{20,16},{24,20},{28,24},{32,28},{36,32}... | collective-permute-start | bytes 3145736 | tf_op jit(solution)/shard_map/ppermute | solution.py:286
  36.1 4.5 %shard_map.60.own_ref = f32[1024,512]{1,0:T(8,128)S(1)} custom-call(s32[1]{0:T(128)S(6)} %copy.6.live_ref, s32[1,4096]{1,0:T(1,128)S(1)} %bitcast.9, bf16[512,3584]{1,0:T(8,128)(2,1)S(1)} %shard_map.55.inner_ref, bf16[512,512]{1,0:T(8,128)(2,1)S(1)} %shard_map.57.edge_ref), custom_call_target="tpu_custom_call" | custom-call | flops 4294967296 | bytes 4210692 | tf_op jit(solution)/shard_map/pallas_call | solution.py:230
  40.6 7.3 %collective-permute-done.3.moved_ref = bf16[1024,512]{1,0:T(8,128)(2,1)S(1)} collective-permute-done((bf16[1024,512]{1,0:T(8,128)(2,1)S(1)}, bf16[1024,512]{1,0:T(8,128)(2,1)S(1)}, u32[]{:S(2)}, u32[]{:S(2)}) %collective-permute-start.3) | collective-permute-done | bytes 1048608 | tf_op jit(solution)/shard_map/ppermute | solution.py:285
  47.9 0.2 shard_map.62
  48.1 0.1 collective-permute-start.4
  48.2 4.5 %shard_map.58.own_ref = f32[1024,512]{1,0:T(8,128)S(1)} custom-call(s32[1]{0:T(128)S(6)} %copy.6.live_ref, s32[1,4096]{1,0:T(1,128)S(1)} %bitcast.10, bf16[512,3584]{1,0:T(8,128)(2,1)S(1)} %shard_map.55.inner_ref, bf16[512,512]{1,0:T(8,128)(2,1)S(1)} %shard_map.57.edge_ref), custom_call_target="tpu_custom_call" | custom-call | flops 4294967296 | bytes 4210692 | tf_op jit(solution)/shard_map/pallas_call | solution.py:230
  52.7 6.4 %collective-permute-done.2.moved_ref = bf16[1024,512]{1,0:T(8,128)(2,1)S(1)} collective-permute-done((bf16[1024,512]{1,0:T(8,128)(2,1)S(1)}, bf16[1024,512]{1,0:T(8,128)(2,1)S(1)}, u32[]{:S(2)}, u32[]{:S(2)}) %collective-permute-start.2) | collective-permute-done | bytes 1048608 | tf_op jit(solution)/shard_map/ppermute | solution.py:286
  59.1 3.5 %collective-permute-done.4.got_ref = bf16[1024,512]{1,0:T(8,128)(2,1)S(1)} collective-permute-done((bf16[1024,512]{1,0:T(8,128)(2,1)S(1)}, bf16[1024,512]{1,0:T(8,128)(2,1)S(1)}, u32[]{:S(2)}, u32[]{:S(2)}) %collective-permute-start.4) | collective-permute-done | bytes 1048608 | tf_op jit(solution)/shard_map/ppermute | solution.py:289
  62.6 0.3 shard_map.63
  62.9 0.1 collective-permute-start.5
  63.0 9.2 %collective-permute-done.5.got_ref = bf16[512,512]{1,0:T(8,128)(2,1)S(1)} collective-permute-done((bf16[512,512]{1,0:T(8,128)(2,1)S(1)}, bf16[512,512]{1,0:T(8,128)(2,1)S(1)}, u32[]{:S(2)}, u32[]{:S(2)}) %collective-permute-start.5) | collective-permute-done | bytes 524320 | tf_op jit(solution)/shard_map/ppermute | solution.py:295
  72.2 1.2 %shard_map.64 = f32[512,512]{1,0:T(8,128)} custom-call(f32[512,512]{1,0:T(8,128)S(1)} %get-tuple-element.11.mine_ref, bf16[512,512]{1,0:T(8,128)(2,1)S(1)} %collective-permute-done.5.got_ref), custom_call_target="tpu_custom_call" | custom-call | flops 1048576 | bytes 1572864 | tf_op jit(solution)/shard_map/pallas_call | solution.py:230
  (7 shorter events, 0.1 us)
Async XLA Ops:
  1.7 7.5 %copy-start = (bf16[4096,512]{1,0:T(8,128)(2,1)S(1)}, bf16[4096,512]{1,0:T(8,128)(2,1)}, u32[]{:S(2)}) copy-start(bf16[4096,512]{1,0:T(8,128)(2,1)} %spectra_ref.1) | copy-start | bytes 12582916
  1.7 7.5 %copy-start.1 = (s32[4096]{0:T(1024)S(1)}, s32[4096]{0:T(1024)}, u32[]{:S(2)}) copy-start(s32[4096]{0:T(1024)} %param.6) | copy-start | bytes 49156
  1.7 7.5 %copy-start.2 = (s32[4096]{0:T(1024)S(1)}, s32[4096]{0:T(1024)}, u32[]{:S(2)}) copy-start(s32[4096]{0:T(1024)} %param.7) | copy-start | bytes 49156
  1.8 18.1 %collective-permute-start = (bf16[272,512]{1,0:T(8,128)(2,1)S(1)}, bf16[272,512]{1,0:T(8,128)(2,1)S(1)}, u32[]{:S(2)}, u32[]{:S(2)}) collective-permute-start(bf16[272,512]{1,0:T(8,128)(2,1)S(1)} %get-tuple-element.9), channel_id=1, source_target_pairs={{0,1},{1,2},{2,3},{3,4},{4,5},{5,6},{6,7},{7,8},{8,9},{9,10},{10,1... | collective-permute-start | bytes 835592 | tf_op jit(solution)/shard_map/ppermute | solution.py:261
  5.3 14.7 %collective-permute-start.1 = (bf16[272,512]{1,0:T(8,128)(2,1)S(1)}, bf16[272,512]{1,0:T(8,128)(2,1)S(1)}, u32[]{:S(2)}, u32[]{:S(2)}) collective-permute-start(bf16[272,512]{1,0:T(8,128)(2,1)S(1)} %get-tuple-element.10), channel_id=1, source_target_pairs={{1,0},{2,1},{3,2},{4,3},{5,4},{6,5},{7,6},{8,7},{9,8},{10,9},{11,1... | collective-permute-start | bytes 835592 | tf_op jit(solution)/shard_map/ppermute | solution.py:262
  19.9 1.8 %copy-start.3 = (s32[4096]{0:T(1024)S(1)}, s32[4096]{0:T(1024)}, u32[]{:S(2)}) copy-start(s32[4096]{0:T(1024)} %param.9) | copy-start | bytes 49156
  26.3 21.6 %collective-permute-start.3 = (bf16[1024,512]{1,0:T(8,128)(2,1)S(1)}, bf16[1024,512]{1,0:T(8,128)(2,1)S(1)}, u32[]{:S(2)}, u32[]{:S(2)}) collective-permute-start(bf16[1024,512]{1,0:T(8,128)(2,1)S(1)} %shard_map.61), channel_id=1, source_target_pairs={{4,0},{8,4},{12,8},{16,12},{20,16},{24,20},{28,24},{32,28},{36,32}... | collective-permute-start | bytes 3145736 | tf_op jit(solution)/shard_map/ppermute | solution.py:285
  34.0 25.1 %collective-permute-start.2 = (bf16[1024,512]{1,0:T(8,128)(2,1)S(1)}, bf16[1024,512]{1,0:T(8,128)(2,1)S(1)}, u32[]{:S(2)}, u32[]{:S(2)}) collective-permute-start(bf16[1024,512]{1,0:T(8,128)(2,1)S(1)} %shard_map.59), channel_id=1, source_target_pairs={{4,0},{8,4},{12,8},{16,12},{20,16},{24,20},{28,24},{32,28},{36,32}... | collective-permute-start | bytes 3145736 | tf_op jit(solution)/shard_map/ppermute | solution.py:286
  48.1 14.5 %collective-permute-start.4 = (bf16[1024,512]{1,0:T(8,128)(2,1)S(1)}, bf16[1024,512]{1,0:T(8,128)(2,1)S(1)}, u32[]{:S(2)}, u32[]{:S(2)}) collective-permute-start(bf16[1024,512]{1,0:T(8,128)(2,1)S(1)} %shard_map.62), channel_id=1, source_target_pairs={{0,3},{1,2},{2,1},{3,0},{4,5},{5,4},{6,7},{7,6},{8,11},{9,10},{10,... | collective-permute-start | bytes 3145736 | tf_op jit(solution)/shard_map/ppermute | solution.py:289
  62.9 9.3 %collective-permute-start.5 = (bf16[512,512]{1,0:T(8,128)(2,1)S(1)}, bf16[512,512]{1,0:T(8,128)(2,1)S(1)}, u32[]{:S(2)}, u32[]{:S(2)}) collective-permute-start(bf16[512,512]{1,0:T(8,128)(2,1)S(1)} %get-tuple-element.12), channel_id=1, source_target_pairs={{0,1},{1,0},{2,3},{3,2},{4,7},{5,6},{6,5},{7,4},{8,9},{9,8},{10,11... | collective-permute-start | bytes 1572872 | tf_op jit(solution)/shard_map/ppermute | solution.py:295

commit v5 on v4

--- a/solution.py
+++ b/solution.py
@@ -58,13 +58,19 @@
     return (mixed * (1.0 / total)).astype(bf16)
 
 
-def pack_kernel(live_ref, first_ref, last_ref, low_ref, high_ref):
+def pack_kernel(live_ref, first_ref, last_ref, one_ref, two_ref):
     live = live_ref[0]
     row = lax.broadcasted_iota(i32, (HALO - BLOCK, DIM), 0)
     digits = jnp.where(row == 0, live >> 6, live & 63).astype(f32).astype(bf16)
-    for source, ref in ((first_ref, low_ref), (last_ref, high_ref)):
-        ref[:BLOCK, :] = source[...]
-        ref[BLOCK:, :] = digits
+    one_ref[BLOCK:, :] = digits
+    two_ref[BLOCK:, :] = digits
+    even = lax.axis_index("rep") % 2 == 0
+    for is_even, one, two in ((True, last_ref, first_ref), (False, first_ref, last_ref)):
+
+        @pl.when(even == is_even)
+        def _():
+            one_ref[:BLOCK, :] = one[...]
+            two_ref[:BLOCK, :] = two[...]
 
 
 def interior_kernel(
@@ -124,26 +130,30 @@
     lax.fori_loop(0, (NBLK - 2) // 2, step, 0)
 
 
-def edges_kernel(live_ref, back_ref, ahead_ref, spectra_ref, below_ref, above_ref, out_ref):
+def edges_kernel(live_ref, back_ref, ahead_ref, spectra_ref, one_ref, two_ref, out_ref):
     live = live_ref[0]
-
-    def count(ref):
-        digits = ref[BLOCK : BLOCK + 8, :BLOCK].astype(f32)
+    even = lax.axis_index("rep") % 2 == 0
+    one, two = one_ref[...].astype(f32), two_ref[...].astype(f32)
+    below = jnp.where(even, two, one)
+    above = jnp.where(even, one, two)
+
+    def count(rows):
+        digits = rows[BLOCK : BLOCK + 8, :BLOCK]
         return (digits[0:1] * 64.0 + digits[1:2]).astype(i32)
 
     def unit(block):
         return unit_rows(spectra_ref[block * BLOCK : (block + 1) * BLOCK, :])
 
-    keys = [unit_rows(below_ref[:BLOCK, :]), unit(0), unit(1)]
+    keys = [unit_rows(below[:BLOCK]), unit(0), unit(1)]
     out_ref[:, :BLOCK] = attend(
         keys[1], back_ref[:, :BLOCK], ahead_ref[:, :BLOCK], live + BLOCK, keys,
-        [transposed(k) for k in keys], count(below_ref) - (ROWS - BLOCK), None,
-    )
-    keys = [unit(NBLK - 2), unit(NBLK - 1), unit_rows(above_ref[:BLOCK, :])]
+        [transposed(k) for k in keys], count(below) - (ROWS - BLOCK), None,
+    )
+    keys = [unit(NBLK - 2), unit(NBLK - 1), unit_rows(above[:BLOCK])]
     out_ref[:, BLOCK:] = attend(
         keys[1], back_ref[:, ROWS - BLOCK :], ahead_ref[:, ROWS - BLOCK :],
         live - (ROWS - 2 * BLOCK), keys, [transposed(k) for k in keys],
-        None, count(above_ref) + 2 * BLOCK,
+        None, count(above) + 2 * BLOCK,
     )
 
 
@@ -160,14 +170,14 @@
     return jnp.where(odd, beside, across), jnp.where(odd, across, beside)
 
 
-def sums_kernel(first_step, away, rep_count, live_ref, ids_ref, inner_ref, edge_ref, out_ref):
+def sums_kernel(role, away, rep_count, live_ref, ids_ref, inner_ref, edge_ref, out_ref):
     rep = lax.axis_index("rep")
     band = lax.axis_index("mz")
     if away:
         band = band + jnp.where(rep == 0, -1, 1)
     one, two = partners(rep, band & 1, rep_count)
-    owners = (partners(one, band & 1, rep_count)[1], one) if first_step else (two, rep)
-    firsts = [band * (CL_DEV * rep_count) + owner * CL_DEV for owner in owners]
+    owner = (rep, one, two, partners(one, band & 1, rep_count)[1])[role]
+    first = band * (CL_DEV * rep_count) + owner * CL_DEV
 
     def work():
         live = live_ref[0]
@@ -182,9 +192,7 @@
                 axis=1,
             )
             cluster = lax.broadcasted_iota(i32, (CL_DEV, CHUNK), 0)
-            hot = jnp.concatenate(
-                [jnp.where(cluster == wanted - first, 1.0, 0.0).astype(bf16) for first in firsts], axis=0
-            )
+            hot = jnp.where(cluster == wanted - first, 1.0, 0.0).astype(bf16)
             return lax.dot_general(hot, rows, NT, preferred_element_type=f32)
 
         acc = added((0, ROWS - BLOCK), edge_ref[...])
@@ -199,18 +207,18 @@
         work()
 
 
-def far_kernel(own_ref, moved_ref, out_ref):
-    out_ref[...] = (own_ref[...] + moved_ref[...].astype(f32)).astype(bf16)
-
-
-def join_kernel(own_ref, moved_ref, got_ref, next_ref, mine_ref):
-    for half, ref in ((slice(0, CL_DEV), next_ref), (slice(CL_DEV, 2 * CL_DEV), mine_ref)):
-        total = own_ref[half, :] + moved_ref[half, :].astype(f32) + got_ref[half, :].astype(f32)
-        ref[...] = total.astype(ref.dtype)
-
-
-def finish_kernel(mine_ref, got_ref, out_ref):
-    owned = mine_ref[...] + got_ref[...].astype(f32)
+def add_kernel(own_ref, *rest):
+    total = own_ref[...]
+    for ref in rest[:-1]:
+        total = total + ref[...].astype(f32)
+    rest[-1][...] = total.astype(bf16)
+
+
+def finish_kernel(own_ref, *rest):
+    out_ref = rest[-1]
+    owned = own_ref[...]
+    for ref in rest[:-1]:
+        owned = owned + ref[...].astype(f32)
     mean = jnp.sum(owned * owned, axis=1, keepdims=True) * (1.0 / DIM)
     out_ref[...] = owned / jnp.sqrt(mean + 1e-06)
 
@@ -247,19 +255,22 @@
     every = bands * reps
     both = ("mz", "rep")
 
-    def sum_pair(first_step, away, dtype):
+    def sum_block(role, away):
         return call(
-            functools.partial(sums_kernel, first_step, away, reps),
-            [live, ids, inner, edge], shape(2 * CL_DEV, DIM, dtype), 4 * CL_DEV * ROWS * DIM, limit=20,
+            functools.partial(sums_kernel, role, away, reps), [live, ids, inner, edge],
+            shape(CL_DEV, DIM, bf16 if away else f32), 2 * CL_DEV * ROWS * DIM,
         )
 
     back, ahead, ids = (x.reshape(1, ROWS) for x in (reach_back, reach_ahead, cluster_ids))
-    low_rows, high_rows = call(
+    blocks = call(
         pack_kernel, [live, spectra[:BLOCK], spectra[ROWS - BLOCK :]],
         [shape(HALO, DIM, bf16)] * 2, 1 << 33, limit=2,
     )
-    from_below = lax.ppermute(high_rows, both, [(i, i + 1) for i in range(every - 1)])
-    from_above = lax.ppermute(low_rows, both, [(i + 1, i) for i in range(every - 1)])
+    pairs = [(i, i + 1) for i in range(every - 1)]
+    halos = [
+        lax.ppermute(block, both, sorted(pair[::way] for pair in pairs[turn::2] for way in (1, -1)))
+        for turn, block in enumerate(blocks)
+    ]
     per_block = 4 * BLOCK * 3 * BLOCK * DIM
     inner = call(
         interior_kernel, [live, back, ahead, spectra], shape(DIM, INNER, bf16), per_block * (NBLK - 2),
@@ -271,7 +282,7 @@
         limit=32,
     )
     edge = call(
-        edges_kernel, [live, back, ahead, spectra, from_below, from_above],
+        edges_kernel, [live, back, ahead, spectra, *halos],
         shape(DIM, 2 * BLOCK, bf16), 2 * per_block,
     )
 
@@ -282,18 +293,18 @@
         [(d * reps + r, d * reps + partners(r, d & 1, reps)[step]) for d in range(bands) for r in range(reps)]
         for step in range(2)
     ]
-    x_far = lax.ppermute(sum_pair(True, True, bf16), both, away_pairs)
-    x_near = lax.ppermute(sum_pair(False, True, bf16), both, away_pairs)
-    own_far = sum_pair(True, False, f32)
-    far = call(far_kernel, [own_far, x_far], shape(2 * CL_DEV, DIM, bf16), 1 << 20)
-    got_first = lax.ppermute(far, both, swaps[0])
-    own_near = sum_pair(False, False, f32)
-    after_first, mine = call(
-        join_kernel, [own_near, x_near, got_first],
-        [shape(CL_DEV, DIM, bf16), shape(CL_DEV, DIM, f32)], 1 << 20,
-    )
-    got_second = lax.ppermute(after_first, both, swaps[1])
-    return call(finish_kernel, [mine, got_second], shape(CL_DEV, DIM, f32), 1 << 20)
+    arrived = {role: lax.ppermute(sum_block(role, True), both, away_pairs) for role in (3, 1, 2, 0)}
+
+    def exchanged(role, step, *more):
+        own = sum_block(role, False)
+        block = call(add_kernel, [own, arrived[role], *more], shape(CL_DEV, DIM, bf16), 1 << 20)
+        return lax.ppermute(block, both, swaps[step])
+
+    for_second = exchanged(3, 0)
+    mine_first = exchanged(1, 0)
+    mine_second = exchanged(2, 1, for_second)
+    own = sum_block(0, False)
+    return call(finish_kernel, [own, arrived[0], mine_first, mine_second], shape(CL_DEV, DIM, f32), 1 << 20)
 
 
 def solution(mesh):

time: 73.6 us -> 67.8 us (0.921)
  waiting for transfers between devices: 26.5 us -> 9.24 us
  starting transfers between devices: 12.8 us -> 23.2 us
  Pallas kernels: 32.3 us -> 33.2 us
    ppermute x6 -> x9, waiting for transfers between devices: 26.5 us -> 9.24 us  [the longest x3 9.22 us: exchanged(): return lax.ppermute(block, both, swaps[step])]
    ppermute x6 -> x9, starting transfers between devices: 12.8 us -> 23.2 us  [the longest x4 13.1 us: shards(): lax.ppermute(sum_block(role, True), both, away_pairs)]
    pallas_call x10 -> x15, Pallas kernels: 32.3 us -> 33.2 us  [call(): pl.pallas_call(kernel, out_shape=out_shape, in_specs=in_specs, out_specs=...]
  transfers between devices with their start and end apart: 6 -> 9, of which waited for: 4 -> 2; matrix products, arithmetic and copies ran while one was open for 0% -> 0% of each run, Pallas kernels for 33% -> 41%
where the time goes in v5:
time: 67.8 us; the launch traced here: 67.6 us
  Pallas kernels  33.2 us (49%)
  starting transfers between devices  23.2 us (34%)
  waiting for transfers between devices  9.24 us (14%)
  local copies, waits for them, and re-layouts  1.09 us (2%)
  between operations  0.92 us (1%)
    pallas_call x15, Pallas kernels, call(): pl.pallas_call(kernel, out_shape=out_shape, in_specs=in_specs, out_specs=...  33.2 us
    ppermute x4, starting transfers between devices, shards(): lax.ppermute(sum_block(role, True), both, away_pairs)  13.1 us
    ppermute x3, waiting for transfers between devices, exchanged(): return lax.ppermute(block, both, swaps[step])  9.22 us
    ppermute x2, starting transfers between devices, shards(): lax.ppermute(block, both, sorted((pair[::way] for pair in pairs[turn::2]...  6.15 us
    ppermute x3, starting transfers between devices, exchanged(): return lax.ppermute(block, both, swaps[step])  3.9 us
  transfers between devices with their start and end apart: 9, of which 2 were waited for; matrix products, arithmetic and copies ran while one was open for 0% of the time, Pallas kernels for 41%

profile of v5, /device:TPU:103, one launch (start us, length us, event | category | flops | bytes accessed | tf_op | source)
XLA Modules:
  0.0 67.6 jit_solution(3668647318469562683)
XLA Ops:
  0.7 1.1 %fusion = (bf16[256,512]{1,0:T(8,128)(2,1)S(1)}, bf16[256,512]{1,0:T(8,128)(2,1)S(1)}) fusion(bf16[4096,512]{1,0:T(8,128)(2,1)} %spectra_ref.1), kind=kLoop, calls=%fused_computation | loop fusion | bytes 1048576 | tf_op jit(solution)/shard_map/slice | solution.py:266
  1.8 1.4 %collective-permute-start = (bf16[272,512]{1,0:T(8,128)(2,1)S(1)}, bf16[272,512]{1,0:T(8,128)(2,1)S(1)}, u32[]{:S(2)}, u32[]{:S(2)}) collective-permute-start(bf16[272,512]{1,0:T(8,128)(2,1)S(1)} %get-tuple-element.7), channel_id=1, source_target_pairs={{0,1},{1,0},{2,3},{3,2},{4,5},{5,4},{6,7},{7,6},{8,9},{9,8},{10,11... | collective-permute-start | bytes 835592 | tf_op jit(solution)/shard_map/ppermute | solution.py:271
  3.2 4.8 %collective-permute-start.1 = (bf16[272,512]{1,0:T(8,128)(2,1)S(1)}, bf16[272,512]{1,0:T(8,128)(2,1)S(1)}, u32[]{:S(2)}, u32[]{:S(2)}) collective-permute-start(bf16[272,512]{1,0:T(8,128)(2,1)S(1)} %get-tuple-element.8), channel_id=1, source_target_pairs={{1,2},{2,1},{3,4},{4,3},{5,6},{6,5},{7,8},{8,7},{9,10},{10,9},{11,... | collective-permute-start | bytes 835592 | tf_op jit(solution)/shard_map/ppermute | solution.py:271
  8.0 10.7 %shard_map.55.inner_ref = bf16[512,3584]{1,0:T(8,128)(2,1)S(1)} custom-call(s32[1]{0:T(128)S(6)} %copy.6.live_ref, s32[1,4096]{1,0:T(1,128)S(1)} %bitcast.3, s32[1,4096]{1,0:T(1,128)S(1)} %bitcast.5, bf16[4096,512]{1,0:T(8,128)(2,1)S(1)} %copy-done), custom_call_target="tpu_custom_call" | custom-call | flops 5637144576 | bytes 4227076 | tf_op jit(solution)/shard_map/pallas_call | solution.py:238
  18.7 1.9 %shard_map.57.edge_ref = bf16[512,512]{1,0:T(8,128)(2,1)S(1)} custom-call(s32[1]{0:T(128)S(6)} %copy.6.live_ref, s32[1,4096]{1,0:T(1,128)S(1)} %bitcast.4, s32[1,4096]{1,0:T(1,128)S(1)} %bitcast.6, bf16[4096,512]{1,0:T(8,128)(2,1)S(1)} %copy-done, bf16[272,512]{1,0:T(8,128)(2,1)S(1)} %collective-permute-done.one_ref, ...), custom_call_target="tpu_custom_call" | custom-call | flops 805306368 | bytes 4784132 | tf_op jit(solution)/shard_map/pallas_call | solution.py:238
  20.6 2.4 %shard_map.66 = bf16[512,512]{1,0:T(8,128)(2,1)S(1)} custom-call(s32[1]{0:T(128)S(6)} %copy.6.live_ref, s32[1,4096]{1,0:T(1,128)S(1)} %bitcast.7, bf16[512,3584]{1,0:T(8,128)(2,1)S(1)} %shard_map.55.inner_ref, bf16[512,512]{1,0:T(8,128)(2,1)S(1)} %shard_map.57.edge_ref), custom_call_target="tpu_custom_call" | custom-call | flops 2147483648 | bytes 4210692 | tf_op jit(solution)/shard_map/pallas_call | solution.py:238
  23.0 1.9 %collective-permute-start.6 = (bf16[512,512]{1,0:T(8,128)(2,1)S(1)}, bf16[512,512]{1,0:T(8,128)(2,1)S(1)}, u32[]{:S(2)}, u32[]{:S(2)}) collective-permute-start(bf16[512,512]{1,0:T(8,128)(2,1)S(1)} %shard_map.66), channel_id=1, source_target_pairs={{4,0},{8,4},{12,8},{16,12},{20,16},{24,20},{28,24},{32,28},{36,32}... | collective-permute-start | bytes 1572872 | tf_op jit(solution)/shard_map/ppermute | solution.py:296
  24.9 2.4 %shard_map.64 = bf16[512,512]{1,0:T(8,128)(2,1)S(1)} custom-call(s32[1]{0:T(128)S(6)} %copy.6.live_ref, s32[1,4096]{1,0:T(1,128)S(1)} %bitcast.8, bf16[512,3584]{1,0:T(8,128)(2,1)S(1)} %shard_map.55.inner_ref, bf16[512,512]{1,0:T(8,128)(2,1)S(1)} %shard_map.57.edge_ref), custom_call_target="tpu_custom_call" | custom-call | flops 2147483648 | bytes 4210692 | tf_op jit(solution)/shard_map/pallas_call | solution.py:238
  27.3 2.8 %collective-permute-start.5 = (bf16[512,512]{1,0:T(8,128)(2,1)S(1)}, bf16[512,512]{1,0:T(8,128)(2,1)S(1)}, u32[]{:S(2)}, u32[]{:S(2)}) collective-permute-start(bf16[512,512]{1,0:T(8,128)(2,1)S(1)} %shard_map.64), channel_id=1, source_target_pairs={{4,0},{8,4},{12,8},{16,12},{20,16},{24,20},{28,24},{32,28},{36,32}... | collective-permute-start | bytes 1572872 | tf_op jit(solution)/shard_map/ppermute | solution.py:296
  30.1 2.4 %shard_map.61 = bf16[512,512]{1,0:T(8,128)(2,1)S(1)} custom-call(s32[1]{0:T(128)S(6)} %copy.6.live_ref, s32[1,4096]{1,0:T(1,128)S(1)} %bitcast.9, bf16[512,3584]{1,0:T(8,128)(2,1)S(1)} %shard_map.55.inner_ref, bf16[512,512]{1,0:T(8,128)(2,1)S(1)} %shard_map.57.edge_ref), custom_call_target="tpu_custom_call" | custom-call | flops 2147483648 | bytes 4210692 | tf_op jit(solution)/shard_map/pallas_call | solution.py:238
  32.5 1.9 %collective-permute-start.3 = (bf16[512,512]{1,0:T(8,128)(2,1)S(1)}, bf16[512,512]{1,0:T(8,128)(2,1)S(1)}, u32[]{:S(2)}, u32[]{:S(2)}) collective-permute-start(bf16[512,512]{1,0:T(8,128)(2,1)S(1)} %shard_map.61), channel_id=1, source_target_pairs={{4,0},{8,4},{12,8},{16,12},{20,16},{24,20},{28,24},{32,28},{36,32}... | collective-permute-start | bytes 1572872 | tf_op jit(solution)/shard_map/ppermute | solution.py:296
  34.4 2.4 %shard_map.65.own_ref = f32[512,512]{1,0:T(8,128)S(1)} custom-call(s32[1]{0:T(128)S(6)} %copy.6.live_ref, s32[1,4096]{1,0:T(1,128)S(1)} %bitcast.10, bf16[512,3584]{1,0:T(8,128)(2,1)S(1)} %shard_map.55.inner_ref, bf16[512,512]{1,0:T(8,128)(2,1)S(1)} %shard_map.57.edge_ref), custom_call_target="tpu_custom_call" | custom-call | flops 2147483648 | bytes 4210692 | tf_op jit(solution)/shard_map/pallas_call | solution.py:238
  36.9 0.3 collective-permute-start.7
  37.2 2.4 %shard_map.59 = bf16[512,512]{1,0:T(8,128)(2,1)S(1)} custom-call(s32[1]{0:T(128)S(6)} %copy.6.live_ref, s32[1,4096]{1,0:T(1,128)S(1)} %bitcast.11, bf16[512,3584]{1,0:T(8,128)(2,1)S(1)} %shard_map.55.inner_ref, bf16[512,512]{1,0:T(8,128)(2,1)S(1)} %shard_map.57.edge_ref), custom_call_target="tpu_custom_call" | custom-call | flops 2147483648 | bytes 4210692 | tf_op jit(solution)/shard_map/pallas_call | solution.py:238
  39.6 6.4 %collective-permute-start.2 = (bf16[512,512]{1,0:T(8,128)(2,1)S(1)}, bf16[512,512]{1,0:T(8,128)(2,1)S(1)}, u32[]{:S(2)}, u32[]{:S(2)}) collective-permute-start(bf16[512,512]{1,0:T(8,128)(2,1)S(1)} %shard_map.59), channel_id=1, source_target_pairs={{4,0},{8,4},{12,8},{16,12},{20,16},{24,20},{28,24},{32,28},{36,32}... | collective-permute-start | bytes 1572872 | tf_op jit(solution)/shard_map/ppermute | solution.py:296
  46.0 2.4 %shard_map.63.own_ref = f32[512,512]{1,0:T(8,128)S(1)} custom-call(s32[1]{0:T(128)S(6)} %copy.6.live_ref, s32[1,4096]{1,0:T(1,128)S(1)} %bitcast.12, bf16[512,3584]{1,0:T(8,128)(2,1)S(1)} %shard_map.55.inner_ref, bf16[512,512]{1,0:T(8,128)(2,1)S(1)} %shard_map.57.edge_ref), custom_call_target="tpu_custom_call" | custom-call | flops 2147483648 | bytes 4210692 | tf_op jit(solution)/shard_map/pallas_call | solution.py:238
  48.4 2.4 %shard_map.60.own_ref = f32[512,512]{1,0:T(8,128)S(1)} custom-call(s32[1]{0:T(128)S(6)} %copy.6.live_ref, s32[1,4096]{1,0:T(1,128)S(1)} %bitcast.13, bf16[512,3584]{1,0:T(8,128)(2,1)S(1)} %shard_map.55.inner_ref, bf16[512,512]{1,0:T(8,128)(2,1)S(1)} %shard_map.57.edge_ref), custom_call_target="tpu_custom_call" | custom-call | flops 2147483648 | bytes 4210692 | tf_op jit(solution)/shard_map/pallas_call | solution.py:238
  50.8 0.1 collective-permute-start.4
  51.0 0.2 shard_map.68
  51.1 3.5 %collective-permute-start.8 = (bf16[512,512]{1,0:T(8,128)(2,1)S(1)}, bf16[512,512]{1,0:T(8,128)(2,1)S(1)}, u32[]{:S(2)}, u32[]{:S(2)}) collective-permute-start(bf16[512,512]{1,0:T(8,128)(2,1)S(1)} %shard_map.68), channel_id=1, source_target_pairs={{0,1},{1,0},{2,3},{3,2},{4,7},{5,6},{6,5},{7,4},{8,9},{9,8},{10,11... | collective-permute-start | bytes 1572872 | tf_op jit(solution)/shard_map/ppermute | solution.py:301
  54.7 2.4 %shard_map.58.own_ref = f32[512,512]{1,0:T(8,128)S(1)} custom-call(s32[1]{0:T(128)S(6)} %copy.6.live_ref, s32[1,4096]{1,0:T(1,128)S(1)} %bitcast.14, bf16[512,3584]{1,0:T(8,128)(2,1)S(1)} %shard_map.55.inner_ref, bf16[512,512]{1,0:T(8,128)(2,1)S(1)} %shard_map.57.edge_ref), custom_call_target="tpu_custom_call" | custom-call | flops 2147483648 | bytes 4210692 | tf_op jit(solution)/shard_map/pallas_call | solution.py:238
  57.0 7.1 %collective-permute-done.4.rest_1_ = bf16[512,512]{1,0:T(8,128)(2,1)S(1)} collective-permute-done((bf16[512,512]{1,0:T(8,128)(2,1)S(1)}, bf16[512,512]{1,0:T(8,128)(2,1)S(1)}, u32[]{:S(2)}, u32[]{:S(2)}) %collective-permute-start.4) | collective-permute-done | bytes 524320 | tf_op jit(solution)/shard_map/ppermute | solution.py:301
  64.1 2.1 %collective-permute-done.8.rest_2_ = bf16[512,512]{1,0:T(8,128)(2,1)S(1)} collective-permute-done((bf16[512,512]{1,0:T(8,128)(2,1)S(1)}, bf16[512,512]{1,0:T(8,128)(2,1)S(1)}, u32[]{:S(2)}, u32[]{:S(2)}) %collective-permute-start.8) | collective-permute-done | bytes 524320 | tf_op jit(solution)/shard_map/ppermute | solution.py:301
  66.2 1.4 %shard_map.69 = f32[512,512]{1,0:T(8,128)} custom-call(f32[512,512]{1,0:T(8,128)S(1)} %shard_map.58.own_ref, bf16[512,512]{1,0:T(8,128)(2,1)S(1)} %collective-permute-done.2.rest_0_, bf16[512,512]{1,0:T(8,128)(2,1)S(1)} %collective-permute-done.4.rest_1_, bf16[512,512]{1,0:T(8,128)(2,1)S(1)} %collective-permute-done.8.rest_2_), custom_call_target="tpu_custom_call" | custom-call | flops 1048576 | bytes 2621440 | tf_op jit(solution)/shard_map/pallas_call | solution.py:238
  (18 shorter events, 0.3 us)
Async XLA Ops:
  1.7 6.3 %copy-start = (bf16[4096,512]{1,0:T(8,128)(2,1)S(1)}, bf16[4096,512]{1,0:T(8,128)(2,1)}, u32[]{:S(2)}) copy-start(bf16[4096,512]{1,0:T(8,128)(2,1)} %spectra_ref.1) | copy-start | bytes 12582916
  1.7 6.3 %copy-start.1 = (s32[4096]{0:T(1024)S(1)}, s32[4096]{0:T(1024)}, u32[]{:S(2)}) copy-start(s32[4096]{0:T(1024)} %param.6) | copy-start | bytes 49156
  1.7 6.3 %copy-start.2 = (s32[4096]{0:T(1024)S(1)}, s32[4096]{0:T(1024)}, u32[]{:S(2)}) copy-start(s32[4096]{0:T(1024)} %param.7) | copy-start | bytes 49156
  1.8 16.9 %collective-permute-start = (bf16[272,512]{1,0:T(8,128)(2,1)S(1)}, bf16[272,512]{1,0:T(8,128)(2,1)S(1)}, u32[]{:S(2)}, u32[]{:S(2)}) collective-permute-start(bf16[272,512]{1,0:T(8,128)(2,1)S(1)} %get-tuple-element.7), channel_id=1, source_target_pairs={{0,1},{1,0},{2,3},{3,2},{4,5},{5,4},{6,7},{7,6},{8,9},{9,8},{10,11... | collective-permute-start | bytes 835592 | tf_op jit(solution)/shard_map/ppermute | solution.py:271
  3.2 15.5 %collective-permute-start.1 = (bf16[272,512]{1,0:T(8,128)(2,1)S(1)}, bf16[272,512]{1,0:T(8,128)(2,1)S(1)}, u32[]{:S(2)}, u32[]{:S(2)}) collective-permute-start(bf16[272,512]{1,0:T(8,128)(2,1)S(1)} %get-tuple-element.8), channel_id=1, source_target_pairs={{1,2},{2,1},{3,4},{4,3},{5,6},{6,5},{7,8},{8,7},{9,10},{10,9},{11,... | collective-permute-start | bytes 835592 | tf_op jit(solution)/shard_map/ppermute | solution.py:271
  18.7 1.9 %copy-start.3 = (s32[4096]{0:T(1024)S(1)}, s32[4096]{0:T(1024)}, u32[]{:S(2)}) copy-start(s32[4096]{0:T(1024)} %param.9) | copy-start | bytes 49156
  23.0 13.8 %collective-permute-start.6 = (bf16[512,512]{1,0:T(8,128)(2,1)S(1)}, bf16[512,512]{1,0:T(8,128)(2,1)S(1)}, u32[]{:S(2)}, u32[]{:S(2)}) collective-permute-start(bf16[512,512]{1,0:T(8,128)(2,1)S(1)} %shard_map.66), channel_id=1, source_target_pairs={{4,0},{8,4},{12,8},{16,12},{20,16},{24,20},{28,24},{32,28},{36,32}... | collective-permute-start | bytes 1572872 | tf_op jit(solution)/shard_map/ppermute | solution.py:296
  27.3 23.7 %collective-permute-start.5 = (bf16[512,512]{1,0:T(8,128)(2,1)S(1)}, bf16[512,512]{1,0:T(8,128)(2,1)S(1)}, u32[]{:S(2)}, u32[]{:S(2)}) collective-permute-start(bf16[512,512]{1,0:T(8,128)(2,1)S(1)} %shard_map.64), channel_id=1, source_target_pairs={{4,0},{8,4},{12,8},{16,12},{20,16},{24,20},{28,24},{32,28},{36,32}... | collective-permute-start | bytes 1572872 | tf_op jit(solution)/shard_map/ppermute | solution.py:296
  32.5 18.2 %collective-permute-start.3 = (bf16[512,512]{1,0:T(8,128)(2,1)S(1)}, bf16[512,512]{1,0:T(8,128)(2,1)S(1)}, u32[]{:S(2)}, u32[]{:S(2)}) collective-permute-start(bf16[512,512]{1,0:T(8,128)(2,1)S(1)} %shard_map.61), channel_id=1, source_target_pairs={{4,0},{8,4},{12,8},{16,12},{20,16},{24,20},{28,24},{32,28},{36,32}... | collective-permute-start | bytes 1572872 | tf_op jit(solution)/shard_map/ppermute | solution.py:296
  36.9 14.0 %collective-permute-start.7 = (bf16[512,512]{1,0:T(8,128)(2,1)S(1)}, bf16[512,512]{1,0:T(8,128)(2,1)S(1)}, u32[]{:S(2)}, u32[]{:S(2)}) collective-permute-start(bf16[512,512]{1,0:T(8,128)(2,1)S(1)} %shard_map.67), channel_id=1, source_target_pairs={{0,3},{1,2},{2,1},{3,0},{4,5},{5,4},{6,7},{7,6},{8,11},{9,10},{10,... | collective-permute-start | bytes 1572872 | tf_op jit(solution)/shard_map/ppermute | solution.py:301
  39.6 17.5 %collective-permute-start.2 = (bf16[512,512]{1,0:T(8,128)(2,1)S(1)}, bf16[512,512]{1,0:T(8,128)(2,1)S(1)}, u32[]{:S(2)}, u32[]{:S(2)}) collective-permute-start(bf16[512,512]{1,0:T(8,128)(2,1)S(1)} %shard_map.59), channel_id=1, source_target_pairs={{4,0},{8,4},{12,8},{16,12},{20,16},{24,20},{28,24},{32,28},{36,32}... | collective-permute-start | bytes 1572872 | tf_op jit(solution)/shard_map/ppermute | solution.py:296
  50.8 13.3 %collective-permute-start.4 = (bf16[512,512]{1,0:T(8,128)(2,1)S(1)}, bf16[512,512]{1,0:T(8,128)(2,1)S(1)}, u32[]{:S(2)}, u32[]{:S(2)}) collective-permute-start(bf16[512,512]{1,0:T(8,128)(2,1)S(1)} %shard_map.62), channel_id=1, source_target_pairs={{0,3},{1,2},{2,1},{3,0},{4,5},{5,4},{6,7},{7,6},{8,11},{9,10},{10,... | collective-permute-start | bytes 1572872 | tf_op jit(solution)/shard_map/ppermute | solution.py:301
  51.1 15.1 %collective-permute-start.8 = (bf16[512,512]{1,0:T(8,128)(2,1)S(1)}, bf16[512,512]{1,0:T(8,128)(2,1)S(1)}, u32[]{:S(2)}, u32[]{:S(2)}) collective-permute-start(bf16[512,512]{1,0:T(8,128)(2,1)S(1)} %shard_map.68), channel_id=1, source_target_pairs={{0,1},{1,0},{2,3},{3,2},{4,7},{5,6},{6,5},{7,4},{8,9},{9,8},{10,11... | collective-permute-start | bytes 1572872 | tf_op jit(solution)/shard_map/ppermute | solution.py:301

commit v6 on v5

--- a/solution.py
+++ b/solution.py
@@ -30,15 +30,15 @@
     return jnp.transpose(unit)
 
 
-def attend(query, back, ahead, cap, keys, keys_t, low_cap, high_cap):
+def attend(query, back, ahead, cap, keys, keys_t, low_cap, high_cap, score_ref, weight_ref):
     at = lax.broadcasted_iota(i32, (1, BLOCK), 1) + BLOCK
     low = at - back
     high = at + ahead
     own = jnp.minimum(high, cap - 1)
-    total = None
-    mixed = None
+    total = jnp.zeros((1, BLOCK), f32)
+    score_ref[...] = lax.dot_general(keys, query, NT, preferred_element_type=f32)
     for k in range(3):
-        scores = lax.dot_general(keys[k], query, NT, preferred_element_type=f32)
+        span = slice(k * BLOCK, (k + 1) * BLOCK)
         slot = lax.broadcasted_iota(i32, (BLOCK, BLOCK), 0) + k * BLOCK
         if k == 0:
             keep = slot >= low
@@ -50,11 +50,10 @@
             keep = slot <= own
         else:
             keep = slot <= jnp.minimum(high, high_cap - 1)
-        weight = jnp.where(keep, jnp.exp2(scores * SCALE - SCALE), 0.0)
-        part = jnp.sum(weight, axis=0, keepdims=True)
-        term = jnp.dot(keys_t[k], weight.astype(bf16), preferred_element_type=f32)
-        total = part if total is None else total + part
-        mixed = term if mixed is None else mixed + term
+        weight = jnp.where(keep, jnp.exp2(score_ref[span, :] * SCALE - SCALE), 0.0)
+        total = total + jnp.sum(weight, axis=0, keepdims=True)
+        weight_ref[span, :] = weight.astype(bf16)
+    mixed = jnp.dot(keys_t, weight_ref[...], preferred_element_type=f32)
     return (mixed * (1.0 / total)).astype(bf16)
 
 
@@ -88,11 +87,8 @@
         unit_t_ref[:, block(index)] = transposed(unit)
 
     def score(index, score_ref):
-        query = unit_ref[block(index), :]
-        for k in range(3):
-            score_ref[k * BLOCK : (k + 1) * BLOCK, :] = lax.dot_general(
-                unit_ref[block(index + k - 1), :], query, NT, preferred_element_type=f32
-            )
+        keys = unit_ref[pl.ds(pl.multiple_of((index - 1) * BLOCK, BLOCK), 3 * BLOCK), :]
+        score_ref[...] = lax.dot_general(keys, unit_ref[block(index), :], NT, preferred_element_type=f32)
 
     def finish(index, score_ref, weight_ref):
         at = lax.broadcasted_iota(i32, (1, BLOCK), 1) + BLOCK
@@ -130,30 +126,40 @@
     lax.fori_loop(0, (NBLK - 2) // 2, step, 0)
 
 
-def edges_kernel(live_ref, back_ref, ahead_ref, spectra_ref, one_ref, two_ref, out_ref):
+def edges_kernel(
+    live_ref, back_ref, ahead_ref, spectra_ref, one_ref, two_ref, out_ref,
+    keys_ref, keys_t_ref, score_a, score_b, weight_a, weight_b,
+):
     live = live_ref[0]
     even = lax.axis_index("rep") % 2 == 0
-    one, two = one_ref[...].astype(f32), two_ref[...].astype(f32)
-    below = jnp.where(even, two, one)
-    above = jnp.where(even, one, two)
-
-    def count(rows):
-        digits = rows[BLOCK : BLOCK + 8, :BLOCK]
+
+    def count(ref):
+        digits = ref[BLOCK : BLOCK + 8, :BLOCK].astype(f32)
         return (digits[0:1] * 64.0 + digits[1:2]).astype(i32)
 
-    def unit(block):
-        return unit_rows(spectra_ref[block * BLOCK : (block + 1) * BLOCK, :])
-
-    keys = [unit_rows(below[:BLOCK]), unit(0), unit(1)]
+    count_one, count_two = count(one_ref), count(two_ref)
+    count_below = jnp.where(even, count_two, count_one)
+    count_above = jnp.where(even, count_one, count_two)
+
+    def rows(block):
+        return spectra_ref[block * BLOCK : (block + 1) * BLOCK, :]
+
+    slot = jnp.where(even, 5, 0)
+    blocks = ((1, rows(0)), (2, rows(1)), (3, rows(NBLK - 2)), (4, rows(NBLK - 1)))
+    for n, block in blocks + ((slot, one_ref[:BLOCK, :]), (5 - slot, two_ref[:BLOCK, :])):
+        unit = unit_rows(block)
+        span = pl.ds(n * BLOCK if isinstance(n, int) else pl.multiple_of(n * BLOCK, BLOCK), BLOCK)
+        keys_ref[span, :] = unit
+        keys_t_ref[:, span] = transposed(unit)
+    side = 3 * BLOCK
     out_ref[:, :BLOCK] = attend(
-        keys[1], back_ref[:, :BLOCK], ahead_ref[:, :BLOCK], live + BLOCK, keys,
-        [transposed(k) for k in keys], count(below) - (ROWS - BLOCK), None,
-    )
-    keys = [unit(NBLK - 2), unit(NBLK - 1), unit_rows(above[:BLOCK])]
+        keys_ref[BLOCK : 2 * BLOCK, :], back_ref[:, :BLOCK], ahead_ref[:, :BLOCK], live + BLOCK,
+        keys_ref[:side, :], keys_t_ref[:, :side], count_below - (ROWS - BLOCK), None, score_a, weight_a,
+    )
     out_ref[:, BLOCK:] = attend(
-        keys[1], back_ref[:, ROWS - BLOCK :], ahead_ref[:, ROWS - BLOCK :],
-        live - (ROWS - 2 * BLOCK), keys, [transposed(k) for k in keys],
-        None, count(above) + 2 * BLOCK,
+        keys_ref[side + BLOCK : side + 2 * BLOCK, :], back_ref[:, ROWS - BLOCK :], ahead_ref[:, ROWS - BLOCK :],
+        live - (ROWS - 2 * BLOCK), keys_ref[side:, :], keys_t_ref[:, side:], None, count_above + 2 * BLOCK,
+        score_b, weight_b,
     )
 
 
@@ -214,13 +220,24 @@
     rest[-1][...] = total.astype(bf16)
 
 
+PIECES = 4
+
+
 def finish_kernel(own_ref, *rest):
-    out_ref = rest[-1]
-    owned = own_ref[...]
-    for ref in rest[:-1]:
-        owned = owned + ref[...].astype(f32)
-    mean = jnp.sum(owned * owned, axis=1, keepdims=True) * (1.0 / DIM)
-    out_ref[...] = owned / jnp.sqrt(mean + 1e-06)
+    *parts, out_hbm, done_ref, sems = rest
+    rows = CL_DEV // PIECES
+    copies = []
+    for n in range(PIECES):
+        span = slice(n * rows, (n + 1) * rows)
+        owned = own_ref[span, :]
+        for ref in parts:
+            owned = owned + ref[span, :].astype(f32)
+        mean = jnp.sum(owned * owned, axis=1, keepdims=True) * (1.0 / DIM)
+        done_ref[span, :] = owned / jnp.sqrt(mean + 1e-06)
+        copies.append(pltpu.make_async_copy(done_ref.at[pl.ds(n * rows, rows)], out_hbm.at[pl.ds(n * rows, rows)], sems.at[n]))
+        copies[-1].start()
+    for copy in copies:
+        copy.wait()
 
 
 VMEM = pl.BlockSpec(memory_space=pltpu.VMEM)
@@ -229,17 +246,17 @@
 MIB = 1024 * 1024
 
 
-def call(kernel, inputs, out_shape, flops, scratch=(), far=(), limit=16):
+def call(kernel, inputs, out_shape, flops, scratch=(), far_out=False, limit=16):
     one = not isinstance(out_shape, (list, tuple))
     in_specs = [
-        FARREF if n in far else SMEM if x.dtype == i32 and x.size < 64 else VMEM for n, x in enumerate(inputs)
+        SMEM if x.dtype == i32 and x.size < 64 else VMEM for x in inputs
     ]
     moved = sum(x.size * x.dtype.itemsize for x in inputs)
     return pl.pallas_call(
         kernel,
         out_shape=out_shape,
         in_specs=in_specs,
-        out_specs=VMEM if one else [VMEM] * len(out_shape),
+        out_specs=FARREF if far_out else VMEM if one else [VMEM] * len(out_shape),
         scratch_shapes=list(scratch),
         cost_estimate=pl.CostEstimate(flops=flops, bytes_accessed=moved, transcendentals=0),
         compiler_params=pltpu.CompilerParams(vmem_limit_bytes=limit * MIB),
@@ -284,6 +301,11 @@
     edge = call(
         edges_kernel, [live, back, ahead, spectra, *halos],
         shape(DIM, 2 * BLOCK, bf16), 2 * per_block,
+        [
+            pltpu.VMEM((6 * BLOCK, DIM), bf16), pltpu.VMEM((DIM, 6 * BLOCK), bf16),
+            pltpu.VMEM((3 * BLOCK, BLOCK), f32), pltpu.VMEM((3 * BLOCK, BLOCK), f32),
+            pltpu.VMEM((3 * BLOCK, BLOCK), bf16), pltpu.VMEM((3 * BLOCK, BLOCK), bf16),
+        ],
     )
 
     last = reps - 1
@@ -304,7 +326,10 @@
     mine_first = exchanged(1, 0)
     mine_second = exchanged(2, 1, for_second)
     own = sum_block(0, False)
-    return call(finish_kernel, [own, arrived[0], mine_first, mine_second], shape(CL_DEV, DIM, f32), 1 << 20)
+    return call(
+        finish_kernel, [own, arrived[0], mine_first, mine_second], shape(CL_DEV, DIM, f32), 1 << 20,
+        [pltpu.VMEM((CL_DEV, DIM), f32), pltpu.SemaphoreType.DMA((PIECES,))], far_out=True,
+    )
 
 
 def solution(mesh):

time: 67.8 us -> 67.1 us (0.990)
  Pallas kernels: 33.2 us -> 32.3 us
    pallas_call x15, Pallas kernels: 33.2 us -> 32.3 us  [call(): pl.pallas_call(kernel, out_shape=out_shape, in_specs=in_specs, out_specs=...]
  transfers between devices with their start and end apart: 9 -> 9, of which waited for: 2 -> 2; matrix products, arithmetic and copies ran while one was open for 0% -> 0% of each run, Pallas kernels for 41% -> 40%
where the time goes in v6:
time: 67.1 us; the launch traced here: 66.9 us
  Pallas kernels  32.3 us (48%)
  starting transfers between devices  23.2 us (35%)
  waiting for transfers between devices  9.24 us (14%)
  local copies, waits for them, and re-layouts  1.09 us (2%)
  between operations  1.09 us (2%)
    pallas_call x15, Pallas kernels, call(): pl.pallas_call(kernel, out_shape=out_shape, in_specs=in_specs, out_specs=...  32.3 us
    ppermute x4, starting transfers between devices, shards(): lax.ppermute(sum_block(role, True), both, away_pairs)  13.1 us
    ppermute x3, waiting for transfers between devices, exchanged(): return lax.ppermute(block, both, swaps[step])  9.22 us
    ppermute x2, starting transfers between devices, shards(): lax.ppermute(block, both, sorted((pair[::way] for pair in pairs[turn::2]...  6.15 us
    ppermute x3, starting transfers between devices, exchanged(): return lax.ppermute(block, both, swaps[step])  3.9 us
  transfers between devices with their start and end apart: 9, of which 2 were waited for; matrix products, arithmetic and copies ran while one was open for 0% of the time, Pallas kernels for 40%

profile of v6, /device:TPU:103, one launch (start us, length us, event | category | flops | bytes accessed | tf_op | source)
XLA Modules:
  0.0 66.9 jit_solution(9304476656991223339)
XLA Ops:
  0.7 1.1 %fusion = (bf16[256,512]{1,0:T(8,128)(2,1)S(1)}, bf16[256,512]{1,0:T(8,128)(2,1)S(1)}) fusion(bf16[4096,512]{1,0:T(8,128)(2,1)} %spectra_ref.1), kind=kLoop, calls=%fused_computation | loop fusion | bytes 1048576 | tf_op jit(solution)/shard_map/slice | solution.py:283
  1.8 1.4 %collective-permute-start = (bf16[272,512]{1,0:T(8,128)(2,1)S(1)}, bf16[272,512]{1,0:T(8,128)(2,1)S(1)}, u32[]{:S(2)}, u32[]{:S(2)}) collective-permute-start(bf16[272,512]{1,0:T(8,128)(2,1)S(1)} %get-tuple-element.7), channel_id=1, source_target_pairs={{0,1},{1,0},{2,3},{3,2},{4,5},{5,4},{6,7},{7,6},{8,9},{9,8},{10,11... | collective-permute-start | bytes 835592 | tf_op jit(solution)/shard_map/ppermute | solution.py:288
  3.2 4.8 %collective-permute-start.1 = (bf16[272,512]{1,0:T(8,128)(2,1)S(1)}, bf16[272,512]{1,0:T(8,128)(2,1)S(1)}, u32[]{:S(2)}, u32[]{:S(2)}) collective-permute-start(bf16[272,512]{1,0:T(8,128)(2,1)S(1)} %get-tuple-element.8), channel_id=1, source_target_pairs={{1,2},{2,1},{3,4},{4,3},{5,6},{6,5},{7,8},{8,7},{9,10},{10,9},{11,... | collective-permute-start | bytes 835592 | tf_op jit(solution)/shard_map/ppermute | solution.py:288
  8.0 9.6 %shard_map.55.inner_ref = bf16[512,3584]{1,0:T(8,128)(2,1)S(1)} custom-call(s32[1]{0:T(128)S(6)} %copy.6.live_ref, s32[1,4096]{1,0:T(1,128)S(1)} %bitcast.3, s32[1,4096]{1,0:T(1,128)S(1)} %bitcast.5, bf16[4096,512]{1,0:T(8,128)(2,1)S(1)} %copy-done), custom_call_target="tpu_custom_call" | custom-call | flops 5637144576 | bytes 4227076 | tf_op jit(solution)/shard_map/pallas_call | solution.py:255
  17.7 2.1 %shard_map.57.edge_ref = bf16[512,512]{1,0:T(8,128)(2,1)S(1)} custom-call(s32[1]{0:T(128)S(6)} %copy.6.live_ref, s32[1,4096]{1,0:T(1,128)S(1)} %bitcast.4, s32[1,4096]{1,0:T(1,128)S(1)} %bitcast.6, bf16[4096,512]{1,0:T(8,128)(2,1)S(1)} %copy-done, bf16[272,512]{1,0:T(8,128)(2,1)S(1)} %collective-permute-done.one_ref, ...), custom_call_target="tpu_custom_call" | custom-call | flops 805306368 | bytes 4784132 | tf_op jit(solution)/shard_map/pallas_call | solution.py:255
  19.7 2.4 %shard_map.66 = bf16[512,512]{1,0:T(8,128)(2,1)S(1)} custom-call(s32[1]{0:T(128)S(6)} %copy.6.live_ref, s32[1,4096]{1,0:T(1,128)S(1)} %bitcast.7, bf16[512,3584]{1,0:T(8,128)(2,1)S(1)} %shard_map.55.inner_ref, bf16[512,512]{1,0:T(8,128)(2,1)S(1)} %shard_map.57.edge_ref), custom_call_target="tpu_custom_call" | custom-call | flops 2147483648 | bytes 4210692 | tf_op jit(solution)/shard_map/pallas_call | solution.py:255
  22.1 1.9 %collective-permute-start.6 = (bf16[512,512]{1,0:T(8,128)(2,1)S(1)}, bf16[512,512]{1,0:T(8,128)(2,1)S(1)}, u32[]{:S(2)}, u32[]{:S(2)}) collective-permute-start(bf16[512,512]{1,0:T(8,128)(2,1)S(1)} %shard_map.66), channel_id=1, source_target_pairs={{4,0},{8,4},{12,8},{16,12},{20,16},{24,20},{28,24},{32,28},{36,32}... | collective-permute-start | bytes 1572872 | tf_op jit(solution)/shard_map/ppermute | solution.py:318
  24.0 2.4 %shard_map.64 = bf16[512,512]{1,0:T(8,128)(2,1)S(1)} custom-call(s32[1]{0:T(128)S(6)} %copy.6.live_ref, s32[1,4096]{1,0:T(1,128)S(1)} %bitcast.8, bf16[512,3584]{1,0:T(8,128)(2,1)S(1)} %shard_map.55.inner_ref, bf16[512,512]{1,0:T(8,128)(2,1)S(1)} %shard_map.57.edge_ref), custom_call_target="tpu_custom_call" | custom-call | flops 2147483648 | bytes 4210692 | tf_op jit(solution)/shard_map/pallas_call | solution.py:255
  26.4 2.8 %collective-permute-start.5 = (bf16[512,512]{1,0:T(8,128)(2,1)S(1)}, bf16[512,512]{1,0:T(8,128)(2,1)S(1)}, u32[]{:S(2)}, u32[]{:S(2)}) collective-permute-start(bf16[512,512]{1,0:T(8,128)(2,1)S(1)} %shard_map.64), channel_id=1, source_target_pairs={{4,0},{8,4},{12,8},{16,12},{20,16},{24,20},{28,24},{32,28},{36,32}... | collective-permute-start | bytes 1572872 | tf_op jit(solution)/shard_map/ppermute | solution.py:318
  29.3 2.4 %shard_map.61 = bf16[512,512]{1,0:T(8,128)(2,1)S(1)} custom-call(s32[1]{0:T(128)S(6)} %copy.6.live_ref, s32[1,4096]{1,0:T(1,128)S(1)} %bitcast.9, bf16[512,3584]{1,0:T(8,128)(2,1)S(1)} %shard_map.55.inner_ref, bf16[512,512]{1,0:T(8,128)(2,1)S(1)} %shard_map.57.edge_ref), custom_call_target="tpu_custom_call" | custom-call | flops 2147483648 | bytes 4210692 | tf_op jit(solution)/shard_map/pallas_call | solution.py:255
  31.7 1.9 %collective-permute-start.3 = (bf16[512,512]{1,0:T(8,128)(2,1)S(1)}, bf16[512,512]{1,0:T(8,128)(2,1)S(1)}, u32[]{:S(2)}, u32[]{:S(2)}) collective-permute-start(bf16[512,512]{1,0:T(8,128)(2,1)S(1)} %shard_map.61), channel_id=1, source_target_pairs={{4,0},{8,4},{12,8},{16,12},{20,16},{24,20},{28,24},{32,28},{36,32}... | collective-permute-start | bytes 1572872 | tf_op jit(solution)/shard_map/ppermute | solution.py:318
  33.6 2.4 %shard_map.65.own_ref = f32[512,512]{1,0:T(8,128)S(1)} custom-call(s32[1]{0:T(128)S(6)} %copy.6.live_ref, s32[1,4096]{1,0:T(1,128)S(1)} %bitcast.10, bf16[512,3584]{1,0:T(8,128)(2,1)S(1)} %shard_map.55.inner_ref, bf16[512,512]{1,0:T(8,128)(2,1)S(1)} %shard_map.57.edge_ref), custom_call_target="tpu_custom_call" | custom-call | flops 2147483648 | bytes 4210692 | tf_op jit(solution)/shard_map/pallas_call | solution.py:255
  36.0 0.3 collective-permute-start.7
  36.3 2.4 %shard_map.59 = bf16[512,512]{1,0:T(8,128)(2,1)S(1)} custom-call(s32[1]{0:T(128)S(6)} %copy.6.live_ref, s32[1,4096]{1,0:T(1,128)S(1)} %bitcast.11, bf16[512,3584]{1,0:T(8,128)(2,1)S(1)} %shard_map.55.inner_ref, bf16[512,512]{1,0:T(8,128)(2,1)S(1)} %shard_map.57.edge_ref), custom_call_target="tpu_custom_call" | custom-call | flops 2147483648 | bytes 4210692 | tf_op jit(solution)/shard_map/pallas_call | solution.py:255
  38.7 6.4 %collective-permute-start.2 = (bf16[512,512]{1,0:T(8,128)(2,1)S(1)}, bf16[512,512]{1,0:T(8,128)(2,1)S(1)}, u32[]{:S(2)}, u32[]{:S(2)}) collective-permute-start(bf16[512,512]{1,0:T(8,128)(2,1)S(1)} %shard_map.59), channel_id=1, source_target_pairs={{4,0},{8,4},{12,8},{16,12},{20,16},{24,20},{28,24},{32,28},{36,32}... | collective-permute-start | bytes 1572872 | tf_op jit(solution)/shard_map/ppermute | solution.py:318
  45.1 2.4 %shard_map.63.own_ref = f32[512,512]{1,0:T(8,128)S(1)} custom-call(s32[1]{0:T(128)S(6)} %copy.6.live_ref, s32[1,4096]{1,0:T(1,128)S(1)} %bitcast.12, bf16[512,3584]{1,0:T(8,128)(2,1)S(1)} %shard_map.55.inner_ref, bf16[512,512]{1,0:T(8,128)(2,1)S(1)} %shard_map.57.edge_ref), custom_call_target="tpu_custom_call" | custom-call | flops 2147483648 | bytes 4210692 | tf_op jit(solution)/shard_map/pallas_call | solution.py:255
  47.5 2.4 %shard_map.60.own_ref = f32[512,512]{1,0:T(8,128)S(1)} custom-call(s32[1]{0:T(128)S(6)} %copy.6.live_ref, s32[1,4096]{1,0:T(1,128)S(1)} %bitcast.13, bf16[512,3584]{1,0:T(8,128)(2,1)S(1)} %shard_map.55.inner_ref, bf16[512,512]{1,0:T(8,128)(2,1)S(1)} %shard_map.57.edge_ref), custom_call_target="tpu_custom_call" | custom-call | flops 2147483648 | bytes 4210692 | tf_op jit(solution)/shard_map/pallas_call | solution.py:255
  50.0 0.1 collective-permute-start.4
  50.1 0.2 shard_map.68
  50.3 3.5 %collective-permute-start.8 = (bf16[512,512]{1,0:T(8,128)(2,1)S(1)}, bf16[512,512]{1,0:T(8,128)(2,1)S(1)}, u32[]{:S(2)}, u32[]{:S(2)}) collective-permute-start(bf16[512,512]{1,0:T(8,128)(2,1)S(1)} %shard_map.68), channel_id=1, source_target_pairs={{0,1},{1,0},{2,3},{3,2},{4,7},{5,6},{6,5},{7,4},{8,9},{9,8},{10,11... | collective-permute-start | bytes 1572872 | tf_op jit(solution)/shard_map/ppermute | solution.py:323
  53.8 2.4 %shard_map.58.own_ref = f32[512,512]{1,0:T(8,128)S(1)} custom-call(s32[1]{0:T(128)S(6)} %copy.6.live_ref, s32[1,4096]{1,0:T(1,128)S(1)} %bitcast.14, bf16[512,3584]{1,0:T(8,128)(2,1)S(1)} %shard_map.55.inner_ref, bf16[512,512]{1,0:T(8,128)(2,1)S(1)} %shard_map.57.edge_ref), custom_call_target="tpu_custom_call" | custom-call | flops 2147483648 | bytes 4210692 | tf_op jit(solution)/shard_map/pallas_call | solution.py:255
  56.2 7.0 %collective-permute-done.4.rest_1_ = bf16[512,512]{1,0:T(8,128)(2,1)S(1)} collective-permute-done((bf16[512,512]{1,0:T(8,128)(2,1)S(1)}, bf16[512,512]{1,0:T(8,128)(2,1)S(1)}, u32[]{:S(2)}, u32[]{:S(2)}) %collective-permute-start.4) | collective-permute-done | bytes 524320 | tf_op jit(solution)/shard_map/ppermute | solution.py:323
  63.2 2.2 %collective-permute-done.8.rest_2_ = bf16[512,512]{1,0:T(8,128)(2,1)S(1)} collective-permute-done((bf16[512,512]{1,0:T(8,128)(2,1)S(1)}, bf16[512,512]{1,0:T(8,128)(2,1)S(1)}, u32[]{:S(2)}, u32[]{:S(2)}) %collective-permute-start.8) | collective-permute-done | bytes 524320 | tf_op jit(solution)/shard_map/ppermute | solution.py:323
  65.4 1.3 %shard_map.69 = f32[512,512]{1,0:T(8,128)} custom-call(f32[512,512]{1,0:T(8,128)S(1)} %shard_map.58.own_ref, bf16[512,512]{1,0:T(8,128)(2,1)S(1)} %collective-permute-done.2.rest_0_, bf16[512,512]{1,0:T(8,128)(2,1)S(1)} %collective-permute-done.4.rest_1_, bf16[512,512]{1,0:T(8,128)(2,1)S(1)} %collective-permute-done.8.rest_2_), custom_call_target="tpu_custom_call" | custom-call | flops 1048576 | bytes 2621440 | tf_op jit(solution)/shard_map/pallas_call | solution.py:255
  (18 shorter events, 0.3 us)
Async XLA Ops:
  1.7 6.3 %copy-start = (bf16[4096,512]{1,0:T(8,128)(2,1)S(1)}, bf16[4096,512]{1,0:T(8,128)(2,1)}, u32[]{:S(2)}) copy-start(bf16[4096,512]{1,0:T(8,128)(2,1)} %spectra_ref.1) | copy-start | bytes 12582916
  1.7 6.3 %copy-start.1 = (s32[4096]{0:T(1024)S(1)}, s32[4096]{0:T(1024)}, u32[]{:S(2)}) copy-start(s32[4096]{0:T(1024)} %param.6) | copy-start | bytes 49156
  1.7 6.3 %copy-start.2 = (s32[4096]{0:T(1024)S(1)}, s32[4096]{0:T(1024)}, u32[]{:S(2)}) copy-start(s32[4096]{0:T(1024)} %param.7) | copy-start | bytes 49156
  1.8 15.8 %collective-permute-start = (bf16[272,512]{1,0:T(8,128)(2,1)S(1)}, bf16[272,512]{1,0:T(8,128)(2,1)S(1)}, u32[]{:S(2)}, u32[]{:S(2)}) collective-permute-start(bf16[272,512]{1,0:T(8,128)(2,1)S(1)} %get-tuple-element.7), channel_id=1, source_target_pairs={{0,1},{1,0},{2,3},{3,2},{4,5},{5,4},{6,7},{7,6},{8,9},{9,8},{10,11... | collective-permute-start | bytes 835592 | tf_op jit(solution)/shard_map/ppermute | solution.py:288
  3.2 14.4 %collective-permute-start.1 = (bf16[272,512]{1,0:T(8,128)(2,1)S(1)}, bf16[272,512]{1,0:T(8,128)(2,1)S(1)}, u32[]{:S(2)}, u32[]{:S(2)}) collective-permute-start(bf16[272,512]{1,0:T(8,128)(2,1)S(1)} %get-tuple-element.8), channel_id=1, source_target_pairs={{1,2},{2,1},{3,4},{4,3},{5,6},{6,5},{7,8},{8,7},{9,10},{10,9},{11,... | collective-permute-start | bytes 835592 | tf_op jit(solution)/shard_map/ppermute | solution.py:288
  17.6 2.1 %copy-start.3 = (s32[4096]{0:T(1024)S(1)}, s32[4096]{0:T(1024)}, u32[]{:S(2)}) copy-start(s32[4096]{0:T(1024)} %param.9) | copy-start | bytes 49156
  22.1 13.8 %collective-permute-start.6 = (bf16[512,512]{1,0:T(8,128)(2,1)S(1)}, bf16[512,512]{1,0:T(8,128)(2,1)S(1)}, u32[]{:S(2)}, u32[]{:S(2)}) collective-permute-start(bf16[512,512]{1,0:T(8,128)(2,1)S(1)} %shard_map.66), channel_id=1, source_target_pairs={{4,0},{8,4},{12,8},{16,12},{20,16},{24,20},{28,24},{32,28},{36,32}... | collective-permute-start | bytes 1572872 | tf_op jit(solution)/shard_map/ppermute | solution.py:318
  26.4 23.7 %collective-permute-start.5 = (bf16[512,512]{1,0:T(8,128)(2,1)S(1)}, bf16[512,512]{1,0:T(8,128)(2,1)S(1)}, u32[]{:S(2)}, u32[]{:S(2)}) collective-permute-start(bf16[512,512]{1,0:T(8,128)(2,1)S(1)} %shard_map.64), channel_id=1, source_target_pairs={{4,0},{8,4},{12,8},{16,12},{20,16},{24,20},{28,24},{32,28},{36,32}... | collective-permute-start | bytes 1572872 | tf_op jit(solution)/shard_map/ppermute | solution.py:318
  31.7 18.2 %collective-permute-start.3 = (bf16[512,512]{1,0:T(8,128)(2,1)S(1)}, bf16[512,512]{1,0:T(8,128)(2,1)S(1)}, u32[]{:S(2)}, u32[]{:S(2)}) collective-permute-start(bf16[512,512]{1,0:T(8,128)(2,1)S(1)} %shard_map.61), channel_id=1, source_target_pairs={{4,0},{8,4},{12,8},{16,12},{20,16},{24,20},{28,24},{32,28},{36,32}... | collective-permute-start | bytes 1572872 | tf_op jit(solution)/shard_map/ppermute | solution.py:318
  36.0 14.0 %collective-permute-start.7 = (bf16[512,512]{1,0:T(8,128)(2,1)S(1)}, bf16[512,512]{1,0:T(8,128)(2,1)S(1)}, u32[]{:S(2)}, u32[]{:S(2)}) collective-permute-start(bf16[512,512]{1,0:T(8,128)(2,1)S(1)} %shard_map.67), channel_id=1, source_target_pairs={{0,3},{1,2},{2,1},{3,0},{4,5},{5,4},{6,7},{7,6},{8,11},{9,10},{10,... | collective-permute-start | bytes 1572872 | tf_op jit(solution)/shard_map/ppermute | solution.py:323
  38.7 17.5 %collective-permute-start.2 = (bf16[512,512]{1,0:T(8,128)(2,1)S(1)}, bf16[512,512]{1,0:T(8,128)(2,1)S(1)}, u32[]{:S(2)}, u32[]{:S(2)}) collective-permute-start(bf16[512,512]{1,0:T(8,128)(2,1)S(1)} %shard_map.59), channel_id=1, source_target_pairs={{4,0},{8,4},{12,8},{16,12},{20,16},{24,20},{28,24},{32,28},{36,32}... | collective-permute-start | bytes 1572872 | tf_op jit(solution)/shard_map/ppermute | solution.py:318
  50.0 13.2 %collective-permute-start.4 = (bf16[512,512]{1,0:T(8,128)(2,1)S(1)}, bf16[512,512]{1,0:T(8,128)(2,1)S(1)}, u32[]{:S(2)}, u32[]{:S(2)}) collective-permute-start(bf16[512,512]{1,0:T(8,128)(2,1)S(1)} %shard_map.62), channel_id=1, source_target_pairs={{0,3},{1,2},{2,1},{3,0},{4,5},{5,4},{6,7},{7,6},{8,11},{9,10},{10,... | collective-permute-start | bytes 1572872 | tf_op jit(solution)/shard_map/ppermute | solution.py:323
  50.3 15.1 %collective-permute-start.8 = (bf16[512,512]{1,0:T(8,128)(2,1)S(1)}, bf16[512,512]{1,0:T(8,128)(2,1)S(1)}, u32[]{:S(2)}, u32[]{:S(2)}) collective-permute-start(bf16[512,512]{1,0:T(8,128)(2,1)S(1)} %shard_map.68), channel_id=1, source_target_pairs={{0,1},{1,0},{2,3},{3,2},{4,7},{5,6},{6,5},{7,4},{8,9},{9,8},{10,11... | collective-permute-start | bytes 1572872 | tf_op jit(solution)/shard_map/ppermute | solution.py:323

commit v7 on v6

--- a/solution.py
+++ b/solution.py
@@ -64,7 +64,7 @@
     one_ref[BLOCK:, :] = digits
     two_ref[BLOCK:, :] = digits
     even = lax.axis_index("rep") % 2 == 0
-    for is_even, one, two in ((True, last_ref, first_ref), (False, first_ref, last_ref)):
+    for is_even, one, two in ((True, first_ref, last_ref), (False, last_ref, first_ref)):
 
         @pl.when(even == is_even)
         def _():
@@ -138,13 +138,13 @@
         return (digits[0:1] * 64.0 + digits[1:2]).astype(i32)
 
     count_one, count_two = count(one_ref), count(two_ref)
-    count_below = jnp.where(even, count_two, count_one)
-    count_above = jnp.where(even, count_one, count_two)
+    count_below = jnp.where(even, count_one, count_two)
+    count_above = jnp.where(even, count_two, count_one)
 
     def rows(block):
         return spectra_ref[block * BLOCK : (block + 1) * BLOCK, :]
 
-    slot = jnp.where(even, 5, 0)
+    slot = jnp.where(even, 0, 5)
     blocks = ((1, rows(0)), (2, rows(1)), (3, rows(NBLK - 2)), (4, rows(NBLK - 1)))
     for n, block in blocks + ((slot, one_ref[:BLOCK, :]), (5 - slot, two_ref[:BLOCK, :])):
         unit = unit_rows(block)
@@ -164,7 +164,7 @@
 
 
 INNER = ROWS - 2 * BLOCK
-CHUNK = 512
+CHUNK = 1792
 
 
 def partners(rep, parity, rep_count):
@@ -197,7 +197,7 @@
                 ],
                 axis=1,
             )
-            cluster = lax.broadcasted_iota(i32, (CL_DEV, CHUNK), 0)
+            cluster = lax.broadcasted_iota(i32, (CL_DEV, rows.shape[1]), 0)
             hot = jnp.where(cluster == wanted - first, 1.0, 0.0).astype(bf16)
             return lax.dot_general(hot, rows, NT, preferred_element_type=f32)
 
@@ -285,7 +285,7 @@
     )
     pairs = [(i, i + 1) for i in range(every - 1)]
     halos = [
-        lax.ppermute(block, both, sorted(pair[::way] for pair in pairs[turn::2] for way in (1, -1)))
+        lax.ppermute(block, both, sorted(pair[::way] for pair in pairs[1 - turn :: 2] for way in (1, -1)))
         for turn, block in enumerate(blocks)
     ]
     per_block = 4 * BLOCK * 3 * BLOCK * DIM

time: 67.1 us -> 65.8 us (0.981)
  waiting for transfers between devices: 9.24 us -> 8.53 us
    ppermute x3, waiting for transfers between devices: 9.22 us -> 8.52 us  [exchanged(): return lax.ppermute(block, both, swaps[step])]
    ppermute x3, starting transfers between devices: 3.9 us -> 4.61 us  [exchanged(): return lax.ppermute(block, both, swaps[step])]
    ppermute x4, starting transfers between devices: 13.1 us -> 12.4 us  [shards(): lax.ppermute(sum_block(role, True), both, away_pairs)]
where the time goes in v7:
time: 65.8 us; the launch traced here: 65.6 us
  Pallas kernels  32.2 us (49%)
  starting transfers between devices  22.6 us (34%)
  waiting for transfers between devices  8.53 us (13%)
  between operations  1.1 us (2%)
  local copies, waits for them, and re-layouts  1.09 us (2%)
    pallas_call x15, Pallas kernels, call(): pl.pallas_call(kernel, out_shape=out_shape, in_specs=in_specs, out_specs=...  32.2 us
    ppermute x4, starting transfers between devices, shards(): lax.ppermute(sum_block(role, True), both, away_pairs)  12.4 us
    ppermute x3, waiting for transfers between devices, exchanged(): return lax.ppermute(block, both, swaps[step])  8.52 us
    ppermute x2, starting transfers between devices, shards(): lax.ppermute(block, both, sorted((pair[::way] for pair in pairs[1 - turn:...  5.56 us
    ppermute x3, starting transfers between devices, exchanged(): return lax.ppermute(block, both, swaps[step])  4.61 us
  transfers between devices with their start and end apart: 9, of which 2 were waited for; matrix products, arithmetic and copies ran while one was open for 0% of the time, Pallas kernels for 40%

profile of v7, /device:TPU:103, one launch (start us, length us, event | category | flops | bytes accessed | tf_op | source)
XLA Modules:
  0.0 65.6 jit_solution(1385607877126217082)
XLA Ops:
  0.7 1.1 %fusion = (bf16[256,512]{1,0:T(8,128)(2,1)S(1)}, bf16[256,512]{1,0:T(8,128)(2,1)S(1)}) fusion(bf16[4096,512]{1,0:T(8,128)(2,1)} %spectra_ref.1), kind=kLoop, calls=%fused_computation | loop fusion | bytes 1048576 | tf_op jit(solution)/shard_map/slice | solution.py:283
  1.8 5.5 %collective-permute-start = (bf16[272,512]{1,0:T(8,128)(2,1)S(1)}, bf16[272,512]{1,0:T(8,128)(2,1)S(1)}, u32[]{:S(2)}, u32[]{:S(2)}) collective-permute-start(bf16[272,512]{1,0:T(8,128)(2,1)S(1)} %get-tuple-element.7), channel_id=1, source_target_pairs={{1,2},{2,1},{3,4},{4,3},{5,6},{6,5},{7,8},{8,7},{9,10},{10,9},{11,... | collective-permute-start | bytes 835592 | tf_op jit(solution)/shard_map/ppermute | solution.py:288
  7.3 0.1 collective-permute-start.1
  7.4 9.6 %shard_map.55.inner_ref = bf16[512,3584]{1,0:T(8,128)(2,1)S(1)} custom-call(s32[1]{0:T(128)S(6)} %copy.6.live_ref, s32[1,4096]{1,0:T(1,128)S(1)} %bitcast.3, s32[1,4096]{1,0:T(1,128)S(1)} %bitcast.5, bf16[4096,512]{1,0:T(8,128)(2,1)S(1)} %copy-done), custom_call_target="tpu_custom_call" | custom-call | flops 5637144576 | bytes 4227076 | tf_op jit(solution)/shard_map/pallas_call | solution.py:255
  17.1 2.1 %shard_map.57.edge_ref = bf16[512,512]{1,0:T(8,128)(2,1)S(1)} custom-call(s32[1]{0:T(128)S(6)} %copy.6.live_ref, s32[1,4096]{1,0:T(1,128)S(1)} %bitcast.4, s32[1,4096]{1,0:T(1,128)S(1)} %bitcast.6, bf16[4096,512]{1,0:T(8,128)(2,1)S(1)} %copy-done, bf16[272,512]{1,0:T(8,128)(2,1)S(1)} %collective-permute-done.one_ref, ...), custom_call_target="tpu_custom_call" | custom-call | flops 805306368 | bytes 4784132 | tf_op jit(solution)/shard_map/pallas_call | solution.py:255
  19.2 2.4 %shard_map.66 = bf16[512,512]{1,0:T(8,128)(2,1)S(1)} custom-call(s32[1]{0:T(128)S(6)} %copy.6.live_ref, s32[1,4096]{1,0:T(1,128)S(1)} %bitcast.7, bf16[512,3584]{1,0:T(8,128)(2,1)S(1)} %shard_map.55.inner_ref, bf16[512,512]{1,0:T(8,128)(2,1)S(1)} %shard_map.57.edge_ref), custom_call_target="tpu_custom_call" | custom-call | flops 2147483648 | bytes 4210692 | tf_op jit(solution)/shard_map/pallas_call | solution.py:255
  21.5 2.4 %collective-permute-start.6 = (bf16[512,512]{1,0:T(8,128)(2,1)S(1)}, bf16[512,512]{1,0:T(8,128)(2,1)S(1)}, u32[]{:S(2)}, u32[]{:S(2)}) collective-permute-start(bf16[512,512]{1,0:T(8,128)(2,1)S(1)} %shard_map.66), channel_id=1, source_target_pairs={{4,0},{8,4},{12,8},{16,12},{20,16},{24,20},{28,24},{32,28},{36,32}... | collective-permute-start | bytes 1572872 | tf_op jit(solution)/shard_map/ppermute | solution.py:318
  23.9 2.4 %shard_map.64 = bf16[512,512]{1,0:T(8,128)(2,1)S(1)} custom-call(s32[1]{0:T(128)S(6)} %copy.6.live_ref, s32[1,4096]{1,0:T(1,128)S(1)} %bitcast.8, bf16[512,3584]{1,0:T(8,128)(2,1)S(1)} %shard_map.55.inner_ref, bf16[512,512]{1,0:T(8,128)(2,1)S(1)} %shard_map.57.edge_ref), custom_call_target="tpu_custom_call" | custom-call | flops 2147483648 | bytes 4210692 | tf_op jit(solution)/shard_map/pallas_call | solution.py:255
  26.3 2.4 %collective-permute-start.5 = (bf16[512,512]{1,0:T(8,128)(2,1)S(1)}, bf16[512,512]{1,0:T(8,128)(2,1)S(1)}, u32[]{:S(2)}, u32[]{:S(2)}) collective-permute-start(bf16[512,512]{1,0:T(8,128)(2,1)S(1)} %shard_map.64), channel_id=1, source_target_pairs={{4,0},{8,4},{12,8},{16,12},{20,16},{24,20},{28,24},{32,28},{36,32}... | collective-permute-start | bytes 1572872 | tf_op jit(solution)/shard_map/ppermute | solution.py:318
  28.7 2.4 %shard_map.61 = bf16[512,512]{1,0:T(8,128)(2,1)S(1)} custom-call(s32[1]{0:T(128)S(6)} %copy.6.live_ref, s32[1,4096]{1,0:T(1,128)S(1)} %bitcast.9, bf16[512,3584]{1,0:T(8,128)(2,1)S(1)} %shard_map.55.inner_ref, bf16[512,512]{1,0:T(8,128)(2,1)S(1)} %shard_map.57.edge_ref), custom_call_target="tpu_custom_call" | custom-call | flops 2147483648 | bytes 4210692 | tf_op jit(solution)/shard_map/pallas_call | solution.py:255
  31.1 2.4 %collective-permute-start.3 = (bf16[512,512]{1,0:T(8,128)(2,1)S(1)}, bf16[512,512]{1,0:T(8,128)(2,1)S(1)}, u32[]{:S(2)}, u32[]{:S(2)}) collective-permute-start(bf16[512,512]{1,0:T(8,128)(2,1)S(1)} %shard_map.61), channel_id=1, source_target_pairs={{4,0},{8,4},{12,8},{16,12},{20,16},{24,20},{28,24},{32,28},{36,32}... | collective-permute-start | bytes 1572872 | tf_op jit(solution)/shard_map/ppermute | solution.py:318
  33.5 2.4 %shard_map.65.own_ref = f32[512,512]{1,0:T(8,128)S(1)} custom-call(s32[1]{0:T(128)S(6)} %copy.6.live_ref, s32[1,4096]{1,0:T(1,128)S(1)} %bitcast.10, bf16[512,3584]{1,0:T(8,128)(2,1)S(1)} %shard_map.55.inner_ref, bf16[512,512]{1,0:T(8,128)(2,1)S(1)} %shard_map.57.edge_ref), custom_call_target="tpu_custom_call" | custom-call | flops 2147483648 | bytes 4210692 | tf_op jit(solution)/shard_map/pallas_call | solution.py:255
  35.9 0.3 collective-permute-start.7
  36.2 2.4 %shard_map.59 = bf16[512,512]{1,0:T(8,128)(2,1)S(1)} custom-call(s32[1]{0:T(128)S(6)} %copy.6.live_ref, s32[1,4096]{1,0:T(1,128)S(1)} %bitcast.11, bf16[512,3584]{1,0:T(8,128)(2,1)S(1)} %shard_map.55.inner_ref, bf16[512,512]{1,0:T(8,128)(2,1)S(1)} %shard_map.57.edge_ref), custom_call_target="tpu_custom_call" | custom-call | flops 2147483648 | bytes 4210692 | tf_op jit(solution)/shard_map/pallas_call | solution.py:255
  38.6 5.3 %collective-permute-start.2 = (bf16[512,512]{1,0:T(8,128)(2,1)S(1)}, bf16[512,512]{1,0:T(8,128)(2,1)S(1)}, u32[]{:S(2)}, u32[]{:S(2)}) collective-permute-start(bf16[512,512]{1,0:T(8,128)(2,1)S(1)} %shard_map.59), channel_id=1, source_target_pairs={{4,0},{8,4},{12,8},{16,12},{20,16},{24,20},{28,24},{32,28},{36,32}... | collective-permute-start | bytes 1572872 | tf_op jit(solution)/shard_map/ppermute | solution.py:318
  43.9 2.4 %shard_map.63.own_ref = f32[512,512]{1,0:T(8,128)S(1)} custom-call(s32[1]{0:T(128)S(6)} %copy.6.live_ref, s32[1,4096]{1,0:T(1,128)S(1)} %bitcast.12, bf16[512,3584]{1,0:T(8,128)(2,1)S(1)} %shard_map.55.inner_ref, bf16[512,512]{1,0:T(8,128)(2,1)S(1)} %shard_map.57.edge_ref), custom_call_target="tpu_custom_call" | custom-call | flops 2147483648 | bytes 4210692 | tf_op jit(solution)/shard_map/pallas_call | solution.py:255
  46.2 2.4 %shard_map.60.own_ref = f32[512,512]{1,0:T(8,128)S(1)} custom-call(s32[1]{0:T(128)S(6)} %copy.6.live_ref, s32[1,4096]{1,0:T(1,128)S(1)} %bitcast.13, bf16[512,3584]{1,0:T(8,128)(2,1)S(1)} %shard_map.55.inner_ref, bf16[512,512]{1,0:T(8,128)(2,1)S(1)} %shard_map.57.edge_ref), custom_call_target="tpu_custom_call" | custom-call | flops 2147483648 | bytes 4210692 | tf_op jit(solution)/shard_map/pallas_call | solution.py:255
  48.7 0.1 collective-permute-start.4
  48.8 0.2 shard_map.68
  49.0 4.2 %collective-permute-start.8 = (bf16[512,512]{1,0:T(8,128)(2,1)S(1)}, bf16[512,512]{1,0:T(8,128)(2,1)S(1)}, u32[]{:S(2)}, u32[]{:S(2)}) collective-permute-start(bf16[512,512]{1,0:T(8,128)(2,1)S(1)} %shard_map.68), channel_id=1, source_target_pairs={{0,1},{1,0},{2,3},{3,2},{4,7},{5,6},{6,5},{7,4},{8,9},{9,8},{10,11... | collective-permute-start | bytes 1572872 | tf_op jit(solution)/shard_map/ppermute | solution.py:323
  53.2 2.4 %shard_map.58.own_ref = f32[512,512]{1,0:T(8,128)S(1)} custom-call(s32[1]{0:T(128)S(6)} %copy.6.live_ref, s32[1,4096]{1,0:T(1,128)S(1)} %bitcast.14, bf16[512,3584]{1,0:T(8,128)(2,1)S(1)} %shard_map.55.inner_ref, bf16[512,512]{1,0:T(8,128)(2,1)S(1)} %shard_map.57.edge_ref), custom_call_target="tpu_custom_call" | custom-call | flops 2147483648 | bytes 4210692 | tf_op jit(solution)/shard_map/pallas_call | solution.py:255
  55.6 4.9 %collective-permute-done.4.rest_1_ = bf16[512,512]{1,0:T(8,128)(2,1)S(1)} collective-permute-done((bf16[512,512]{1,0:T(8,128)(2,1)S(1)}, bf16[512,512]{1,0:T(8,128)(2,1)S(1)}, u32[]{:S(2)}, u32[]{:S(2)}) %collective-permute-start.4) | collective-permute-done | bytes 524320 | tf_op jit(solution)/shard_map/ppermute | solution.py:323
  60.4 3.6 %collective-permute-done.8.rest_2_ = bf16[512,512]{1,0:T(8,128)(2,1)S(1)} collective-permute-done((bf16[512,512]{1,0:T(8,128)(2,1)S(1)}, bf16[512,512]{1,0:T(8,128)(2,1)S(1)}, u32[]{:S(2)}, u32[]{:S(2)}) %collective-permute-start.8) | collective-permute-done | bytes 524320 | tf_op jit(solution)/shard_map/ppermute | solution.py:323
  64.1 1.3 %shard_map.69 = f32[512,512]{1,0:T(8,128)} custom-call(f32[512,512]{1,0:T(8,128)S(1)} %shard_map.58.own_ref, bf16[512,512]{1,0:T(8,128)(2,1)S(1)} %collective-permute-done.2.rest_0_, bf16[512,512]{1,0:T(8,128)(2,1)S(1)} %collective-permute-done.4.rest_1_, bf16[512,512]{1,0:T(8,128)(2,1)S(1)} %collective-permute-done.8.rest_2_), custom_call_target="tpu_custom_call" | custom-call | flops 1048576 | bytes 2621440 | tf_op jit(solution)/shard_map/pallas_call | solution.py:255
  (18 shorter events, 0.3 us)
Async XLA Ops:
  1.7 5.7 %copy-start = (bf16[4096,512]{1,0:T(8,128)(2,1)S(1)}, bf16[4096,512]{1,0:T(8,128)(2,1)}, u32[]{:S(2)}) copy-start(bf16[4096,512]{1,0:T(8,128)(2,1)} %spectra_ref.1) | copy-start | bytes 12582916
  1.7 5.7 %copy-start.1 = (s32[4096]{0:T(1024)S(1)}, s32[4096]{0:T(1024)}, u32[]{:S(2)}) copy-start(s32[4096]{0:T(1024)} %param.6) | copy-start | bytes 49156
  1.7 5.7 %copy-start.2 = (s32[4096]{0:T(1024)S(1)}, s32[4096]{0:T(1024)}, u32[]{:S(2)}) copy-start(s32[4096]{0:T(1024)} %param.7) | copy-start | bytes 49156
  1.8 15.2 %collective-permute-start = (bf16[272,512]{1,0:T(8,128)(2,1)S(1)}, bf16[272,512]{1,0:T(8,128)(2,1)S(1)}, u32[]{:S(2)}, u32[]{:S(2)}) collective-permute-start(bf16[272,512]{1,0:T(8,128)(2,1)S(1)} %get-tuple-element.7), channel_id=1, source_target_pairs={{1,2},{2,1},{3,4},{4,3},{5,6},{6,5},{7,8},{8,7},{9,10},{10,9},{11,... | collective-permute-start | bytes 835592 | tf_op jit(solution)/shard_map/ppermute | solution.py:288
  7.3 9.8 %collective-permute-start.1 = (bf16[272,512]{1,0:T(8,128)(2,1)S(1)}, bf16[272,512]{1,0:T(8,128)(2,1)S(1)}, u32[]{:S(2)}, u32[]{:S(2)}) collective-permute-start(bf16[272,512]{1,0:T(8,128)(2,1)S(1)} %get-tuple-element.8), channel_id=1, source_target_pairs={{0,1},{1,0},{2,3},{3,2},{4,5},{5,4},{6,7},{7,6},{8,9},{9,8},{10,11... | collective-permute-start | bytes 835592 | tf_op jit(solution)/shard_map/ppermute | solution.py:288
  17.0 2.1 %copy-start.3 = (s32[4096]{0:T(1024)S(1)}, s32[4096]{0:T(1024)}, u32[]{:S(2)}) copy-start(s32[4096]{0:T(1024)} %param.9) | copy-start | bytes 49156
  21.5 14.3 %collective-permute-start.6 = (bf16[512,512]{1,0:T(8,128)(2,1)S(1)}, bf16[512,512]{1,0:T(8,128)(2,1)S(1)}, u32[]{:S(2)}, u32[]{:S(2)}) collective-permute-start(bf16[512,512]{1,0:T(8,128)(2,1)S(1)} %shard_map.66), channel_id=1, source_target_pairs={{4,0},{8,4},{12,8},{16,12},{20,16},{24,20},{28,24},{32,28},{36,32}... | collective-permute-start | bytes 1572872 | tf_op jit(solution)/shard_map/ppermute | solution.py:318
  26.3 22.5 %collective-permute-start.5 = (bf16[512,512]{1,0:T(8,128)(2,1)S(1)}, bf16[512,512]{1,0:T(8,128)(2,1)S(1)}, u32[]{:S(2)}, u32[]{:S(2)}) collective-permute-start(bf16[512,512]{1,0:T(8,128)(2,1)S(1)} %shard_map.64), channel_id=1, source_target_pairs={{4,0},{8,4},{12,8},{16,12},{20,16},{24,20},{28,24},{32,28},{36,32}... | collective-permute-start | bytes 1572872 | tf_op jit(solution)/shard_map/ppermute | solution.py:318
  31.1 17.5 %collective-permute-start.3 = (bf16[512,512]{1,0:T(8,128)(2,1)S(1)}, bf16[512,512]{1,0:T(8,128)(2,1)S(1)}, u32[]{:S(2)}, u32[]{:S(2)}) collective-permute-start(bf16[512,512]{1,0:T(8,128)(2,1)S(1)} %shard_map.61), channel_id=1, source_target_pairs={{4,0},{8,4},{12,8},{16,12},{20,16},{24,20},{28,24},{32,28},{36,32}... | collective-permute-start | bytes 1572872 | tf_op jit(solution)/shard_map/ppermute | solution.py:318
  35.9 12.9 %collective-permute-start.7 = (bf16[512,512]{1,0:T(8,128)(2,1)S(1)}, bf16[512,512]{1,0:T(8,128)(2,1)S(1)}, u32[]{:S(2)}, u32[]{:S(2)}) collective-permute-start(bf16[512,512]{1,0:T(8,128)(2,1)S(1)} %shard_map.67), channel_id=1, source_target_pairs={{0,3},{1,2},{2,1},{3,0},{4,5},{5,4},{6,7},{7,6},{8,11},{9,10},{10,... | collective-permute-start | bytes 1572872 | tf_op jit(solution)/shard_map/ppermute | solution.py:323
  38.6 17.0 %collective-permute-start.2 = (bf16[512,512]{1,0:T(8,128)(2,1)S(1)}, bf16[512,512]{1,0:T(8,128)(2,1)S(1)}, u32[]{:S(2)}, u32[]{:S(2)}) collective-permute-start(bf16[512,512]{1,0:T(8,128)(2,1)S(1)} %shard_map.59), channel_id=1, source_target_pairs={{4,0},{8,4},{12,8},{16,12},{20,16},{24,20},{28,24},{32,28},{36,32}... | collective-permute-start | bytes 1572872 | tf_op jit(solution)/shard_map/ppermute | solution.py:318
  48.7 11.8 %collective-permute-start.4 = (bf16[512,512]{1,0:T(8,128)(2,1)S(1)}, bf16[512,512]{1,0:T(8,128)(2,1)S(1)}, u32[]{:S(2)}, u32[]{:S(2)}) collective-permute-start(bf16[512,512]{1,0:T(8,128)(2,1)S(1)} %shard_map.62), channel_id=1, source_target_pairs={{0,3},{1,2},{2,1},{3,0},{4,5},{5,4},{6,7},{7,6},{8,11},{9,10},{10,... | collective-permute-start | bytes 1572872 | tf_op jit(solution)/shard_map/ppermute | solution.py:323
  49.0 15.1 %collective-permute-start.8 = (bf16[512,512]{1,0:T(8,128)(2,1)S(1)}, bf16[512,512]{1,0:T(8,128)(2,1)S(1)}, u32[]{:S(2)}, u32[]{:S(2)}) collective-permute-start(bf16[512,512]{1,0:T(8,128)(2,1)S(1)} %shard_map.68), channel_id=1, source_target_pairs={{0,1},{1,0},{2,3},{3,2},{4,7},{5,6},{6,5},{7,4},{8,9},{9,8},{10,11... | collective-permute-start | bytes 1572872 | tf_op jit(solution)/shard_map/ppermute | solution.py:323
